TPU v7x, 32 devices: a whole 2x2x4 slice. The times are simulated.
32 devices in a mesh: lat: 4 (over y, x), lon: 8 (over z, core).
Axes of the slice: x: 2, y: 2, z: 4, core: 2. Of those that a mesh axis runs over, the one named last changes fastest.
Arguments:
- ensemble: bfloat16 [32, 32, 10240], P('lon', 'lat'), may hold values from -0.625 to 0.625
- innovation: float32 [64, 64, 128], P('lon', 'lat'), may hold values from -6 to 6
- obs_weight: float32 [64, 64, 128], P('lon', 'lat'), may hold values from 0.5 to 20
- lat_offset: int32 [64], P('lat'), may hold values from 0 to 3
- lat_weight: float32 [64], P('lat'), may hold values from 0 to 1
- band_widths: int32 [80], replicated, may hold values from 1 to 63
Outputs:
- coefficients: float32 [2, 2], replicated
- next_vector: bfloat16 [32, 32, 5120], P('lon', 'lat')
All inputs are finite; a program needn't handle non-finite values.
Results may differ from a plain program's by a relative error of at most 0.0014.
Values sent between devices are 32-bit elements; how exact they have to be, the bound alone decides.
No kernel may reach another device: no remote copies, remote signals or barrier semaphores. Data moves between devices by JAX's collectives and lax.ppermute only.
A program may use at most 64 MiB of HBM per device.

v0:
```python
import jax
import jax.numpy as jnp
from jax import lax
from jax.sharding import PartitionSpec as P

M = 80
LEV = 64
FIELDS = 2
ITERS = 2


EVEN_TAPS = (-0.0234375, 0.2265625, 0.8671875, -0.0703125)
ODD_TAPS = (-0.0703125, 0.8671875, 0.2265625, -0.0234375)
EPSILON = 1e-06


def padded_2(block, sides, width, periodic):
    for axis, dim in sides:
        count = lax.axis_size(axis)
        forward = [(i, i + 1) for i in range(count - 1)]
        if periodic:
            forward.append((count - 1, 0))
        backward = [(target, source) for source, target in forward]
        low = lax.ppermute(
            lax.slice_in_dim(block, block.shape[dim] - width, None, axis=dim), axis, forward
        )
        high = lax.ppermute(lax.slice_in_dim(block, 0, width, axis=dim), axis, backward)
        block = jnp.concatenate([low, block, high], axis=dim)
    return block


def tent_matrix(band_widths, levels):
    level_ids = jnp.arange(levels, dtype=jnp.int32)
    distance = jnp.abs(level_ids[:, None] - level_ids[None, :]).astype(jnp.float32)
    widths = (band_widths + 1).astype(jnp.float32)[:, None, None]
    return jnp.maximum(0.0, 1.0 - distance[None] / widths) / widths


def tap_sum(padded, taps, first, length):
    result = taps[0] * padded[first : first + length]
    for offset in range(1, 4):
        result = result + taps[offset] * padded[first + offset : first + offset + length]
    return result


def fold_taps(padded, taps, first, length):
    result = taps[0] * padded[first : first + 2 * length : 2]
    for offset in range(1, 4):
        start_at = first - 2 * offset
        result = result + taps[offset] * padded[start_at : start_at + 2 * length : 2]
    return result


def localize(values, tent):
    lon_cols, lat_rows = (values.shape[0], values.shape[1])
    shaped = values.reshape(lon_cols, lat_rows, M, LEV)
    mapped = jnp.einsum("abml,mlk->abmk", shaped, tent, precision=lax.Precision.HIGHEST)
    return mapped.reshape(lon_cols, lat_rows, M * LEV)


def settle_rows(gathered, lat_rows):
    lon_cols, columns_all = (gathered.shape[0], gathered.shape[2])
    zeros_mid = jnp.zeros((lon_cols, lat_rows - 4, columns_all), jnp.float32)
    rim_out = jnp.concatenate([gathered[:, :2], zeros_mid, gathered[:, lat_rows + 2 :]], axis=1)
    rim_in = padded_2(rim_out, (("lat", 1),), 2, False)
    return gathered[:, 2 : lat_rows + 2] + jnp.concatenate(
        [rim_in[:, :2], zeros_mid, rim_in[:, lat_rows + 2 :]], axis=1
    )


def per_device(ensemble, innovation, obs_weight, lat_offset, lat_weight, band_widths):
    lon_cols, lat_rows = (ensemble.shape[0], ensemble.shape[1])
    fine_cols, fine_rows = (innovation.shape[0], innovation.shape[1])
    columns_all = innovation.shape[2]
    tent = tent_matrix(band_widths, LEV)
    row_ids = jnp.arange(fine_rows, dtype=jnp.int32)
    lower = row_ids // 2 + lat_offset
    columns = jnp.arange(lat_rows + 4, dtype=jnp.int32)
    interp = (1.0 - lat_weight)[:, None] * (columns[None, :] == lower[:, None]) + lat_weight[
        :, None
    ] * (columns[None, :] == lower[:, None] + 1)
    entries = float(lon_cols * lat_rows * M * LEV * lax.axis_size("lat") * lax.axis_size("lon"))
    position = lax.axis_index("lat")
    keep_rows = (
        ((columns >= 2) | (position > 0))
        & ((columns < lat_rows + 2) | (position < lax.axis_size("lat") - 1))
    ).astype(jnp.float32)

    def spread(coarse):
        shaped = ensemble.reshape(lon_cols, lat_rows, M, FIELDS, LEV)
        summed = jnp.sum(shaped * coarse.reshape(lon_cols, lat_rows, 1, FIELDS, LEV), axis=3)
        return localize(summed.reshape(lon_cols, lat_rows, M * LEV), tent)

    def restrict(fine):
        padded = padded_2(fine, (("lon", 0),), 3, True)
        coarse_lon = fold_taps(padded, EVEN_TAPS, 7, lon_cols) + fold_taps(
            padded, ODD_TAPS, 6, lon_cols
        )
        gathered = jnp.einsum("ri,crl->cil", interp, coarse_lon, precision=lax.Precision.HIGHEST)
        return settle_rows(gathered, lat_rows)

    current = spread(restrict(obs_weight * innovation))
    basis = []
    diagonal = []
    off_diagonal = []
    for step in range(ITERS):
        weights = localize(current, tent)
        combine_shaped = ensemble.reshape(lon_cols, lat_rows, M, FIELDS, LEV)
        combine_summed = jnp.sum(
            combine_shaped * weights.reshape(lon_cols, lat_rows, M, 1, LEV), axis=2
        )
        prolong_padded = padded_2(
            combine_summed.reshape(lon_cols, lat_rows, FIELDS * LEV),
            (("lat", 1), ("lon", 0)),
            2,
            True,
        )
        prolong_padded = prolong_padded * keep_rows[None, :, None]
        fine_lat = jnp.einsum(
            "ri,cil->crl", interp, prolong_padded, precision=lax.Precision.HIGHEST
        )
        even_cols = tap_sum(fine_lat, EVEN_TAPS, 0, lon_cols)
        odd_cols = tap_sum(fine_lat, ODD_TAPS, 1, lon_cols)
        image_raw = current + spread(
            restrict(
                obs_weight
                * jnp.stack([even_cols, odd_cols], axis=1).reshape(
                    fine_cols, fine_rows, columns_all
                )
            )
        )
        local_dots = jnp.stack(
            [jnp.sum(member * image_raw) for member in basis]
            + [jnp.sum(current * image_raw), jnp.sum(current * current)]
        )
        sums_all = lax.psum(local_dots, ("lat", "lon"))
        norm_value = jnp.sqrt(sums_all[-1] / entries + EPSILON)
        normed = current / norm_value
        image = image_raw / norm_value
        dots = jnp.concatenate(
            [
                sums_all[:-2] / (entries * norm_value),
                sums_all[-2:-1] / (entries * norm_value * norm_value),
            ]
        )
        basis.append(normed)
        for which_one, member in enumerate(basis):
            image = image - dots[which_one] * member
        diagonal.append(dots[-1])
        off_diagonal.append(norm_value)
        current = image
    coefficients = jnp.stack([jnp.stack(diagonal), jnp.stack(off_diagonal)])
    return (coefficients, current.astype(jnp.bfloat16))


def solution(mesh):
    return jax.shard_map(
        per_device,
        mesh=mesh,
        in_specs=(
            P("lon", "lat", None),
            P("lon", "lat", None),
            P("lon", "lat", None),
            P("lat"),
            P("lat"),
            P(),
        ),
        out_specs=(P(), P("lon", "lat", None)),
        check_vma=False,
    )
```

profile of v0, /device:TPU:0, one launch (start us, length us, event | category | flops | bytes accessed | tf_op | source)
XLA Modules:
  0.0 196.1 jit_solution(7050286283298592275)
XLA Ops:
  0.6 0.9 mul.260
  1.5 0.5 collective-permute-start
  2.1 4.1 %collective-permute-start.1 = (f32[3,16,128]{2,1,0:T(8,128)S(1)}, f32[3,16,128]{2,1,0:T(8,128)S(1)}, u32[]{:S(2)}, u32[]{:S(2)}) collective-permute-start(f32[3,16,128]{2,1,0:T(8,128)S(1)} %get-tuple-element.18), channel_id=1, source_target_pairs={{1,0},{2,1},{3,2},{4,3},{5,4},{6,5},{7,6},{0,7},{9,8},{10,9},{11,1... | collective-permute-start | bytes 73736 | tf_op jit(solution)/shard_map/ppermute | solution.py:27
  6.2 0.7 add_convert_fusion
  6.8 0.7 broadcast_add_fusion
  7.5 0.7 broadcast_subtract_fusion
  8.2 0.8 convolution_bitcast_fusion.8
  9.0 3.8 %collective-permute-start.2 = (f32[4,2,128]{2,1,0:T(2,128)S(1)}, f32[4,2,128]{2,1,0:T(2,128)S(1)}, u32[]{:S(2)}, u32[]{:S(2)}) collective-permute-start(f32[4,2,128]{2,1,0:T(2,128)S(1)} %get-tuple-element.27), channel_id=1, source_target_pairs={{0,8},{8,16},{16,24},{1,9},{9,17},{17,25},{2,10},{10,18},{18,26},{... | collective-permute-start | bytes 12296 | tf_op jit(solution)/shard_map/ppermute | solution.py:24
  12.9 1.3 collective-permute-start.3
  14.2 3.7 %reshape.94 = f32[4,8,80,2,64]{4,3,2,1,0:T(2,128)S(1)} reshape(bf16[4,8,10240]{2,1,0:T(8,128)(2,1)} %param.6) | data formatting | bytes 1966080 | tf_op jit(solution)/shard_map/convert_element_type | solution.py:91
  18.0 0.4 collective-permute-done.3
  18.4 0.1 mul.273
  18.5 3.8 %multiply_reduce_fusion.4 = f32[4,8,80,64]{3,2,1,0:T(8,128)S(1)} fusion(f32[4,8,80,2,64]{4,3,2,1,0:T(2,128)S(1)} %reshape.94, f32[4,8,2,64]{3,2,1,0:T(2,128)S(1)} %mul.273), kind=kLoop, calls=%fused_computation.7 | loop fusion | flops 491520 | bytes 1982464 | tf_op jit(solution)/shard_map/reduce_sum | solution.py:91
  22.4 3.0 %fusion.8 = f32[80,64,32]{1,2,0:S(1)} fusion(f32[4,8,80,64]{3,2,1,0:T(8,128)S(1)} %multiply_reduce_fusion.4, f32[80]{0:T(128)S(1)} %add_convert_fusion, f32[64,64]{1,0:T(8,128)S(1)} %abs_convert_fusion), kind=kOutput, calls=%fused_computation.18 | convolution fusion | flops 127139840 | bytes 1327424
  25.4 2.8 %convolution_bitcast_fusion.3 = f32[4,8,80,64]{3,1,0,2:T(8,128)S(1)} fusion(f32[80,64,32]{1,2,0:S(1)} %fusion.8, f32[80]{0:T(128)S(1)} %add_convert_fusion, f32[64,64]{1,0:T(8,128)S(1)} %abs_convert_fusion), kind=kOutput, calls=%fused_computation.11 | convolution fusion | flops 127139840 | bytes 1327424
  28.3 0.8 copy.20
  29.1 1.6 multiply_reduce_fusion.3
  30.8 2.4 %collective-permute-start.4 = (f32[4,2,128]{2,1,0:T(2,128)S(1)}, f32[4,2,128]{2,1,0:T(2,128)S(1)}, u32[]{:S(2)}, u32[]{:S(2)}) collective-permute-start(f32[4,2,128]{2,1,0:T(2,128)S(1)} %get-tuple-element.31), channel_id=1, source_target_pairs={{0,8},{8,16},{16,24},{24,0},{1,9},{9,17},{17,25},{25,1},{2,10},{10... | collective-permute-start | bytes 12296 | tf_op jit(solution)/shard_map/ppermute | solution.py:24
  33.2 0.9 collective-permute-start.5
  34.1 1.5 collective-permute-done.4
  35.6 1.5 collective-permute-done.5
  37.2 3.5 %collective-permute-start.7 = (f32[2,12,128]{2,1,0:T(8,128)S(1)}, f32[2,12,128]{2,1,0:T(8,128)S(1)}, u32[]{:S(2)}, u32[]{:S(2)}) collective-permute-start(f32[2,12,128]{2,1,0:T(8,128)S(1)} %get-tuple-element.26), channel_id=1, source_target_pairs={{1,0},{2,1},{3,2},{4,3},{5,4},{6,5},{7,6},{0,7},{9,8},{10,9},{11,1... | collective-permute-start | bytes 36872 | tf_op jit(solution)/shard_map/ppermute | solution.py:27
  40.7 1.4 collective-permute-done.6
  42.2 0.3 convolution_bitcast_fusion.5
  42.6 3.6 %collective-permute-start.9 = (f32[3,16,128]{2,1,0:T(8,128)S(1)}, f32[3,16,128]{2,1,0:T(8,128)S(1)}, u32[]{:S(2)}, u32[]{:S(2)}) collective-permute-start(f32[3,16,128]{2,1,0:T(8,128)S(1)} %get-tuple-element.14), channel_id=1, source_target_pairs={{1,0},{2,1},{3,2},{4,3},{5,4},{6,5},{7,6},{0,7},{9,8},{10,9},{11,1... | collective-permute-start | bytes 73736 | tf_op jit(solution)/shard_map/ppermute | solution.py:27
  46.2 1.5 collective-permute-done.8
  47.7 0.2 convolution_bitcast_fusion.7
  47.9 4.8 %collective-permute-start.10 = (f32[4,2,128]{2,1,0:T(2,128)S(1)}, f32[4,2,128]{2,1,0:T(2,128)S(1)}, u32[]{:S(2)}, u32[]{:S(2)}) collective-permute-start(f32[4,2,128]{2,1,0:T(2,128)S(1)} %get-tuple-element.23), channel_id=1, source_target_pairs={{0,8},{8,16},{16,24},{1,9},{9,17},{17,25},{2,10},{10,18},{18,26},{... | collective-permute-start | bytes 12296 | tf_op jit(solution)/shard_map/ppermute | solution.py:24
  52.7 1.3 collective-permute-start.11
  54.0 4.2 %collective-permute-done.11 = f32[4,2,128]{2,1,0:T(2,128)S(1)} collective-permute-done((f32[4,2,128]{2,1,0:T(2,128)S(1)}, f32[4,2,128]{2,1,0:T(2,128)S(1)}, u32[]{:S(2)}, u32[]{:S(2)}) %collective-permute-start.11) | collective-permute-done | bytes 4128 | tf_op jit(solution)/shard_map/ppermute | solution.py:27
  58.3 0.1 mul.296
  58.4 3.8 %multiply_reduce_fusion.2 = f32[4,8,80,64]{3,2,1,0:T(8,128)S(1)} fusion(f32[4,8,80,2,64]{4,3,2,1,0:T(2,128)S(1)} %reshape.94, f32[4,8,2,64]{3,2,1,0:T(2,128)S(1)} %mul.296), kind=kLoop, calls=%fused_computation.5 | loop fusion | flops 491520 | bytes 1982464 | tf_op jit(solution)/shard_map/reduce_sum | solution.py:91
  62.2 4.8 %fusion.10 = (f32[]{:T(128)}, f32[]{:T(128)}, f32[4,8,80,64]{3,1,0,2:T(8,128)}) fusion(f32[80,64,32]{1,2,0:S(1)} %copy-done.1, f32[4,8,80,64]{3,2,1,0:T(8,128)S(1)} %multiply_reduce_fusion.2, f32[80]{0:T(128)S(1)} %add_convert_fusion, f32[64,64]{1,0:T(8,128)S(1)} %abs_convert_fusion), kind=kOutput, calls=%fused_computation.23 | convolution fusion | flops 127959040 | bytes 1982792
  67.0 1.4 pad_maximum_fusion.8
  68.4 37.1 %psum.14 = f32[2]{0:T(128)S(1)} all-reduce(f32[2]{0:T(128)S(1)} %pad_maximum_fusion.8), channel_id=1, replica_groups=mesh['lat'=4,'lon'=8] {'lat','lon'}, use_global_device_ids=true, to_apply=%region_5.6 | all-reduce | flops 2 | bytes 16 | tf_op jit(solution)/shard_map/psum | solution.py:136
  105.5 0.6 fusion.203
  107.5 4.7 %convolution_bitcast_fusion.1 = f32[4,8,80,64]{3,1,0,2:T(8,128)S(1)} fusion(f32[80]{0:T(128)S(1)} %add_convert_fusion, f32[64,64]{1,0:T(8,128)S(1)} %abs_convert_fusion, f32[4,8,80,64]{3,1,0,2:T(8,128)} %get-tuple-element.38, f32[]{:T(128)} %bitcast.25, f32[]{:T(128)} %bitcast.23, f32[80,64,32]{1,2,0} %copy-done), kind=kOutput, calls=%fused_computation.9 | convolution fusion | flops 127795200 | bytes 1982792
  112.2 0.8 copy.24
  113.0 1.4 multiply_reduce_fusion.1
  114.4 0.1 reshape.92
  114.5 2.3 %collective-permute-start.12 = (f32[4,2,128]{2,1,0:T(2,128)S(1)}, f32[4,2,128]{2,1,0:T(2,128)S(1)}, u32[]{:S(2)}, u32[]{:S(2)}) collective-permute-start(f32[4,2,128]{2,1,0:T(2,128)S(1)} %get-tuple-element.29), channel_id=1, source_target_pairs={{0,8},{8,16},{16,24},{24,0},{1,9},{9,17},{17,25},{25,1},{2,10},{10... | collective-permute-start | bytes 12296 | tf_op jit(solution)/shard_map/ppermute | solution.py:24
  116.8 0.6 collective-permute-start.13
  117.5 1.6 collective-permute-done.12
  119.1 1.4 collective-permute-done.13
  120.5 3.5 %collective-permute-start.15 = (f32[2,12,128]{2,1,0:T(8,128)S(1)}, f32[2,12,128]{2,1,0:T(8,128)S(1)}, u32[]{:S(2)}, u32[]{:S(2)}) collective-permute-start(f32[2,12,128]{2,1,0:T(8,128)S(1)} %get-tuple-element.22), channel_id=1, source_target_pairs={{1,0},{2,1},{3,2},{4,3},{5,4},{6,5},{7,6},{0,7},{9,8},{10,9},{11,1... | collective-permute-start | bytes 36872 | tf_op jit(solution)/shard_map/ppermute | solution.py:27
  124.0 1.4 collective-permute-done.14
  125.5 0.3 convolution_bitcast_fusion.4
  125.9 1.1 collective-permute-start.16
  127.0 2.5 %collective-permute-start.17 = (f32[3,16,128]{2,1,0:T(8,128)S(1)}, f32[3,16,128]{2,1,0:T(8,128)S(1)}, u32[]{:S(2)}, u32[]{:S(2)}) collective-permute-start(f32[3,16,128]{2,1,0:T(8,128)S(1)} %get-tuple-element.10), channel_id=1, source_target_pairs={{1,0},{2,1},{3,2},{4,3},{5,4},{6,5},{7,6},{0,7},{9,8},{10,9},{11,1... | collective-permute-start | bytes 73736 | tf_op jit(solution)/shard_map/ppermute | solution.py:27
  129.5 1.5 collective-permute-done.16
  131.0 0.2 convolution_bitcast_fusion.6
  131.2 4.3 %collective-permute-start.18 = (f32[4,2,128]{2,1,0:T(2,128)S(1)}, f32[4,2,128]{2,1,0:T(2,128)S(1)}, u32[]{:S(2)}, u32[]{:S(2)}) collective-permute-start(f32[4,2,128]{2,1,0:T(2,128)S(1)} %get-tuple-element.19), channel_id=1, source_target_pairs={{0,8},{8,16},{16,24},{1,9},{9,17},{17,25},{2,10},{10,18},{18,26},{... | collective-permute-start | bytes 12296 | tf_op jit(solution)/shard_map/ppermute | solution.py:24
  135.5 1.5 collective-permute-start.19
  137.1 3.9 %collective-permute-done.19 = f32[4,2,128]{2,1,0:T(2,128)S(1)} collective-permute-done((f32[4,2,128]{2,1,0:T(2,128)S(1)}, f32[4,2,128]{2,1,0:T(2,128)S(1)}, u32[]{:S(2)}, u32[]{:S(2)}) %collective-permute-start.19) | collective-permute-done | bytes 4128 | tf_op jit(solution)/shard_map/ppermute | solution.py:27
  141.1 0.1 mul.324
  141.2 3.8 %multiply_reduce_fusion = f32[4,8,80,64]{3,2,1,0:T(8,128)S(1)} fusion(f32[4,8,80,2,64]{4,3,2,1,0:T(2,128)S(1)} %reshape.94, f32[4,8,2,64]{3,2,1,0:T(2,128)S(1)} %mul.324), kind=kLoop, calls=%fused_computation.3 | loop fusion | flops 491520 | bytes 1982464 | tf_op jit(solution)/shard_map/reduce_sum | solution.py:91
  145.1 5.1 %multiply_reduce_fusion.7 = (f32[]{:T(128)}, f32[]{:T(128)}, f32[]{:T(128)}, f32[4,8,80,64]{3,1,0,2:T(8,128)}) fusion(f32[]{:T(128)} %bitcast.23, f32[80,64,32]{1,2,0:S(1)} %copy-done.2, f32[4,8,80,64]{3,2,1,0:T(8,128)S(1)} %multiply_reduce_fusion, f32[80]{0:T(128)S(1)} %add_convert_fusion, f32[64,64]{1,0:T(8,128)S(1)} %abs_convert_fusion, f32[]{:T(128)} %bitcast.25, ...), kind=kOutput, calls=%fused_computation.31 | convolution fusion | flops 128942080 | bytes 2638164
  150.2 2.1 %pad_maximum_fusion.9 = f32[3]{0:T(128)S(1)} fusion(f32[1]{0:T(128)} %bitcast.42, f32[1]{0:T(128)} %bitcast.41, f32[1]{0:T(128)} %bitcast.40), kind=kLoop, calls=%fused_computation.211 | loop fusion | flops 6 | bytes 24 | tf_op jit(solution)/shard_map/stack | solution.py:132
  152.3 36.9 %psum.15 = f32[3]{0:T(128)S(1)} all-reduce(f32[3]{0:T(128)S(1)} %pad_maximum_fusion.9), channel_id=1, replica_groups=mesh['lat'=4,'lon'=8] {'lat','lon'}, use_global_device_ids=true, to_apply=%region_11.12 | all-reduce | flops 3 | bytes 24 | tf_op jit(solution)/shard_map/psum | solution.py:136
  189.2 0.6 fusion.202
  192.0 1.8 subtract_convert_fusion
  193.8 0.3 copy.28
  194.1 1.2 reshape.103
  195.2 0.6 pad_maximum_fusion.7
  (60 shorter events, 1.1 us)
Async XLA Ops:
  1.5 6.6 %collective-permute-start = (f32[3,16,128]{2,1,0:T(8,128)S(1)}, f32[3,16,128]{2,1,0:T(8,128)S(1)}, u32[]{:S(2)}, u32[]{:S(2)}) collective-permute-start(f32[3,16,128]{2,1,0:T(8,128)S(1)} %get-tuple-element.17), channel_id=1, source_target_pairs={{0,1},{1,2},{2,3},{3,4},{4,5},{5,6},{6,7},{7,0},{8,9},{9,10},{10,1... | collective-permute-start | bytes 73736 | tf_op jit(solution)/shard_map/ppermute | solution.py:24
  2.1 6.1 %collective-permute-start.1 = (f32[3,16,128]{2,1,0:T(8,128)S(1)}, f32[3,16,128]{2,1,0:T(8,128)S(1)}, u32[]{:S(2)}, u32[]{:S(2)}) collective-permute-start(f32[3,16,128]{2,1,0:T(8,128)S(1)} %get-tuple-element.18), channel_id=1, source_target_pairs={{1,0},{2,1},{3,2},{4,3},{5,4},{6,5},{7,6},{0,7},{9,8},{10,9},{11,1... | collective-permute-start | bytes 73736 | tf_op jit(solution)/shard_map/ppermute | solution.py:27
  9.0 9.0 %collective-permute-start.2 = (f32[4,2,128]{2,1,0:T(2,128)S(1)}, f32[4,2,128]{2,1,0:T(2,128)S(1)}, u32[]{:S(2)}, u32[]{:S(2)}) collective-permute-start(f32[4,2,128]{2,1,0:T(2,128)S(1)} %get-tuple-element.27), channel_id=1, source_target_pairs={{0,8},{8,16},{16,24},{1,9},{9,17},{17,25},{2,10},{10,18},{18,26},{... | collective-permute-start | bytes 12296 | tf_op jit(solution)/shard_map/ppermute | solution.py:24
  12.9 5.5 %collective-permute-start.3 = (f32[4,2,128]{2,1,0:T(2,128)S(1)}, f32[4,2,128]{2,1,0:T(2,128)S(1)}, u32[]{:S(2)}, u32[]{:S(2)}) collective-permute-start(f32[4,2,128]{2,1,0:T(2,128)S(1)} %get-tuple-element.28), channel_id=1, source_target_pairs={{8,0},{16,8},{24,16},{9,1},{17,9},{25,17},{10,2},{18,10},{26,18},{... | collective-permute-start | bytes 12296 | tf_op jit(solution)/shard_map/ppermute | solution.py:27
  25.4 2.9 %copy-start = (f32[80,64,32]{1,2,0}, f32[80,64,32]{1,2,0:S(1)}, u32[]{:S(2)}) copy-start(f32[80,64,32]{1,2,0:S(1)} %fusion.8) | copy-start | bytes 1966084
  29.0 13.1 %copy-start.7 = (f32[16]{0:T(128)S(1)}, f32[16]{0:T(128)}, u32[]{:S(2)}) copy-start(f32[16]{0:T(128)} %param.10) | copy-start | bytes 196
  29.1 13.4 %copy-start.6 = (f32[8,16,128]{2,1,0:T(8,128)S(1)}, f32[8,16,128]{2,1,0:T(8,128)}, u32[]{:S(2)}) copy-start(f32[8,16,128]{2,1,0:T(8,128)} %param.8) | copy-start | bytes 196612
  30.8 4.9 %collective-permute-start.4 = (f32[4,2,128]{2,1,0:T(2,128)S(1)}, f32[4,2,128]{2,1,0:T(2,128)S(1)}, u32[]{:S(2)}, u32[]{:S(2)}) collective-permute-start(f32[4,2,128]{2,1,0:T(2,128)S(1)} %get-tuple-element.31), channel_id=1, source_target_pairs={{0,8},{8,16},{16,24},{24,0},{1,9},{9,17},{17,25},{25,1},{2,10},{10... | collective-permute-start | bytes 12296 | tf_op jit(solution)/shard_map/ppermute | solution.py:24
  33.2 3.9 %collective-permute-start.5 = (f32[4,2,128]{2,1,0:T(2,128)S(1)}, f32[4,2,128]{2,1,0:T(2,128)S(1)}, u32[]{:S(2)}, u32[]{:S(2)}) collective-permute-start(f32[4,2,128]{2,1,0:T(2,128)S(1)} %get-tuple-element.32), channel_id=1, source_target_pairs={{8,0},{16,8},{24,16},{0,24},{9,1},{17,9},{25,17},{1,25},{10,2},{18... | collective-permute-start | bytes 12296 | tf_op jit(solution)/shard_map/ppermute | solution.py:27
  37.1 5.0 %collective-permute-start.6 = (f32[2,12,128]{2,1,0:T(8,128)S(1)}, f32[2,12,128]{2,1,0:T(8,128)S(1)}, u32[]{:S(2)}, u32[]{:S(2)}) collective-permute-start(f32[2,12,128]{2,1,0:T(8,128)S(1)} %get-tuple-element.25), channel_id=1, source_target_pairs={{0,1},{1,2},{2,3},{3,4},{4,5},{5,6},{6,7},{7,0},{8,9},{9,10},{10,1... | collective-permute-start | bytes 36872 | tf_op jit(solution)/shard_map/ppermute | solution.py:24
  37.2 5.0 %collective-permute-start.7 = (f32[2,12,128]{2,1,0:T(8,128)S(1)}, f32[2,12,128]{2,1,0:T(8,128)S(1)}, u32[]{:S(2)}, u32[]{:S(2)}) collective-permute-start(f32[2,12,128]{2,1,0:T(8,128)S(1)} %get-tuple-element.26), channel_id=1, source_target_pairs={{1,0},{2,1},{3,2},{4,3},{5,4},{6,5},{7,6},{0,7},{9,8},{10,9},{11,1... | collective-permute-start | bytes 36872 | tf_op jit(solution)/shard_map/ppermute | solution.py:27
  42.5 5.1 %collective-permute-start.8 = (f32[3,16,128]{2,1,0:T(8,128)S(1)}, f32[3,16,128]{2,1,0:T(8,128)S(1)}, u32[]{:S(2)}, u32[]{:S(2)}) collective-permute-start(f32[3,16,128]{2,1,0:T(8,128)S(1)} %get-tuple-element.13), channel_id=1, source_target_pairs={{0,1},{1,2},{2,3},{3,4},{4,5},{5,6},{6,7},{7,0},{8,9},{9,10},{10,1... | collective-permute-start | bytes 73736 | tf_op jit(solution)/shard_map/ppermute | solution.py:24
  42.6 5.1 %collective-permute-start.9 = (f32[3,16,128]{2,1,0:T(8,128)S(1)}, f32[3,16,128]{2,1,0:T(8,128)S(1)}, u32[]{:S(2)}, u32[]{:S(2)}) collective-permute-start(f32[3,16,128]{2,1,0:T(8,128)S(1)} %get-tuple-element.14), channel_id=1, source_target_pairs={{1,0},{2,1},{3,2},{4,3},{5,4},{6,5},{7,6},{0,7},{9,8},{10,9},{11,1... | collective-permute-start | bytes 73736 | tf_op jit(solution)/shard_map/ppermute | solution.py:27
  47.9 6.1 %collective-permute-start.10 = (f32[4,2,128]{2,1,0:T(2,128)S(1)}, f32[4,2,128]{2,1,0:T(2,128)S(1)}, u32[]{:S(2)}, u32[]{:S(2)}) collective-permute-start(f32[4,2,128]{2,1,0:T(2,128)S(1)} %get-tuple-element.23), channel_id=1, source_target_pairs={{0,8},{8,16},{16,24},{1,9},{9,17},{17,25},{2,10},{10,18},{18,26},{... | collective-permute-start | bytes 12296 | tf_op jit(solution)/shard_map/ppermute | solution.py:24
  52.7 5.5 %collective-permute-start.11 = (f32[4,2,128]{2,1,0:T(2,128)S(1)}, f32[4,2,128]{2,1,0:T(2,128)S(1)}, u32[]{:S(2)}, u32[]{:S(2)}) collective-permute-start(f32[4,2,128]{2,1,0:T(2,128)S(1)} %get-tuple-element.24), channel_id=1, source_target_pairs={{8,0},{16,8},{24,16},{9,1},{17,9},{25,17},{10,2},{18,10},{26,18},{... | collective-permute-start | bytes 12296 | tf_op jit(solution)/shard_map/ppermute | solution.py:27
  58.4 3.9 %copy-start.1 = (f32[80,64,32]{1,2,0:S(1)}, f32[80,64,32]{1,2,0}, u32[]{:S(2)}) copy-start(f32[80,64,32]{1,2,0} %copy-done) | copy-start | bytes 1966084
  114.5 4.5 %collective-permute-start.12 = (f32[4,2,128]{2,1,0:T(2,128)S(1)}, f32[4,2,128]{2,1,0:T(2,128)S(1)}, u32[]{:S(2)}, u32[]{:S(2)}) collective-permute-start(f32[4,2,128]{2,1,0:T(2,128)S(1)} %get-tuple-element.29), channel_id=1, source_target_pairs={{0,8},{8,16},{16,24},{24,0},{1,9},{9,17},{17,25},{25,1},{2,10},{10... | collective-permute-start | bytes 12296 | tf_op jit(solution)/shard_map/ppermute | solution.py:24
  116.8 3.6 %collective-permute-start.13 = (f32[4,2,128]{2,1,0:T(2,128)S(1)}, f32[4,2,128]{2,1,0:T(2,128)S(1)}, u32[]{:S(2)}, u32[]{:S(2)}) collective-permute-start(f32[4,2,128]{2,1,0:T(2,128)S(1)} %get-tuple-element.30), channel_id=1, source_target_pairs={{8,0},{16,8},{24,16},{0,24},{9,1},{17,9},{25,17},{1,25},{10,2},{18... | collective-permute-start | bytes 12296 | tf_op jit(solution)/shard_map/ppermute | solution.py:27
  120.5 5.0 %collective-permute-start.14 = (f32[2,12,128]{2,1,0:T(8,128)S(1)}, f32[2,12,128]{2,1,0:T(8,128)S(1)}, u32[]{:S(2)}, u32[]{:S(2)}) collective-permute-start(f32[2,12,128]{2,1,0:T(8,128)S(1)} %get-tuple-element.21), channel_id=1, source_target_pairs={{0,1},{1,2},{2,3},{3,4},{4,5},{5,6},{6,7},{7,0},{8,9},{9,10},{10,1... | collective-permute-start | bytes 36872 | tf_op jit(solution)/shard_map/ppermute | solution.py:24
  120.5 5.0 %collective-permute-start.15 = (f32[2,12,128]{2,1,0:T(8,128)S(1)}, f32[2,12,128]{2,1,0:T(8,128)S(1)}, u32[]{:S(2)}, u32[]{:S(2)}) collective-permute-start(f32[2,12,128]{2,1,0:T(8,128)S(1)} %get-tuple-element.22), channel_id=1, source_target_pairs={{1,0},{2,1},{3,2},{4,3},{5,4},{6,5},{7,6},{0,7},{9,8},{10,9},{11,1... | collective-permute-start | bytes 36872 | tf_op jit(solution)/shard_map/ppermute | solution.py:27
  125.9 5.1 %collective-permute-start.16 = (f32[3,16,128]{2,1,0:T(8,128)S(1)}, f32[3,16,128]{2,1,0:T(8,128)S(1)}, u32[]{:S(2)}, u32[]{:S(2)}) collective-permute-start(f32[3,16,128]{2,1,0:T(8,128)S(1)} %get-tuple-element.9), channel_id=1, source_target_pairs={{0,1},{1,2},{2,3},{3,4},{4,5},{5,6},{6,7},{7,0},{8,9},{9,10},{10,1... | collective-permute-start | bytes 73736 | tf_op jit(solution)/shard_map/ppermute | solution.py:24
  127.0 4.1 %collective-permute-start.17 = (f32[3,16,128]{2,1,0:T(8,128)S(1)}, f32[3,16,128]{2,1,0:T(8,128)S(1)}, u32[]{:S(2)}, u32[]{:S(2)}) collective-permute-start(f32[3,16,128]{2,1,0:T(8,128)S(1)} %get-tuple-element.10), channel_id=1, source_target_pairs={{1,0},{2,1},{3,2},{4,3},{5,4},{6,5},{7,6},{0,7},{9,8},{10,9},{11,1... | collective-permute-start | bytes 73736 | tf_op jit(solution)/shard_map/ppermute | solution.py:27
  131.2 5.8 %collective-permute-start.18 = (f32[4,2,128]{2,1,0:T(2,128)S(1)}, f32[4,2,128]{2,1,0:T(2,128)S(1)}, u32[]{:S(2)}, u32[]{:S(2)}) collective-permute-start(f32[4,2,128]{2,1,0:T(2,128)S(1)} %get-tuple-element.19), channel_id=1, source_target_pairs={{0,8},{8,16},{16,24},{1,9},{9,17},{17,25},{2,10},{10,18},{18,26},{... | collective-permute-start | bytes 12296 | tf_op jit(solution)/shard_map/ppermute | solution.py:24
  135.5 5.5 %collective-permute-start.19 = (f32[4,2,128]{2,1,0:T(2,128)S(1)}, f32[4,2,128]{2,1,0:T(2,128)S(1)}, u32[]{:S(2)}, u32[]{:S(2)}) collective-permute-start(f32[4,2,128]{2,1,0:T(2,128)S(1)} %get-tuple-element.20), channel_id=1, source_target_pairs={{8,0},{16,8},{24,16},{9,1},{17,9},{25,17},{10,2},{18,10},{26,18},{... | collective-permute-start | bytes 12296 | tf_op jit(solution)/shard_map/ppermute | solution.py:27
  141.2 3.9 %copy-start.2 = (f32[80,64,32]{1,2,0:S(1)}, f32[80,64,32]{1,2,0}, u32[]{:S(2)}) copy-start(f32[80,64,32]{1,2,0} %copy-done) | copy-start | bytes 1966084
  141.2 3.9 %copy-start.4 = (f32[4,8,80,64]{3,1,0,2:T(8,128)S(1)}, f32[4,8,80,64]{3,1,0,2:T(8,128)}, u32[]{:S(2)}) copy-start(f32[4,8,80,64]{3,1,0,2:T(8,128)} %get-tuple-element.38) | copy-start | bytes 1966084
  145.1 46.9 %copy-start.3 = (f32[80,64,32]{1,2,0:S(1)}, f32[80,64,32]{1,2,0}, u32[]{:S(2)}) copy-start(f32[80,64,32]{1,2,0} %copy-done) | copy-start | bytes 1966084
  145.1 46.9 %copy-start.5 = (f32[4,8,80,64]{3,1,0,2:T(8,128)S(1)}, f32[4,8,80,64]{3,1,0,2:T(8,128)}, u32[]{:S(2)}) copy-start(f32[4,8,80,64]{3,1,0,2:T(8,128)} %get-tuple-element.38) | copy-start | bytes 1966084
where the time goes:
time: 200 us; the launch traced here: 196 us
  blocking collectives  74 us (37%)
  starting transfers between devices  42.4 us (21%)
  other arithmetic  23.7 us (12%)
  matrix products  22.2 us (11%)
  waiting for transfers between devices  20.4 us (10%)
  local copies, waits for them, and re-layouts  8.51 us (4%)
  between operations  4.82 us (2%)
    psum x2, blocking collectives, per_device(): sums_all = lax.psum(local_dots, ('lat', 'lon'))  74 us
    ppermute x10, starting transfers between devices, padded_2(): lax.ppermute(lax.slice_in_dim(block, 0, width, axis=dim), axis, backward)  22.9 us
    unnamed x5, matrix products  20.5 us
    ppermute x10, starting transfers between devices, padded_2(): lax.ppermute(lax.slice_in_dim(block, block.shape[dim] - width, None, axis...  19.5 us
    ppermute x10, waiting for transfers between devices, padded_2(): lax.ppermute(lax.slice_in_dim(block, 0, width, axis=dim), axis, backward)  11.5 us
    reduce_sum x3, other arithmetic, spread(): jnp.sum(shaped * coarse.reshape(lon_cols, lat_rows, 1, FIELDS, LEV), axis=3)  11.5 us
    ppermute x10, waiting for transfers between devices, padded_2(): lax.ppermute(lax.slice_in_dim(block, block.shape[dim] - width, None, axis...  8.87 us
  transfers between devices with their start and end apart: 20, of which 13 were waited for; matrix products, arithmetic and copies ran while one was open for 3% of the time, Pallas kernels for 0%

commit v1 on v0

v1 whole, which is shorter than its diff:
```python
import jax
import jax.numpy as jnp
from jax import lax
from jax.experimental import pallas as pl
from jax.experimental.pallas import tpu as pltpu
from jax.sharding import PartitionSpec as P

M = 80
LEV = 64
FIELDS = 2

EVEN_TAPS = (-0.0234375, 0.2265625, 0.8671875, -0.0703125)
ODD_TAPS = (-0.0703125, 0.8671875, 0.2265625, -0.0234375)
EPSILON = 1e-06

F32 = jnp.float32
BF16 = jnp.bfloat16
CH = FIELDS * LEV
PAIRS = M // 2
PAD = 8
VMEM_SPEC = pl.BlockSpec(memory_space=pltpu.VMEM)


def in_vmem(value):
    return pltpu.with_memory_space_constraint(value, pltpu.VMEM)


def kernel_call(body, outs, operands, scratch=()):
    return pl.pallas_call(
        body,
        out_shape=outs,
        in_specs=[VMEM_SPEC] * len(operands),
        out_specs=jax.tree.map(lambda _: VMEM_SPEC, outs),
        scratch_shapes=list(scratch),
    )(*[in_vmem(operand) for operand in operands])


def split(value):
    high = value.astype(BF16)
    return high, (value - high.astype(F32)).astype(BF16)


def pair_distances():
    row = lax.broadcasted_iota(jnp.int32, (CH, CH), 0)
    col = lax.broadcasted_iota(jnp.int32, (CH, CH), 1)
    distance = jnp.where(row // LEV == col // LEV, jnp.abs(row - col), CH)
    return distance.astype(F32).astype(BF16).reshape(CH // 16, 16, CH)


def hat(widths_ref, pair, distances):
    widths = jnp.broadcast_to(widths_ref[pair : pair + 1, :], (16, CH)).astype(BF16)
    return jnp.maximum(widths[None] - distances, jnp.zeros((), BF16)).reshape(CH, CH)


def product(value, matrix):
    cells = value.shape[0]
    parts = jnp.concatenate(split(value), axis=0)
    both = jnp.dot(parts, matrix, preferred_element_type=F32)
    return both[:cells] + both[cells:]


def swap_halves(value):
    return pltpu.roll(value, LEV, 1)


def members(ens_ref, pair):
    first = ens_ref[:, pair * 2 * CH : (pair * 2 + 1) * CH].astype(F32)
    second = ens_ref[:, (pair * 2 + 1) * CH : (pair * 2 + 2) * CH].astype(F32)
    return first, second


def field_sum(first, second, coarse, low_half):
    left, right = first * coarse, second * coarse
    return jnp.where(low_half, left, right) + swap_halves(jnp.where(low_half, right, left))


def gram(ens_ref, widths_ref, scales_ref, coarse):
    distances = pair_distances()
    low_half = lax.broadcasted_iota(jnp.int32, coarse.shape, 1) < LEV
    total = jnp.zeros(coarse.shape, F32)
    for pair in range(PAIRS):
        matrix = hat(widths_ref, pair, distances)
        first, second = members(ens_ref, pair)
        summed = field_sum(first, second, coarse, low_half)
        scale = scales_ref[pair : pair + 1, :]
        twice = product(product(summed, matrix), matrix) * (scale * scale)
        swapped = swap_halves(twice)
        total = total + (
            first * jnp.where(low_half, twice, swapped)
            + second * jnp.where(low_half, swapped, twice)
        )
    return total


def lat_coefficients(stencil_ref, fine):
    weight, offset = stencil_ref[0:fine, :], stencil_ref[fine : 2 * fine, :]
    result = []
    for step in range(5):
        lower = jnp.where(offset == float(step), 1.0 - weight, 0.0)
        result.append(lower + jnp.where(offset == float(step - 1), weight, 0.0))
    return result


def restrict_block(even, odd, coefs, spill_ref, sum_ref, cols, rows):
    fine = 2 * rows + 8
    blocks = []
    for col in range(cols):
        folded = None
        for tap in range(4):
            term = EVEN_TAPS[tap] * even[col + 3 - tap] + ODD_TAPS[tap] * odd[col + 3 - tap]
            folded = term if folded is None else folded + term
        total = None
        for step in range(5):
            slot = col * 5 + step
            spill_ref[slot] = coefs[step] * folded
            term = spill_ref[slot, 8 - 2 * step : 8 - 2 * step + 2 * rows, :]
            total = term if total is None else total + term
        sum_ref[col] = total
        blocks.append(
            sum_ref[col, pl.ds(0, rows, stride=2), :] + sum_ref[col, pl.ds(1, rows, stride=2), :]
        )
    return jnp.concatenate(blocks, axis=0)


def middle(mid_ref, left_ref, right_ref, weight_ref, coefs, dup_ref, spill_ref, sum_ref):
    cols, rows = mid_ref.shape[0], mid_ref.shape[1] - 2
    fine = 2 * rows + 8
    lat = []
    for col in range(cols + 6):
        if col < 3:
            block = left_ref[col]
        elif col < cols + 3:
            block = mid_ref[col - 3]
        else:
            block = right_ref[col - cols - 3]
        dup_ref[col] = jnp.zeros(dup_ref.shape[1:], F32)
        dup_ref[col, pl.ds(PAD, rows + 2, stride=2), :] = block
        dup_ref[col, pl.ds(PAD + 1, rows + 2, stride=2), :] = block
        total = None
        for step in range(5):
            term = coefs[step] * dup_ref[col, 2 + 2 * step : 2 + 2 * step + fine, :]
            total = term if total is None else total + term
        lat.append(total)
    even, odd = [], []
    for at in range(cols + 3):
        first = sum(EVEN_TAPS[tap] * lat[at + tap] for tap in range(4))
        second = sum(ODD_TAPS[tap] * lat[at + tap] for tap in range(4))
        even.append(first * weight_ref[2 * at + 1, 0:fine, :])
        odd.append(second * weight_ref[2 * at, 0:fine, :])
    return restrict_block(even, odd, coefs, spill_ref, sum_ref, cols, rows)


def start_kernel(cols, rows):
    fine = 2 * rows + 8

    def body(weight_ref, stencil_ref, ens_ref, widths_ref, scales_ref, coarse_ref, image_ref, spill_ref, sum_ref):
        coefs = lat_coefficients(stencil_ref, fine)
        even = [weight_ref[2 * at + 1, fine : 2 * fine, :] for at in range(cols + 3)]
        odd = [weight_ref[2 * at, fine : 2 * fine, :] for at in range(cols + 3)]
        coarse = restrict_block(even, odd, coefs, spill_ref, sum_ref, cols, rows)
        coarse_ref[...] = coarse
        image_ref[...] = gram(ens_ref, widths_ref, scales_ref, coarse)

    return body


def step_kernel(cols, rows):
    fine = 2 * rows + 8

    def body(mid_ref, left_ref, right_ref, weight_ref, stencil_ref, ens_ref, widths_ref, scales_ref,
             coarse_ref, image_ref, dup_ref, spill_ref, sum_ref):
        coefs = lat_coefficients(stencil_ref, fine)
        coarse = middle(mid_ref, left_ref, right_ref, weight_ref, coefs, dup_ref, spill_ref, sum_ref)
        coarse_ref[...] = coarse
        image_ref[...] = gram(ens_ref, widths_ref, scales_ref, coarse)

    return body


def last_kernel(cols, rows, devices):
    fine = 2 * rows + 8

    def body(mid_ref, left_ref, right_ref, weight_ref, stencil_ref, y0_ref, b0_ref, y1_ref, b1_ref,
             coarse_ref, dots_ref, dup_ref, spill_ref, sum_ref):
        coefs = lat_coefficients(stencil_ref, fine)
        coarse = middle(mid_ref, left_ref, right_ref, weight_ref, coefs, dup_ref, spill_ref, sum_ref)
        coarse_ref[...] = coarse
        lane = lax.broadcasted_iota(jnp.int32, (1, CH), 1)
        row = jnp.zeros((1, CH), F32)
        b0, b1, y1 = b0_ref[...], b1_ref[...], y1_ref[...]
        pairs = (y0_ref[...] * b0, y1 * b0, y1 * b1, coarse * b1)
        for place, terms in enumerate(pairs):
            total = jnp.sum(jnp.sum(terms, axis=0, keepdims=True), axis=1, keepdims=True)
            row = jnp.where(lane == place, total, row)
        dots_ref[...] = jnp.broadcast_to(row, (devices, CH))

    return body


def final_kernel(entries):
    def body(dots_ref, y0_ref, y1_ref, y2_ref, ens_ref, widths_ref, scales_ref, coef_ref, vector_ref):
        sums = jnp.sum(dots_ref[...], axis=0, keepdims=True)
        lane = lax.broadcasted_iota(jnp.int32, (1, CH), 1)

        def pick(place):
            return jnp.sum(jnp.where(lane == place, sums, 0.0), axis=1, keepdims=True)

        m00, m01, m11, m12 = (pick(place) for place in range(4))
        beta0 = jnp.sqrt(m00 / entries + EPSILON)
        alpha0 = (m00 + m01) / (entries * beta0 * beta0)
        s1 = 1.0 / beta0
        s0 = (1.0 - alpha0) * s1
        u1u1 = s0 * s0 * m00 + 2.0 * s0 * s1 * m01 + s1 * s1 * m11
        beta1 = jnp.sqrt(u1u1 / entries + EPSILON)
        u0u1 = s0 * m00 + s1 * m01
        u0lu1 = s0 * m01 + s1 * m11
        u1lu1 = s0 * s0 * m01 + 2.0 * s0 * s1 * m11 + s1 * s1 * m12
        c0 = (u0u1 + u0lu1) / (entries * beta0 * beta1)
        alpha1 = (u1u1 + u1lu1) / (entries * beta1 * beta1)
        r1 = 1.0 / beta1
        keep = (1.0 - alpha1) * r1
        k0 = keep * s0 - c0 / beta0
        k1 = keep * s1 + s0 * r1
        k2 = s1 * r1
        row = lax.broadcasted_iota(jnp.int32, (2, 2), 0)
        col = lax.broadcasted_iota(jnp.int32, (2, 2), 1)
        coef_ref[...] = jnp.where(
            row == 0, jnp.where(col == 0, alpha0, alpha1), jnp.where(col == 0, beta0, beta1)
        )
        coarse = k0 * y0_ref[...] + k1 * y1_ref[...] + k2 * y2_ref[...]
        distances = pair_distances()
        low_half = lax.broadcasted_iota(jnp.int32, coarse.shape, 1) < LEV
        for pair in range(PAIRS):
            matrix = hat(widths_ref, pair, distances)
            first, second = members(ens_ref, pair)
            summed = field_sum(first, second, coarse, low_half)
            out = product(summed, matrix) * scales_ref[pair : pair + 1, :]
            vector_ref[:, pair * CH : (pair + 1) * CH] = out.astype(BF16)

    return body


def shift(value, axis, step):
    count = lax.axis_size(axis)
    return lax.ppermute(value, axis, [(at, (at + step) % count) for at in range(count)])


def per_device(ensemble, innovation, obs_weight, lat_offset, lat_weight, band_widths):
    cols, rows = ensemble.shape[0], ensemble.shape[1]
    cells = cols * rows
    fine_rows = innovation.shape[1]
    fine = fine_rows + 8
    lat_count, lon_count = lax.axis_size("lat"), lax.axis_size("lon")
    devices = lat_count * lon_count
    entries = float(cells * M * LEV * devices)
    position = lax.axis_index("lat")
    keep_low = (position > 0).astype(F32)
    keep_high = (position < lat_count - 1).astype(F32)

    ens = ensemble.reshape(cells, M * CH)
    widths = jnp.broadcast_to(
        (band_widths + 1).astype(F32).reshape(PAIRS, 2, 1), (PAIRS, 2, LEV)
    ).reshape(PAIRS, CH)
    scales = 1.0 / (widths * widths)

    weighted = obs_weight * innovation
    weight_row = jnp.broadcast_to(lat_weight[:, None], (fine_rows, CH))
    offset_row = jnp.broadcast_to(lat_offset.astype(F32)[:, None], (fine_rows, CH))

    def edge(at):
        part = slice(at, at + 4)
        fields = jnp.concatenate([obs_weight[:, part], weighted[:, part]], axis=1)
        stencil = jnp.concatenate([weight_row[part], offset_row[part]], axis=0)
        return jnp.concatenate([fields, stencil[None]], axis=0)

    low = shift(edge(fine_rows - 4), "lat", 1)
    high = shift(edge(0), "lat", -1)
    low_fields, high_fields = low[:-1] * keep_low, high[:-1] * keep_high
    stencil = jnp.concatenate(
        [low[-1, :4], weight_row, high[-1, :4], low[-1, 4:], offset_row, high[-1, 4:]], axis=0
    )
    tall = jnp.concatenate(
        [low_fields[:, :4], obs_weight, high_fields[:, :4],
         low_fields[:, 4:], weighted, high_fields[:, 4:]], axis=1
    )
    left = shift(tall[-3:], "lon", 1)
    right = shift(tall[:3], "lon", -1)
    weight = jnp.concatenate([left, tall, right], axis=0)

    cell_block = pltpu.VMEM((cells, CH), F32)
    restrict_scratch = (
        pltpu.VMEM((cols * 5, fine, CH), F32),
        pltpu.VMEM((cols, 2 * rows, CH), F32),
    )
    middle_scratch = (pltpu.VMEM((cols + 6, fine + 16, CH), F32),) + restrict_scratch

    def padded(image):
        block = image.reshape(cols, rows, CH)
        low_row = shift(block[:, -1], "lat", 1) * keep_low
        high_row = shift(block[:, 0], "lat", -1) * keep_high
        mid = jnp.concatenate([low_row[:, None], block, high_row[:, None]], axis=1)
        return mid, shift(mid[-3:], "lon", 1), shift(mid[:3], "lon", -1)

    y0, b0 = kernel_call(
        start_kernel(cols, rows), (cell_block, cell_block),
        (weight, stencil, ens, widths, scales), restrict_scratch,
    )
    y1, b1 = kernel_call(
        step_kernel(cols, rows), (cell_block, cell_block),
        (*padded(b0), weight, stencil, ens, widths, scales), middle_scratch,
    )
    y2, dots = kernel_call(
        last_kernel(cols, rows, devices), (cell_block, pltpu.VMEM((devices, CH), F32)),
        (*padded(b1), weight, stencil, y0, b0, y1, b1), middle_scratch,
    )
    shared = lax.all_to_all(dots.reshape(devices, 1, CH), ("lat", "lon"), 0, 0).reshape(devices, CH)
    coefficients, vector = kernel_call(
        final_kernel(entries),
        (jax.ShapeDtypeStruct((2, 2), F32), jax.ShapeDtypeStruct((cells, M * LEV), BF16)),
        (shared, y0, y1, y2, ens, widths, scales),
    )
    return coefficients, vector.reshape(cols, rows, M * LEV)


def solution(mesh):
    return jax.shard_map(
        per_device,
        mesh=mesh,
        in_specs=(
            P("lon", "lat", None),
            P("lon", "lat", None),
            P("lon", "lat", None),
            P("lat"),
            P("lat"),
            P(),
        ),
        out_specs=(P(), P("lon", "lat", None)),
        check_vma=False,
    )
```

time: 200 us -> 53.9 us (0.27); the launches traced: 196 us -> 53.7 us
  blocking collectives: 74 us -> 9.06 us
  starting transfers between devices: 42.4 us -> 14.9 us
  matrix products: 22.2 us -> 0 us
  other arithmetic: 23.7 us -> 1.77 us
  local copies, waits for them, and re-layouts: 8.51 us -> 1.98 us
  Pallas kernels: 0 us -> 4.11 us
  between operations: 4.82 us -> 0.78 us
    psum x2 -> x0, blocking collectives: 74 us -> none  [per_device(): sums_all = lax.psum(local_dots, ('lat', 'lon'))]
    ppermute x20 -> x12, starting transfers between devices: 42.4 us -> 14.9 us  [shift(): lax.ppermute(value, axis, [(at, (at + step) % count) for at in range(coun...]
    unnamed x5 -> x0, matrix products: 20.5 us -> none
    reduce_sum x5 -> x0, other arithmetic: 14.6 us -> none  [the longest x3 11.5 us: spread(): jnp.sum(shaped * coarse.reshape(lon_cols, lat_rows, 1, FIELDS, LEV), axis=3)]
    all_to_all x0 -> x1, blocking collectives: none -> 9.06 us  [per_device(): lax.all_to_all(dots.reshape(devices, 1, CH), ('lat', 'lon'), 0, 0)]
    convert_element_type x3 -> x0, local copies, waits for them, and re-layouts: 5.12 us -> none  [the longest x1 3.71 us: spread(): shaped * coarse.reshape(lon_cols, lat_rows, 1, FIELDS, LEV)]
    another operation x8 -> x0, other arithmetic: 4.12 us -> none  [the longest x2 3.42 us: per_device(): jnp.stack([jnp.sum(member * image_raw) for member in basis] + [jnp.sum(cu...]
    pallas_call x0 -> x4, Pallas kernels: none -> 4.11 us  [kernel_call(): pl.pallas_call(body, out_shape=outs, in_specs=[VMEM_SPEC] * len(operands)...]
  transfers between devices with their start and end apart: 20 -> 12, of which waited for: 13 -> 11; matrix products, arithmetic and copies ran while one was open for 3% -> 1% of each run, Pallas kernels for 0% -> 0%
where the time goes in v1:
time: 53.9 us; the launch traced here: 53.7 us
  waiting for transfers between devices  21.1 us (39%)
  starting transfers between devices  14.9 us (28%)
  blocking collectives  9.06 us (17%)
  Pallas kernels  4.11 us (8%)
  local copies, waits for them, and re-layouts  1.98 us (4%)
  other arithmetic  1.77 us (3%)
  between operations  0.78 us (1%)
    ppermute x12, waiting for transfers between devices, shift(): lax.ppermute(value, axis, [(at, (at + step) % count) for at in range(coun...  21.1 us
    ppermute x12, starting transfers between devices, shift(): lax.ppermute(value, axis, [(at, (at + step) % count) for at in range(coun...  14.9 us
    all_to_all x1, blocking collectives, per_device(): lax.all_to_all(dots.reshape(devices, 1, CH), ('lat', 'lon'), 0, 0)  9.06 us
    pallas_call x4, Pallas kernels, kernel_call(): pl.pallas_call(body, out_shape=outs, in_specs=[VMEM_SPEC] * len(operands)...  4.11 us
  transfers between devices with their start and end apart: 12, of which 11 were waited for; matrix products, arithmetic and copies ran while one was open for 1% of the time, Pallas kernels for 0%

profile of v1, /device:TPU:0, one launch (start us, length us, event | category | flops | bytes accessed | tf_op | source)
XLA Modules:
  0.0 53.7 jit_solution(5576365242579292954)
XLA Ops:
  0.6 0.7 %convert_element_type.12 = f32[16]{0:T(128)S(1)} convert(s32[16]{0:T(128)} %param.9) | non-fusion elementwise | flops 16 | bytes 128 | tf_op jit(solution)/shard_map/convert_element_type | solution.py:268
  1.3 0.0 copy-start.2
  1.3 0.1 fusion.10
  1.4 0.6 %copy-done.2 = f32[16]{0:T(128)S(1)} copy-done((f32[16]{0:T(128)S(1)}, f32[16]{0:T(128)}, u32[]{:S(2)}) %copy-start.2) | copy-done | bytes 88
  1.9 0.1 fusion.9
  2.0 0.1 pad_maximum_fusion.5
  2.1 0.1 broadcast_bitcast_fusion.1
  2.2 0.0 copy-start.1
  2.2 0.9 %mul.38 = f32[8,16,128]{2,1,0:T(8,128)S(1)} multiply(f32[8,16,128]{2,1,0:T(8,128)} %param.8, f32[8,16,128]{2,1,0:T(8,128)} %param.7) | non-fusion elementwise | flops 16384 | bytes 196608 | tf_op jit(solution)/shard_map/mul | solution.py:266
  3.1 0.0 copy-done.1
  3.1 3.0 %collective-permute-start = (f32[9,8,128]{2,1,0:T(8,128)S(1)}, f32[9,8,128]{2,1,0:T(8,128)S(1)}, u32[]{:S(2)}, u32[]{:S(2)}) collective-permute-start(f32[9,8,128]{2,1,0:T(8,128)S(1)} %pad_maximum_fusion.1), channel_id=1, source_target_pairs={{0,8},{8,16},{16,24},{24,0},{1,9},{9,17},{17,25},{25,1},{2,10},{10... | collective-permute-start | bytes 110600 | tf_op jit(solution)/shard_map/ppermute | solution.py:245
  6.2 0.1 broadcast_bitcast_fusion
  6.2 0.0 copy-start.3
  6.3 1.0 %collective-permute-start.1 = (f32[9,8,128]{2,1,0:T(8,128)S(1)}, f32[9,8,128]{2,1,0:T(8,128)S(1)}, u32[]{:S(2)}, u32[]{:S(2)}) collective-permute-start(f32[9,8,128]{2,1,0:T(8,128)S(1)} %pad_maximum_fusion.2), channel_id=1, source_target_pairs={{0,24},{8,0},{16,8},{24,16},{1,25},{9,1},{17,9},{25,17},{2,26},{10... | collective-permute-start | bytes 110600 | tf_op jit(solution)/shard_map/ppermute | solution.py:245
  7.3 0.0 copy-done.3
  7.3 0.1 broadcast_in_dim.53
  7.4 0.1 broadcast_in_dim.54
  7.5 0.1 reshape.32.widths_ref
  7.6 1.4 %collective-permute-done = f32[9,8,128]{2,1,0:T(8,128)S(1)} collective-permute-done((f32[9,8,128]{2,1,0:T(8,128)S(1)}, f32[9,8,128]{2,1,0:T(8,128)S(1)}, u32[]{:S(2)}, u32[]{:S(2)}) %collective-permute-start) | collective-permute-done | bytes 36896 | tf_op jit(solution)/shard_map/ppermute | solution.py:245
  9.1 1.2 %collective-permute-done.1 = f32[9,8,128]{2,1,0:T(8,128)S(1)} collective-permute-done((f32[9,8,128]{2,1,0:T(8,128)S(1)}, f32[9,8,128]{2,1,0:T(8,128)S(1)}, u32[]{:S(2)}, u32[]{:S(2)}) %collective-permute-start.1) | collective-permute-done | bytes 36896 | tf_op jit(solution)/shard_map/ppermute | solution.py:245
  10.3 0.0 copy-start
  10.3 0.3 concatenate.39
  10.7 0.1 collective-permute-start.2
  10.7 3.5 %collective-permute-start.3 = (f32[3,48,128]{2,1,0:T(8,128)S(1)}, f32[3,48,128]{2,1,0:T(8,128)S(1)}, u32[]{:S(2)}, u32[]{:S(2)}) collective-permute-start(f32[3,48,128]{2,1,0:T(8,128)S(1)} %get-tuple-element.19), channel_id=1, source_target_pairs={{0,7},{1,0},{2,1},{3,2},{4,3},{5,4},{6,5},{7,6},{8,15},{9,8},{10,9... | collective-permute-start | bytes 221192 | tf_op jit(solution)/shard_map/ppermute | solution.py:245
  14.3 0.1 broadcast_in_dim.52
  14.3 0.1 broadcast_in_dim.51
  14.4 0.2 concatenate.41.stencil_ref
  14.6 1.7 %collective-permute-done.2 = f32[3,48,128]{2,1,0:T(8,128)S(1)} collective-permute-done((f32[3,48,128]{2,1,0:T(8,128)S(1)}, f32[3,48,128]{2,1,0:T(8,128)S(1)}, u32[]{:S(2)}, u32[]{:S(2)}) %collective-permute-start.2) | collective-permute-done | bytes 73760 | tf_op jit(solution)/shard_map/ppermute | solution.py:245
  16.4 0.0 collective-permute-done.3
  16.4 0.0 copy-done
  16.4 1.2 %shard_map.77 = (f32[32,128]{1,0:T(8,128)S(1)}, f32[32,128]{1,0:T(8,128)S(1)}) custom-call(f32[14,48,128]{2,1,0:T(8,128)S(1)} %pad_maximum_fusion.weight_ref, f32[48,128]{1,0:T(8,128)S(1)} %concatenate.41.stencil_ref, bf16[32,10240]{1,0:T(8,128)(2,1)S(1)} %bitcast.40, f32[40,128]{1,0:T(8,128)S(1)} %reshape.32.widths_ref, ...), custom_call_target="tpu_custom_call" | custom-call | tf_op jit(solution)/shard_map/pallas_call | solution.py:29
  17.6 1.9 %collective-permute-start.5 = (f32[4,128]{1,0:T(4,128)S(1)}, f32[4,128]{1,0:T(4,128)S(1)}, u32[]{:S(2)}, u32[]{:S(2)}) collective-permute-start(f32[4,128]{1,0:T(4,128)S(1)} %bitcast.55), channel_id=1, source_target_pairs={{0,24},{8,0},{16,8},{24,16},{1,25},{9,1},{17,9},{25,17},{2,26},{10... | collective-permute-start | bytes 6152 | tf_op jit(solution)/shard_map/ppermute | solution.py:245
  19.5 0.6 %collective-permute-start.4 = (f32[4,128]{1,0:T(4,128)S(1)}, f32[4,128]{1,0:T(4,128)S(1)}, u32[]{:S(2)}, u32[]{:S(2)}) collective-permute-start(f32[4,128]{1,0:T(4,128)S(1)} %bitcast.54), channel_id=1, source_target_pairs={{0,8},{8,16},{16,24},{24,0},{1,9},{9,17},{17,25},{25,1},{2,10},{10... | collective-permute-start | bytes 6152 | tf_op jit(solution)/shard_map/ppermute | solution.py:245
  20.1 1.5 %collective-permute-done.5 = f32[4,128]{1,0:T(4,128)S(1)} collective-permute-done((f32[4,128]{1,0:T(4,128)S(1)}, f32[4,128]{1,0:T(4,128)S(1)}, u32[]{:S(2)}, u32[]{:S(2)}) %collective-permute-start.5) | collective-permute-done | bytes 2080 | tf_op jit(solution)/shard_map/ppermute | solution.py:245
  21.6 2.3 %collective-permute-done.4 = f32[4,128]{1,0:T(4,128)S(1)} collective-permute-done((f32[4,128]{1,0:T(4,128)S(1)}, f32[4,128]{1,0:T(4,128)S(1)}, u32[]{:S(2)}, u32[]{:S(2)}) %collective-permute-start.4) | collective-permute-done | bytes 2080 | tf_op jit(solution)/shard_map/ppermute | solution.py:245
  24.0 2.1 %collective-permute-start.7 = (f32[3,10,128]{2,1,0:T(8,128)S(1)}, f32[3,10,128]{2,1,0:T(8,128)S(1)}, u32[]{:S(2)}, u32[]{:S(2)}) collective-permute-start(f32[3,10,128]{2,1,0:T(8,128)S(1)} %get-tuple-element.30), channel_id=1, source_target_pairs={{0,7},{1,0},{2,1},{3,2},{4,3},{5,4},{6,5},{7,6},{8,15},{9,8},{10,9... | collective-permute-start | bytes 46088 | tf_op jit(solution)/shard_map/ppermute | solution.py:245
  26.1 0.0 collective-permute-start.6
  26.1 1.5 %collective-permute-done.7.right_ref = f32[3,10,128]{2,1,0:T(8,128)S(1)} collective-permute-done((f32[3,10,128]{2,1,0:T(8,128)S(1)}, f32[3,10,128]{2,1,0:T(8,128)S(1)}, u32[]{:S(2)}, u32[]{:S(2)}) %collective-permute-start.7) | collective-permute-done | bytes 15392 | tf_op jit(solution)/shard_map/ppermute | solution.py:245
  27.6 3.5 %collective-permute-done.6.left_ref = f32[3,10,128]{2,1,0:T(8,128)S(1)} collective-permute-done((f32[3,10,128]{2,1,0:T(8,128)S(1)}, f32[3,10,128]{2,1,0:T(8,128)S(1)}, u32[]{:S(2)}, u32[]{:S(2)}) %collective-permute-start.6) | collective-permute-done | bytes 15392 | tf_op jit(solution)/shard_map/ppermute | solution.py:245
  31.2 1.3 %shard_map.78 = (f32[32,128]{1,0:T(8,128)S(1)}, f32[32,128]{1,0:T(8,128)S(1)}) custom-call(f32[4,10,128]{2,1,0:T(8,128)S(1)} %pad_maximum_fusion.3.mid_ref, f32[3,10,128]{2,1,0:T(8,128)S(1)} %collective-permute-done.6.left_ref, f32[3,10,128]{2,1,0:T(8,128)S(1)} %collective-permute-done.7.right_ref, f32[14,48,128]{2,1,0:T(8,128)S(1)} %pad_maximum_fusion.weight_ref, ...), custom_call_target="tpu_custom_call" | custom-call | tf_op jit(solution)/shard_map/pallas_call | solution.py:29
  32.4 0.9 %collective-permute-start.9 = (f32[4,128]{1,0:T(4,128)S(1)}, f32[4,128]{1,0:T(4,128)S(1)}, u32[]{:S(2)}, u32[]{:S(2)}) collective-permute-start(f32[4,128]{1,0:T(4,128)S(1)} %bitcast.56), channel_id=1, source_target_pairs={{0,24},{8,0},{16,8},{24,16},{1,25},{9,1},{17,9},{25,17},{2,26},{10... | collective-permute-start | bytes 6152 | tf_op jit(solution)/shard_map/ppermute | solution.py:245
  33.3 1.2 %collective-permute-start.8 = (f32[4,128]{1,0:T(4,128)S(1)}, f32[4,128]{1,0:T(4,128)S(1)}, u32[]{:S(2)}, u32[]{:S(2)}) collective-permute-start(f32[4,128]{1,0:T(4,128)S(1)} %bitcast.53), channel_id=1, source_target_pairs={{0,8},{8,16},{16,24},{24,0},{1,9},{9,17},{17,25},{25,1},{2,10},{10... | collective-permute-start | bytes 6152 | tf_op jit(solution)/shard_map/ppermute | solution.py:245
  34.5 1.6 %collective-permute-done.9 = f32[4,128]{1,0:T(4,128)S(1)} collective-permute-done((f32[4,128]{1,0:T(4,128)S(1)}, f32[4,128]{1,0:T(4,128)S(1)}, u32[]{:S(2)}, u32[]{:S(2)}) %collective-permute-start.9) | collective-permute-done | bytes 2080 | tf_op jit(solution)/shard_map/ppermute | solution.py:245
  36.1 1.7 %collective-permute-done.8 = f32[4,128]{1,0:T(4,128)S(1)} collective-permute-done((f32[4,128]{1,0:T(4,128)S(1)}, f32[4,128]{1,0:T(4,128)S(1)}, u32[]{:S(2)}, u32[]{:S(2)}) %collective-permute-start.8) | collective-permute-done | bytes 2080 | tf_op jit(solution)/shard_map/ppermute | solution.py:245
  37.8 0.1 collective-permute-start.11
  37.9 0.5 collective-permute-start.10
  38.4 1.0 %collective-permute-done.11.right_ref = f32[3,10,128]{2,1,0:T(8,128)S(1)} collective-permute-done((f32[3,10,128]{2,1,0:T(8,128)S(1)}, f32[3,10,128]{2,1,0:T(8,128)S(1)}, u32[]{:S(2)}, u32[]{:S(2)}) %collective-permute-start.11) | collective-permute-done | bytes 15392 | tf_op jit(solution)/shard_map/ppermute | solution.py:245
  39.4 3.6 %collective-permute-done.10.left_ref = f32[3,10,128]{2,1,0:T(8,128)S(1)} collective-permute-done((f32[3,10,128]{2,1,0:T(8,128)S(1)}, f32[3,10,128]{2,1,0:T(8,128)S(1)}, u32[]{:S(2)}, u32[]{:S(2)}) %collective-permute-start.10) | collective-permute-done | bytes 15392 | tf_op jit(solution)/shard_map/ppermute | solution.py:245
  43.0 0.2 shard_map.79
  43.3 9.1 %all_to_all.5 = f32[32,1,128]{2,1,0:T(1,128)S(1)} all-to-all(f32[32,1,128]{2,1,0:T(1,128)S(1)} %bitcast.48), channel_id=1, replica_groups=mesh['lat'=4,'lon'=8] {'lat','lon'}, dimensions={0} | all-to-all | bytes 32768 | tf_op jit(solution)/shard_map/all_to_all | solution.py:316
  52.3 1.4 %shard_map.80 = (f32[2,2]{1,0:T(2,128)}, bf16[32,5120]{1,0:T(8,128)(2,1)}) custom-call(f32[32,128]{1,0:T(8,128)S(1)} %bitcast.47, f32[32,128]{1,0:T(8,128)S(1)} %get-tuple-element.12.y0_ref, f32[32,128]{1,0:T(8,128)S(1)} %get-tuple-element.13.y1_ref, f32[32,128]{1,0:T(8,128)S(1)} %get-tuple-element.15.y2_ref, bf16[32,10240]{1,0:T(8,128)(2,1)S(1)} %bitcast.42, ...), custom_call_target="tpu_custom_call" | custom-call | tf_op jit(solution)/shard_map/pallas_call | solution.py:29
  (23 shorter events, 0.2 us)
Async XLA Ops:
  1.3 0.7 %copy-start.2 = (f32[16]{0:T(128)S(1)}, f32[16]{0:T(128)}, u32[]{:S(2)}) copy-start(f32[16]{0:T(128)} %param.10) | copy-start | bytes 196
  2.2 0.9 %copy-start.1 = (f32[8,16,128]{2,1,0:T(8,128)S(1)}, f32[8,16,128]{2,1,0:T(8,128)}, u32[]{:S(2)}) copy-start(f32[8,16,128]{2,1,0:T(8,128)} %param.8) | copy-start | bytes 196612
  3.1 5.9 %collective-permute-start = (f32[9,8,128]{2,1,0:T(8,128)S(1)}, f32[9,8,128]{2,1,0:T(8,128)S(1)}, u32[]{:S(2)}, u32[]{:S(2)}) collective-permute-start(f32[9,8,128]{2,1,0:T(8,128)S(1)} %pad_maximum_fusion.1), channel_id=1, source_target_pairs={{0,8},{8,16},{16,24},{24,0},{1,9},{9,17},{17,25},{25,1},{2,10},{10... | collective-permute-start | bytes 110600 | tf_op jit(solution)/shard_map/ppermute | solution.py:245
  6.2 1.0 %copy-start.3 = (s32[80]{0:T(128)S(1)}, s32[80]{0:T(128)}, u32[]{:S(2)}) copy-start(s32[80]{0:T(128)} %param.11) | copy-start | bytes 964
  6.3 4.0 %collective-permute-start.1 = (f32[9,8,128]{2,1,0:T(8,128)S(1)}, f32[9,8,128]{2,1,0:T(8,128)S(1)}, u32[]{:S(2)}, u32[]{:S(2)}) collective-permute-start(f32[9,8,128]{2,1,0:T(8,128)S(1)} %pad_maximum_fusion.2), channel_id=1, source_target_pairs={{0,24},{8,0},{16,8},{24,16},{1,25},{9,1},{17,9},{25,17},{2,26},{10... | collective-permute-start | bytes 110600 | tf_op jit(solution)/shard_map/ppermute | solution.py:245
  10.3 6.1 %copy-start = (bf16[4,8,10240]{2,1,0:T(8,128)(2,1)S(1)}, bf16[4,8,10240]{2,1,0:T(8,128)(2,1)}, u32[]{:S(2)}) copy-start(bf16[4,8,10240]{2,1,0:T(8,128)(2,1)} %param.6) | copy-start | bytes 1966084
  10.7 5.7 %collective-permute-start.2 = (f32[3,48,128]{2,1,0:T(8,128)S(1)}, f32[3,48,128]{2,1,0:T(8,128)S(1)}, u32[]{:S(2)}, u32[]{:S(2)}) collective-permute-start(f32[3,48,128]{2,1,0:T(8,128)S(1)} %get-tuple-element.18), channel_id=1, source_target_pairs={{0,1},{1,2},{2,3},{3,4},{4,5},{5,6},{6,7},{7,0},{8,9},{9,10},{10,1... | collective-permute-start | bytes 221192 | tf_op jit(solution)/shard_map/ppermute | solution.py:245
  10.7 5.6 %collective-permute-start.3 = (f32[3,48,128]{2,1,0:T(8,128)S(1)}, f32[3,48,128]{2,1,0:T(8,128)S(1)}, u32[]{:S(2)}, u32[]{:S(2)}) collective-permute-start(f32[3,48,128]{2,1,0:T(8,128)S(1)} %get-tuple-element.19), channel_id=1, source_target_pairs={{0,7},{1,0},{2,1},{3,2},{4,3},{5,4},{6,5},{7,6},{8,15},{9,8},{10,9... | collective-permute-start | bytes 221192 | tf_op jit(solution)/shard_map/ppermute | solution.py:245
  17.6 4.0 %collective-permute-start.5 = (f32[4,128]{1,0:T(4,128)S(1)}, f32[4,128]{1,0:T(4,128)S(1)}, u32[]{:S(2)}, u32[]{:S(2)}) collective-permute-start(f32[4,128]{1,0:T(4,128)S(1)} %bitcast.55), channel_id=1, source_target_pairs={{0,24},{8,0},{16,8},{24,16},{1,25},{9,1},{17,9},{25,17},{2,26},{10... | collective-permute-start | bytes 6152 | tf_op jit(solution)/shard_map/ppermute | solution.py:245
  19.5 4.5 %collective-permute-start.4 = (f32[4,128]{1,0:T(4,128)S(1)}, f32[4,128]{1,0:T(4,128)S(1)}, u32[]{:S(2)}, u32[]{:S(2)}) collective-permute-start(f32[4,128]{1,0:T(4,128)S(1)} %bitcast.54), channel_id=1, source_target_pairs={{0,8},{8,16},{16,24},{24,0},{1,9},{9,17},{17,25},{25,1},{2,10},{10... | collective-permute-start | bytes 6152 | tf_op jit(solution)/shard_map/ppermute | solution.py:245
  24.0 3.7 %collective-permute-start.7 = (f32[3,10,128]{2,1,0:T(8,128)S(1)}, f32[3,10,128]{2,1,0:T(8,128)S(1)}, u32[]{:S(2)}, u32[]{:S(2)}) collective-permute-start(f32[3,10,128]{2,1,0:T(8,128)S(1)} %get-tuple-element.30), channel_id=1, source_target_pairs={{0,7},{1,0},{2,1},{3,2},{4,3},{5,4},{6,5},{7,6},{8,15},{9,8},{10,9... | collective-permute-start | bytes 46088 | tf_op jit(solution)/shard_map/ppermute | solution.py:245
  26.1 5.0 %collective-permute-start.6 = (f32[3,10,128]{2,1,0:T(8,128)S(1)}, f32[3,10,128]{2,1,0:T(8,128)S(1)}, u32[]{:S(2)}, u32[]{:S(2)}) collective-permute-start(f32[3,10,128]{2,1,0:T(8,128)S(1)} %get-tuple-element.31), channel_id=1, source_target_pairs={{0,1},{1,2},{2,3},{3,4},{4,5},{5,6},{6,7},{7,0},{8,9},{9,10},{10,1... | collective-permute-start | bytes 46088 | tf_op jit(solution)/shard_map/ppermute | solution.py:245
  32.4 3.6 %collective-permute-start.9 = (f32[4,128]{1,0:T(4,128)S(1)}, f32[4,128]{1,0:T(4,128)S(1)}, u32[]{:S(2)}, u32[]{:S(2)}) collective-permute-start(f32[4,128]{1,0:T(4,128)S(1)} %bitcast.56), channel_id=1, source_target_pairs={{0,24},{8,0},{16,8},{24,16},{1,25},{9,1},{17,9},{25,17},{2,26},{10... | collective-permute-start | bytes 6152 | tf_op jit(solution)/shard_map/ppermute | solution.py:245
  33.3 4.5 %collective-permute-start.8 = (f32[4,128]{1,0:T(4,128)S(1)}, f32[4,128]{1,0:T(4,128)S(1)}, u32[]{:S(2)}, u32[]{:S(2)}) collective-permute-start(f32[4,128]{1,0:T(4,128)S(1)} %bitcast.53), channel_id=1, source_target_pairs={{0,8},{8,16},{16,24},{24,0},{1,9},{9,17},{17,25},{25,1},{2,10},{10... | collective-permute-start | bytes 6152 | tf_op jit(solution)/shard_map/ppermute | solution.py:245
  37.8 1.6 %collective-permute-start.11 = (f32[3,10,128]{2,1,0:T(8,128)S(1)}, f32[3,10,128]{2,1,0:T(8,128)S(1)}, u32[]{:S(2)}, u32[]{:S(2)}) collective-permute-start(f32[3,10,128]{2,1,0:T(8,128)S(1)} %get-tuple-element.28), channel_id=1, source_target_pairs={{0,7},{1,0},{2,1},{3,2},{4,3},{5,4},{6,5},{7,6},{8,15},{9,8},{10,9... | collective-permute-start | bytes 46088 | tf_op jit(solution)/shard_map/ppermute | solution.py:245
  37.9 5.1 %collective-permute-start.10 = (f32[3,10,128]{2,1,0:T(8,128)S(1)}, f32[3,10,128]{2,1,0:T(8,128)S(1)}, u32[]{:S(2)}, u32[]{:S(2)}) collective-permute-start(f32[3,10,128]{2,1,0:T(8,128)S(1)} %get-tuple-element.29), channel_id=1, source_target_pairs={{0,1},{1,2},{2,3},{3,4},{4,5},{5,6},{6,7},{7,0},{8,9},{9,10},{10,1... | collective-permute-start | bytes 46088 | tf_op jit(solution)/shard_map/ppermute | solution.py:245

commit v2 on v1

v2 whole, which is shorter than its diff:
```python
import jax
import jax.numpy as jnp
from jax import lax
from jax.experimental import pallas as pl
from jax.experimental.pallas import tpu as pltpu
from jax.sharding import PartitionSpec as P

M = 80
LEV = 64
FIELDS = 2

EVEN_TAPS = (-0.0234375, 0.2265625, 0.8671875, -0.0703125)
ODD_TAPS = (-0.0703125, 0.8671875, 0.2265625, -0.0234375)
EPSILON = 1e-06

F32 = jnp.float32
BF16 = jnp.bfloat16
CH = FIELDS * LEV
PAIRS = M // 2
PAD = 8
FINE_HALO = 6
VMEM_SPEC = pl.BlockSpec(memory_space=pltpu.VMEM)


def in_vmem(value):
    return pltpu.with_memory_space_constraint(value, pltpu.VMEM)


def kernel_call(body, outs, operands, scratch=()):
    return pl.pallas_call(
        body,
        out_shape=outs,
        in_specs=[VMEM_SPEC] * len(operands),
        out_specs=jax.tree.map(lambda _: VMEM_SPEC, outs),
        scratch_shapes=list(scratch),
    )(*[in_vmem(operand) for operand in operands])


def split(value):
    high = value.astype(BF16)
    return high, (value - high.astype(F32)).astype(BF16)


def pair_distances():
    row = lax.broadcasted_iota(jnp.int32, (CH, CH), 0)
    col = lax.broadcasted_iota(jnp.int32, (CH, CH), 1)
    distance = jnp.where(row // LEV == col // LEV, jnp.abs(row - col), CH)
    return distance.astype(F32).astype(BF16).reshape(CH // 16, 16, CH)


def hat(widths_ref, pair, distances):
    widths = jnp.broadcast_to(widths_ref[pair : pair + 1, :], (16, CH)).astype(BF16)
    return jnp.maximum(widths[None] - distances, jnp.zeros((), BF16)).reshape(CH, CH)


def product(value, matrix):
    cells = value.shape[0]
    parts = jnp.concatenate(split(value), axis=0)
    both = jnp.dot(parts, matrix, preferred_element_type=F32)
    return both[:cells] + both[cells:]


def swap_halves(value):
    return pltpu.roll(value, LEV, 1)


def members(ens_refs, pair):
    result = []
    for member in (2 * pair, 2 * pair + 1):
        parts = [ref[:, member * CH : (member + 1) * CH].astype(F32) for ref in ens_refs]
        result.append(parts[0] if len(parts) == 1 else jnp.concatenate(parts, axis=0))
    return result


def field_sum(first, second, coarse, low_half):
    left, right = first * coarse, second * coarse
    return jnp.where(low_half, left, right) + swap_halves(jnp.where(low_half, right, left))


def gram(ens_refs, widths_ref, scales_ref, coarse):
    distances = pair_distances()
    low_half = lax.broadcasted_iota(jnp.int32, coarse.shape, 1) < LEV
    total = jnp.zeros(coarse.shape, F32)
    for pair in range(PAIRS):
        matrix = hat(widths_ref, pair, distances)
        first, second = members(ens_refs, pair)
        summed = field_sum(first, second, coarse, low_half)
        scale = scales_ref[pair : pair + 1, :]
        twice = product(product(summed, matrix), matrix) * (scale * scale)
        swapped = swap_halves(twice)
        total = total + (
            first * jnp.where(low_half, twice, swapped)
            + second * jnp.where(low_half, swapped, twice)
        )
    return total


def prepare_kernel():
    depth = FINE_HALO

    def body(weight_ref, innovation_ref, lat_weight_ref, lat_offset_ref, band_ref,
             up_ref, down_ref, own_ref, own_stencil_ref, widths_ref, scales_ref):
        fine_cols, fine_rows = weight_ref.shape[0], weight_ref.shape[1]
        for col in range(fine_cols):
            weight = weight_ref[col]
            weighted = weight * innovation_ref[col]
            own_ref[col, 0:fine_rows, :] = weight
            own_ref[col, fine_rows : 2 * fine_rows, :] = weighted
            at = 2 * depth * col
            up_ref[at : at + depth, :] = weight[fine_rows - depth :]
            up_ref[at + depth : at + 2 * depth, :] = weighted[fine_rows - depth :]
            down_ref[at : at + depth, :] = weight[:depth]
            down_ref[at + depth : at + 2 * depth, :] = weighted[:depth]
        row = lax.broadcasted_iota(jnp.int32, (fine_rows, fine_rows), 0)
        col = lax.broadcasted_iota(jnp.int32, (fine_rows, fine_rows), 1)

        def column(line):
            spread = jnp.broadcast_to(line, (fine_rows, fine_rows))
            values = jnp.sum(jnp.where(row == col, spread, 0.0), axis=1, keepdims=True)
            return jnp.broadcast_to(values, (fine_rows, CH))

        weight = column(lat_weight_ref[...])
        offset = column(lat_offset_ref[...].astype(F32))
        own_stencil_ref[0:fine_rows, :] = weight
        own_stencil_ref[fine_rows : 2 * fine_rows, :] = offset
        at = 2 * depth * fine_cols
        up_ref[at : at + depth, :] = weight[fine_rows - depth :]
        up_ref[at + depth : at + 2 * depth, :] = offset[fine_rows - depth :]
        down_ref[at : at + depth, :] = weight[:depth]
        down_ref[at + depth : at + 2 * depth, :] = offset[:depth]
        bands = jnp.broadcast_to((band_ref[...] + 1).astype(F32), (PAIRS, M))
        pair = lax.broadcasted_iota(jnp.int32, (PAIRS, M), 0)
        member = lax.broadcasted_iota(jnp.int32, (PAIRS, M), 1)
        first = jnp.sum(jnp.where(member == 2 * pair, bands, 0.0), axis=1, keepdims=True)
        second = jnp.sum(jnp.where(member == 2 * pair + 1, bands, 0.0), axis=1, keepdims=True)
        lane = lax.broadcasted_iota(jnp.int32, (PAIRS, CH), 1)
        widths = jnp.where(lane < LEV, first, second)
        widths_ref[...] = widths
        scales_ref[...] = 1.0 / (widths * widths)

    return body


def join_kernel():
    depth = FINE_HALO

    def body(low_ref, high_ref, own_ref, own_stencil_ref, flags_ref, tall_ref, stencil_ref):
        fine_cols, fine_rows = own_ref.shape[0], own_ref.shape[1] // 2
        total = fine_rows + 2 * depth
        keep_low, keep_high = flags_ref[0:1, :], flags_ref[1:2, :]
        for part in range(2):
            base = part * total
            for col in range(fine_cols):
                at = 2 * depth * col + part * depth
                tall_ref[col, base : base + depth, :] = low_ref[at : at + depth, :] * keep_low
                tall_ref[col, base + depth : base + depth + fine_rows, :] = own_ref[
                    col, part * fine_rows : (part + 1) * fine_rows, :
                ]
                tall_ref[col, base + depth + fine_rows : base + total, :] = (
                    high_ref[at : at + depth, :] * keep_high
                )
            at = 2 * depth * fine_cols + part * depth
            stencil_ref[base : base + depth, :] = low_ref[at : at + depth, :]
            stencil_ref[base + depth : base + depth + fine_rows, :] = own_stencil_ref[
                part * fine_rows : (part + 1) * fine_rows, :
            ]
            stencil_ref[base + depth + fine_rows : base + total, :] = high_ref[at : at + depth, :]

    return body


def edges_kernel(cols, rows):
    def body(ens_ref, after_ref, up_ref, down_ref):
        row = lax.broadcasted_iota(jnp.int32, (8, CH), 0)
        for member in range(M):
            lanes = slice(member * CH, (member + 1) * CH)
            block = ens_ref[:, lanes].astype(F32)
            for ref, at in ((up_ref, rows - 1), (down_ref, 0)):
                picked = jnp.zeros((8, CH), F32)
                for col in range(cols):
                    line = block[col * rows + at : col * rows + at + 1]
                    picked = jnp.where(row == col, jnp.broadcast_to(line, (8, CH)), picked)
                ref[:, lanes] = picked[:cols]

    return body


def fine_span(rows, halo):
    return FINE_HALO - 4 - 2 * halo, 2 * rows + 8 + 4 * halo


def lat_coefficients(stencil_ref, rows, halo):
    first, count = fine_span(rows, halo)
    total = 2 * rows + 2 * FINE_HALO
    weight = stencil_ref[first : first + count, :]
    offset = stencil_ref[total + first : total + first + count, :]
    result = []
    for step in range(5):
        lower = jnp.where(offset == float(step), 1.0 - weight, 0.0)
        result.append(lower + jnp.where(offset == float(step - 1), weight, 0.0))
    return result


def restrict_block(even, odd, coefs, spill_ref, sum_ref, cols, rows, halo):
    count = fine_span(rows, halo)[1]
    out = rows + 2 * halo
    for col in range(cols):
        folded = None
        for tap in range(4):
            term = EVEN_TAPS[tap] * even[col + 3 - tap] + ODD_TAPS[tap] * odd[col + 3 - tap]
            folded = term if folded is None else folded + term
        total = None
        for step in range(5):
            slot = col * 5 + step
            spill_ref[slot, 0:count, :] = coefs[step] * folded
            term = spill_ref[slot, 8 - 2 * step : 8 - 2 * step + 2 * out, :]
            total = term if total is None else total + term
        sum_ref[col, 0 : 2 * out, :] = total
    blocks = [
        sum_ref[col, pl.ds(2 * halo, rows, stride=2), :]
        + sum_ref[col, pl.ds(2 * halo + 1, rows, stride=2), :]
        for col in range(cols)
    ]
    return jnp.concatenate(blocks, axis=0)


def middle(mid_ref, left_ref, right_ref, weight_ref, coefs, dup_ref, spill_ref, sum_ref, rows, halo):
    cols = mid_ref.shape[0]
    first, count = fine_span(rows, halo)
    given = rows + 2 * halo + 2
    lat = []
    for col in range(cols + 6):
        if col < 3:
            block = left_ref[col]
        elif col < cols + 3:
            block = mid_ref[col - 3]
        else:
            block = right_ref[col - cols - 3]
        dup_ref[col] = jnp.zeros(dup_ref.shape[1:], F32)
        dup_ref[col, pl.ds(PAD, given, stride=2), :] = block
        dup_ref[col, pl.ds(PAD + 1, given, stride=2), :] = block
        total = None
        for step in range(5):
            at = 2 + 2 * step
            term = coefs[step] * dup_ref[col, at : at + count, :]
            total = term if total is None else total + term
        lat.append(total)
    even, odd = [], []
    for at in range(cols + 3):
        left = sum(EVEN_TAPS[tap] * lat[at + tap] for tap in range(4))
        right = sum(ODD_TAPS[tap] * lat[at + tap] for tap in range(4))
        even.append(left * weight_ref[2 * at + 1, first : first + count, :])
        odd.append(right * weight_ref[2 * at, first : first + count, :])
    return restrict_block(even, odd, coefs, spill_ref, sum_ref, cols, rows, halo)


def start_kernel(cols, rows):
    first, count = fine_span(rows, 0)
    base = 2 * rows + 2 * FINE_HALO + first

    def body(weight_ref, stencil_ref, ens_ref, widths_ref, scales_ref, coarse_ref, image_ref, spill_ref, sum_ref):
        coefs = lat_coefficients(stencil_ref, rows, 0)
        even = [weight_ref[2 * at + 1, base : base + count, :] for at in range(cols + 3)]
        odd = [weight_ref[2 * at, base : base + count, :] for at in range(cols + 3)]
        coarse = restrict_block(even, odd, coefs, spill_ref, sum_ref, cols, rows, 0)
        coarse_ref[...] = coarse
        image_ref[...] = gram((ens_ref,), widths_ref, scales_ref, coarse)

    return body


def step_kernel(cols, rows):
    cells = cols * rows

    def body(mid_ref, left_ref, right_ref, weight_ref, stencil_ref, flags_ref, ens_ref, ens_low_ref, ens_high_ref,
             widths_ref, scales_ref, coarse_ref, image_ref, padded_ref, dup_ref, spill_ref, sum_ref, rim_ref):
        coefs = lat_coefficients(stencil_ref, rows, 1)
        coarse = middle(
            mid_ref, left_ref, right_ref, weight_ref, coefs, dup_ref, spill_ref, sum_ref, rows, 1
        )
        coarse_ref[...] = coarse
        end = 2 * rows + 2
        for col in range(cols):
            low = sum_ref[col, 0:1, :] + sum_ref[col, 1:2, :]
            high = sum_ref[col, end : end + 1, :] + sum_ref[col, end + 1 : end + 2, :]
            rim_ref[col : col + 1, :] = low * flags_ref[0:1, :]
            rim_ref[cols + col : cols + col + 1, :] = high * flags_ref[1:2, :]
        image = gram(
            (ens_ref, ens_low_ref, ens_high_ref), widths_ref, scales_ref,
            jnp.concatenate([coarse, rim_ref[...]], axis=0),
        )
        image_ref[...] = image[:cells]
        for col in range(cols):
            padded_ref[col, 0:1, :] = image[cells + col : cells + col + 1]
            padded_ref[col, 1 : rows + 1, :] = image[col * rows : (col + 1) * rows]
            padded_ref[col, rows + 1 : rows + 2, :] = image[
                cells + cols + col : cells + cols + col + 1
            ]

    return body


def last_kernel(rows, devices):
    def body(mid_ref, left_ref, right_ref, weight_ref, stencil_ref, y0_ref, b0_ref, y1_ref, b1_ref,
             coarse_ref, dots_ref, dup_ref, spill_ref, sum_ref):
        coefs = lat_coefficients(stencil_ref, rows, 0)
        coarse = middle(
            mid_ref, left_ref, right_ref, weight_ref, coefs, dup_ref, spill_ref, sum_ref, rows, 0
        )
        coarse_ref[...] = coarse
        lane = lax.broadcasted_iota(jnp.int32, (1, CH), 1)
        row = jnp.zeros((1, CH), F32)
        b0, b1, y1 = b0_ref[...], b1_ref[...], y1_ref[...]
        pairs = (y0_ref[...] * b0, y1 * b0, y1 * b1, coarse * b1)
        for place, terms in enumerate(pairs):
            total = jnp.sum(jnp.sum(terms, axis=0, keepdims=True), axis=1, keepdims=True)
            row = jnp.where(lane == place, total, row)
        dots_ref[...] = jnp.broadcast_to(row, (devices, CH))

    return body


def final_kernel(entries):
    def body(dots_ref, y0_ref, y1_ref, y2_ref, ens_ref, widths_ref, scales_ref, coef_ref, vector_ref):
        sums = jnp.sum(dots_ref[...], axis=0, keepdims=True)
        lane = lax.broadcasted_iota(jnp.int32, (1, CH), 1)

        def pick(place):
            return jnp.sum(jnp.where(lane == place, sums, 0.0), axis=1, keepdims=True)

        m00, m01, m11, m12 = (pick(place) for place in range(4))
        beta0 = jnp.sqrt(m00 / entries + EPSILON)
        alpha0 = (m00 + m01) / (entries * beta0 * beta0)
        s1 = 1.0 / beta0
        s0 = (1.0 - alpha0) * s1
        u1u1 = s0 * s0 * m00 + 2.0 * s0 * s1 * m01 + s1 * s1 * m11
        beta1 = jnp.sqrt(u1u1 / entries + EPSILON)
        u0u1 = s0 * m00 + s1 * m01
        u0lu1 = s0 * m01 + s1 * m11
        u1lu1 = s0 * s0 * m01 + 2.0 * s0 * s1 * m11 + s1 * s1 * m12
        c0 = (u0u1 + u0lu1) / (entries * beta0 * beta1)
        alpha1 = (u1u1 + u1lu1) / (entries * beta1 * beta1)
        r1 = 1.0 / beta1
        keep = (1.0 - alpha1) * r1
        k0 = keep * s0 - c0 / beta0
        k1 = keep * s1 + s0 * r1
        k2 = s1 * r1
        row = lax.broadcasted_iota(jnp.int32, (2, 2), 0)
        col = lax.broadcasted_iota(jnp.int32, (2, 2), 1)
        coef_ref[...] = jnp.where(
            row == 0, jnp.where(col == 0, alpha0, alpha1), jnp.where(col == 0, beta0, beta1)
        )
        coarse = k0 * y0_ref[...] + k1 * y1_ref[...] + k2 * y2_ref[...]
        distances = pair_distances()
        low_half = lax.broadcasted_iota(jnp.int32, coarse.shape, 1) < LEV
        for pair in range(PAIRS):
            matrix = hat(widths_ref, pair, distances)
            first, second = members((ens_ref,), pair)
            summed = field_sum(first, second, coarse, low_half)
            out = product(summed, matrix) * scales_ref[pair : pair + 1, :]
            vector_ref[:, pair * CH : (pair + 1) * CH] = out.astype(BF16)

    return body


def from_neighbours(up, down, axis, paired):
    count = lax.axis_size(axis)
    if paired and count % 2 == 0:
        odd = lax.axis_index(axis) % 2 == 1
        outer = [(at, (at + 1) % count if at % 2 else (at - 1) % count) for at in range(count)]
        inner = [(at, at + 1 - 2 * (at % 2)) for at in range(count)]
        far = lax.ppermute(jnp.where(odd, up, down), axis, outer)
        near = lax.ppermute(jnp.where(odd, down, up), axis, inner)
        return jnp.where(odd, near, far), jnp.where(odd, far, near)
    low = lax.ppermute(up, axis, [(at, (at + 1) % count) for at in range(count)])
    high = lax.ppermute(down, axis, [((at + 1) % count, at) for at in range(count)])
    return low, high


def per_device(ensemble, innovation, obs_weight, lat_offset, lat_weight, band_widths):
    cols, rows = ensemble.shape[0], ensemble.shape[1]
    cells = cols * rows
    fine_cols, fine_rows = innovation.shape[0], innovation.shape[1]
    total = fine_rows + 2 * FINE_HALO
    lat_count, lon_count = lax.axis_size("lat"), lax.axis_size("lon")
    devices = lat_count * lon_count
    entries = float(cells * M * LEV * devices)
    position = lax.axis_index("lat")
    keeps = jnp.stack([position > 0, position < lat_count - 1]).astype(F32)
    flags = jnp.broadcast_to(keeps[:, None], (2, CH))
    keep_low, keep_high = keeps[0], keeps[1]

    edge_block = pltpu.VMEM(((fine_cols + 1) * 2 * FINE_HALO, CH), F32)
    pair_block = pltpu.VMEM((PAIRS, CH), F32)
    up, down, own, own_stencil, widths, scales = pl.pallas_call(
        prepare_kernel(),
        out_shape=(
            edge_block, edge_block, pltpu.VMEM((fine_cols, 2 * fine_rows, CH), F32),
            pltpu.VMEM((2 * fine_rows, CH), F32), pair_block, pair_block,
        ),
        in_specs=[VMEM_SPEC] * 5,
        out_specs=(VMEM_SPEC,) * 6,
    )(obs_weight, innovation, lat_weight[None], lat_offset[None], band_widths[None])
    low, high = from_neighbours(up, down, "lat", False)
    tall, stencil = kernel_call(
        join_kernel(),
        (pltpu.VMEM((fine_cols, 2 * total, CH), F32), pltpu.VMEM((2 * total, CH), F32)),
        (low, high, own, own_stencil, flags),
    )
    left, right = from_neighbours(tall[-3:], tall[:3], "lon", True)
    weight = jnp.concatenate([left, tall, right], axis=0)

    ens = ensemble.reshape(cells, M * CH)
    edge_rows = pltpu.VMEM((cols, M * CH), F32)
    ens_up, ens_down = kernel_call(edges_kernel(cols, rows), (edge_rows, edge_rows), (ens, stencil))
    ens_low, ens_high = from_neighbours(ens_up, ens_down, "lat", False)

    cell_block = pltpu.VMEM((cells, CH), F32)
    restrict_scratch = (
        pltpu.VMEM((cols * 5, total, CH), F32),
        pltpu.VMEM((cols, 2 * rows + 8, CH), F32),
    )
    middle_scratch = (pltpu.VMEM((cols + 6, total + 16, CH), F32),) + restrict_scratch

    y0, b0 = kernel_call(
        start_kernel(cols, rows), (cell_block, cell_block),
        (weight, stencil, ens, widths, scales), restrict_scratch,
    )
    block = b0.reshape(cols, rows, CH)
    low_rows, high_rows = from_neighbours(block[:, -2:], block[:, :2], "lat", False)
    mid = jnp.concatenate([low_rows * keep_low, block, high_rows * keep_high], axis=1)
    y1, b1, mid1 = kernel_call(
        step_kernel(cols, rows), (cell_block, cell_block, pltpu.VMEM((cols, rows + 2, CH), F32)),
        (mid, *from_neighbours(mid[-3:], mid[:3], "lon", True), weight, stencil, flags,
         ens, ens_low, ens_high, widths, scales),
        middle_scratch + (pltpu.VMEM((2 * cols, CH), F32),),
    )
    y2, dots = kernel_call(
        last_kernel(rows, devices), (cell_block, pltpu.VMEM((devices, CH), F32)),
        (mid1, *from_neighbours(mid1[-3:], mid1[:3], "lon", True), weight, stencil, y0, b0, y1, b1),
        middle_scratch,
    )
    shared = lax.all_to_all(dots.reshape(devices, 1, CH), ("lat", "lon"), 0, 0).reshape(devices, CH)
    coefficients, vector = kernel_call(
        final_kernel(entries),
        (jax.ShapeDtypeStruct((2, 2), F32), jax.ShapeDtypeStruct((cells, M * LEV), BF16)),
        (shared, y0, y1, y2, ens, widths, scales),
    )
    return coefficients, vector.reshape(cols, rows, M * LEV)


def solution(mesh):
    return jax.shard_map(
        per_device,
        mesh=mesh,
        in_specs=(
            P("lon", "lat", None),
            P("lon", "lat", None),
            P("lon", "lat", None),
            P("lat"),
            P("lat"),
            P(),
        ),
        out_specs=(P(), P("lon", "lat", None)),
        check_vma=False,
    )
```

time: 53.9 us -> 54.3 us (level)
  Pallas kernels: 4.11 us -> 5.61 us
  local copies, waits for them, and re-layouts: 1.98 us -> 0.66 us
  waiting for transfers between devices: 21.1 us -> 19.8 us
  starting transfers between devices: 14.9 us -> 16.1 us
  blocking collectives: 9.06 us -> 9.78 us
    ppermute x12, waiting for transfers between devices: 21.1 us -> 19.8 us  [the longest x3 8.05 us: from_neighbours(): lax.ppermute(up, axis, [(at, (at + 1) % count) for at in range(count)])]
    ppermute x12, starting transfers between devices: 14.9 us -> 16.1 us  [the longest x3 6.83 us: from_neighbours(): lax.ppermute(up, axis, [(at, (at + 1) % count) for at in range(count)])]
    pallas_call x0 -> x1, Pallas kernels: none -> 0.99 us  [per_device(): pl.pallas_call(prepare_kernel(), out_shape=(edge_block, edge_block, pltpu...]
    all_to_all x1, blocking collectives: 9.06 us -> 9.78 us  [per_device(): lax.all_to_all(dots.reshape(devices, 1, CH), ('lat', 'lon'), 0, 0)]
    unnamed x8 -> x2, local copies, waits for them, and re-layouts: 0.6 us -> 0.01 us
    convert_element_type x2 -> x1, other arithmetic: 0.66 us -> 0.08 us  [per_device(): keeps = jnp.stack([position > 0, position < lat_count - 1]).astype(F32)]
    concatenate x2 -> x0, local copies, waits for them, and re-layouts: 0.58 us -> none  [the longest x1 0.35 us: per_device(): jnp.concatenate([low_fields[:, :4], obs_weight, high_fields[:, :4], low_f...]
    pallas_call x4 -> x6, Pallas kernels: 4.11 us -> 4.62 us  [kernel_call(): pl.pallas_call(body, out_shape=outs, in_specs=[VMEM_SPEC] * len(operands)...]
  transfers between devices with their start and end apart: 12 -> 12, of which waited for: 11 -> 8; matrix products, arithmetic and copies ran while one was open for 1% -> 2% of each run, Pallas kernels for 0% -> 0%
where the time goes in v2:
time: 54.3 us; the launch traced here: 54.1 us
  waiting for transfers between devices  19.8 us (36%)
  starting transfers between devices  16.1 us (30%)
  blocking collectives  9.78 us (18%)
  Pallas kernels  5.61 us (10%)
  other arithmetic  1.47 us (3%)
  between operations  0.76 us (1%)
  local copies, waits for them, and re-layouts  0.66 us (1%)
    all_to_all x1, blocking collectives, per_device(): lax.all_to_all(dots.reshape(devices, 1, CH), ('lat', 'lon'), 0, 0)  9.78 us
    ppermute x3, waiting for transfers between devices, from_neighbours(): lax.ppermute(up, axis, [(at, (at + 1) % count) for at in range(count)])  8.05 us
    ppermute x3, waiting for transfers between devices, from_neighbours(): far = lax.ppermute(jnp.where(odd, up, down), axis, outer)  7.14 us
    ppermute x3, starting transfers between devices, from_neighbours(): lax.ppermute(up, axis, [(at, (at + 1) % count) for at in range(count)])  6.83 us
    ppermute x3, starting transfers between devices, from_neighbours(): far = lax.ppermute(jnp.where(odd, up, down), axis, outer)  6.02 us
    pallas_call x6, Pallas kernels, kernel_call(): pl.pallas_call(body, out_shape=outs, in_specs=[VMEM_SPEC] * len(operands)...  4.62 us
    ppermute x3, waiting for transfers between devices, from_neighbours(): lax.ppermute(down, axis, [((at + 1) % count, at) for at in range(count)])  4.57 us
    ppermute x3, starting transfers between devices, from_neighbours(): lax.ppermute(down, axis, [((at + 1) % count, at) for at in range(count)])  3.16 us
  transfers between devices with their start and end apart: 12, of which 8 were waited for; matrix products, arithmetic and copies ran while one was open for 2% of the time, Pallas kernels for 0%

profile of v2, /device:TPU:0, one launch (start us, length us, event | category | flops | bytes accessed | tf_op | source)
XLA Modules:
  0.0 54.1 jit_solution(16208028078628797743)
XLA Ops:
  0.6 1.0 %shard_map.77 = (f32[108,128]{1,0:T(8,128)S(1)}, f32[108,128]{1,0:T(8,128)S(1)}, f32[8,32,128]{2,1,0:T(8,128)S(1)}, f32[32,128]{1,0:T(8,128)S(1)}, f32[40,128]{1,0:T(8,128)S(1)}, /*index=5*/f32[40,128]{1,0:T(8,128)S(1)}) custom-call(f32[8,16,128]{2,1,0:T(8,128)} %weight_ref.1, f32[8,16,128]{2,1,0:T(8,128)} %innovation_ref.1, f32[1,16]{1,0:T(1,128)} %bitcast.30, ...), custom_call_target="tpu_custom_call" | custom-call | tf_op jit(solution)/shard_map/pallas_call | solution.py:395
  1.6 3.0 %collective-permute-start = (f32[108,128]{1,0:T(8,128)S(1)}, f32[108,128]{1,0:T(8,128)S(1)}, u32[]{:S(2)}, u32[]{:S(2)}) collective-permute-start(f32[108,128]{1,0:T(8,128)S(1)} %get-tuple-element.21), channel_id=1, source_target_pairs={{0,8},{8,16},{16,24},{24,0},{1,9},{9,17},{17,25},{25,1},{2,10},{10... | collective-permute-start | bytes 165896 | tf_op jit(solution)/shard_map/ppermute | solution.py:375
  4.7 1.0 %collective-permute-start.1 = (f32[108,128]{1,0:T(8,128)S(1)}, f32[108,128]{1,0:T(8,128)S(1)}, u32[]{:S(2)}, u32[]{:S(2)}) collective-permute-start(f32[108,128]{1,0:T(8,128)S(1)} %get-tuple-element.22), channel_id=1, source_target_pairs={{8,0},{16,8},{24,16},{0,24},{9,1},{17,9},{25,17},{1,25},{10,2},{18... | collective-permute-start | bytes 165896 | tf_op jit(solution)/shard_map/ppermute | solution.py:376
  5.7 0.1 add_convert_fusion
  5.7 2.0 %collective-permute-done.low_ref = f32[108,128]{1,0:T(8,128)S(1)} collective-permute-done((f32[108,128]{1,0:T(8,128)S(1)}, f32[108,128]{1,0:T(8,128)S(1)}, u32[]{:S(2)}, u32[]{:S(2)}) %collective-permute-start) | collective-permute-done | bytes 55328 | tf_op jit(solution)/shard_map/ppermute | solution.py:375
  7.8 1.2 %collective-permute-done.1.high_ref = f32[108,128]{1,0:T(8,128)S(1)} collective-permute-done((f32[108,128]{1,0:T(8,128)S(1)}, f32[108,128]{1,0:T(8,128)S(1)}, u32[]{:S(2)}, u32[]{:S(2)}) %collective-permute-start.1) | collective-permute-done | bytes 55328 | tf_op jit(solution)/shard_map/ppermute | solution.py:376
  9.0 0.1 broadcast_in_dim.18.flags_ref
  9.1 0.0 copy-start
  9.1 0.1 collective-permute-start.2
  9.2 3.7 %collective-permute-start.3 = (f32[3,56,128]{2,1,0:T(8,128)S(1)}, f32[3,56,128]{2,1,0:T(8,128)S(1)}, u32[]{:S(2)}, u32[]{:S(2)}) collective-permute-start(f32[3,56,128]{2,1,0:T(8,128)S(1)} %get-tuple-element.41), channel_id=1, source_target_pairs={{0,7},{1,2},{2,1},{3,4},{4,3},{5,6},{6,5},{7,0},{8,15},{9,10},{10,... | collective-permute-start | bytes 258056 | tf_op jit(solution)/shard_map/ppermute | solution.py:372
  12.9 0.0 collective-permute-done.2
  12.9 2.3 %collective-permute-done.3 = f32[3,56,128]{2,1,0:T(8,128)S(1)} collective-permute-done((f32[3,56,128]{2,1,0:T(8,128)S(1)}, f32[3,56,128]{2,1,0:T(8,128)S(1)}, u32[]{:S(2)}, u32[]{:S(2)}) %collective-permute-start.3) | collective-permute-done | bytes 86048 | tf_op jit(solution)/shard_map/ppermute | solution.py:372
  15.3 0.0 copy-done
  15.3 1.2 %shard_map.79 = (f32[32,128]{1,0:T(8,128)S(1)}, f32[32,128]{1,0:T(8,128)S(1)}) custom-call(f32[14,56,128]{2,1,0:T(8,128)S(1)} %pad_maximum_fusion.weight_ref, f32[56,128]{1,0:T(8,128)S(1)} %get-tuple-element.26.stencil_ref.after_ref, bf16[32,10240]{1,0:T(8,128)(2,1)S(1)} %bitcast.18, f32[40,128]{1,0:T(8,128)S(1)} %get-tuple-element.27.widths_ref, ...), custom_call_target="tpu_custom_call" | custom-call | tf_op jit(solution)/shard_map/pallas_call | solution.py:30
  16.5 2.3 %collective-permute-start.4 = (f32[4,2,128]{2,1,0:T(2,128)S(1)}, f32[4,2,128]{2,1,0:T(2,128)S(1)}, u32[]{:S(2)}, u32[]{:S(2)}) collective-permute-start(f32[4,2,128]{2,1,0:T(2,128)S(1)} %get-tuple-element.52), channel_id=1, source_target_pairs={{0,8},{8,16},{16,24},{24,0},{1,9},{9,17},{17,25},{25,1},{2,10},{10... | collective-permute-start | bytes 12296 | tf_op jit(solution)/shard_map/ppermute | solution.py:375
  18.8 0.6 %fusion.1 = (f32[1]{0:T(128)}, f32[1]{0:T(128)}) fusion(f32[2]{0:T(128)S(1)} %add_convert_fusion), kind=kLoop, calls=%fused_computation.18 | loop fusion | bytes 16 | tf_op jit(solution)/shard_map/slice | solution.py:391
  19.4 0.7 %collective-permute-start.5 = (f32[4,2,128]{2,1,0:T(2,128)S(1)}, f32[4,2,128]{2,1,0:T(2,128)S(1)}, u32[]{:S(2)}, u32[]{:S(2)}) collective-permute-start(f32[4,2,128]{2,1,0:T(2,128)S(1)} %get-tuple-element.53), channel_id=1, source_target_pairs={{8,0},{16,8},{24,16},{0,24},{9,1},{17,9},{25,17},{1,25},{10,2},{18... | collective-permute-start | bytes 12296 | tf_op jit(solution)/shard_map/ppermute | solution.py:376
  20.1 1.0 %collective-permute-done.4 = f32[4,2,128]{2,1,0:T(2,128)S(1)} collective-permute-done((f32[4,2,128]{2,1,0:T(2,128)S(1)}, f32[4,2,128]{2,1,0:T(2,128)S(1)}, u32[]{:S(2)}, u32[]{:S(2)}) %collective-permute-start.4) | collective-permute-done | bytes 4128 | tf_op jit(solution)/shard_map/ppermute | solution.py:375
  21.1 0.6 %broadcast_multiply_fusion.1 = f32[1,8,128]{2,1,0:T(8,128)S(1)} fusion(f32[1,8,128]{2,1,0:T(8,128)S(1)} %bitcast.28, f32[]{:T(128)} %bitcast.7), kind=kLoop, calls=%fused_computation.15 | loop fusion | flops 1024 | bytes 8196 | tf_op jit(solution)/shard_map/mul | solution.py:431
  21.7 1.2 %collective-permute-done.5 = f32[4,2,128]{2,1,0:T(2,128)S(1)} collective-permute-done((f32[4,2,128]{2,1,0:T(2,128)S(1)}, f32[4,2,128]{2,1,0:T(2,128)S(1)}, u32[]{:S(2)}, u32[]{:S(2)}) %collective-permute-start.5) | collective-permute-done | bytes 4128 | tf_op jit(solution)/shard_map/ppermute | solution.py:376
  23.0 0.6 %broadcast_multiply_fusion = f32[1,8,128]{2,1,0:T(8,128)S(1)} fusion(f32[1,8,128]{2,1,0:T(8,128)S(1)} %bitcast.29, f32[]{:T(128)} %bitcast.8), kind=kLoop, calls=%fused_computation.14 | loop fusion | flops 1024 | bytes 8196 | tf_op jit(solution)/shard_map/mul | solution.py:431
  23.7 2.0 %collective-permute-start.7 = (f32[3,12,128]{2,1,0:T(8,128)S(1)}, f32[3,12,128]{2,1,0:T(8,128)S(1)}, u32[]{:S(2)}, u32[]{:S(2)}) collective-permute-start(f32[3,12,128]{2,1,0:T(8,128)S(1)} %get-tuple-element.50), channel_id=1, source_target_pairs={{0,7},{1,2},{2,1},{3,4},{4,3},{5,6},{6,5},{7,0},{8,15},{9,10},{10,... | collective-permute-start | bytes 55304 | tf_op jit(solution)/shard_map/ppermute | solution.py:372
  25.7 0.0 collective-permute-start.6
  25.7 0.2 shard_map.80
  25.9 1.5 %collective-permute-start.8 = (f32[4,10240]{1,0:T(4,128)S(1)}, f32[4,10240]{1,0:T(4,128)S(1)}, u32[]{:S(2)}, u32[]{:S(2)}) collective-permute-start(f32[4,10240]{1,0:T(4,128)S(1)} %get-tuple-element.30), channel_id=1, source_target_pairs={{0,8},{8,16},{16,24},{24,0},{1,9},{9,17},{17,25},{25,1},{2,10},{10... | collective-permute-start | bytes 491528 | tf_op jit(solution)/shard_map/ppermute | solution.py:375
  27.4 1.4 %collective-permute-start.9 = (f32[4,10240]{1,0:T(4,128)S(1)}, f32[4,10240]{1,0:T(4,128)S(1)}, u32[]{:S(2)}, u32[]{:S(2)}) collective-permute-start(f32[4,10240]{1,0:T(4,128)S(1)} %get-tuple-element.31), channel_id=1, source_target_pairs={{8,0},{16,8},{24,16},{0,24},{9,1},{17,9},{25,17},{1,25},{10,2},{18... | collective-permute-start | bytes 491528 | tf_op jit(solution)/shard_map/ppermute | solution.py:376
  28.9 0.0 collective-permute-done.7
  28.9 0.0 collective-permute-done.6
  28.9 5.0 %collective-permute-done.8.ens_low_ref = f32[4,10240]{1,0:T(4,128)S(1)} collective-permute-done((f32[4,10240]{1,0:T(4,128)S(1)}, f32[4,10240]{1,0:T(4,128)S(1)}, u32[]{:S(2)}, u32[]{:S(2)}) %collective-permute-start.8) | collective-permute-done | bytes 163872 | tf_op jit(solution)/shard_map/ppermute | solution.py:375
  33.9 2.1 %collective-permute-done.9.ens_high_ref = f32[4,10240]{1,0:T(4,128)S(1)} collective-permute-done((f32[4,10240]{1,0:T(4,128)S(1)}, f32[4,10240]{1,0:T(4,128)S(1)}, u32[]{:S(2)}, u32[]{:S(2)}) %collective-permute-start.9) | collective-permute-done | bytes 163872 | tf_op jit(solution)/shard_map/ppermute | solution.py:376
  36.0 1.5 %shard_map.81 = (f32[32,128]{1,0:T(8,128)S(1)}, f32[32,128]{1,0:T(8,128)S(1)}, f32[4,10,128]{2,1,0:T(8,128)S(1)}) custom-call(f32[4,12,128]{2,1,0:T(8,128)S(1)} %pad_maximum_fusion.1.mid_ref, f32[3,12,128]{2,1,0:T(8,128)S(1)} %get-tuple-element.47.left_ref, f32[3,12,128]{2,1,0:T(8,128)S(1)} %get-tuple-element.46.right_ref, ...), custom_call_target="tpu_custom_call" | custom-call | tf_op jit(solution)/shard_map/pallas_call | solution.py:30
  37.6 0.3 collective-permute-start.11
  37.9 0.0 collective-permute-start.10
  37.9 4.8 %collective-permute-done.11 = f32[3,10,128]{2,1,0:T(8,128)S(1)} collective-permute-done((f32[3,10,128]{2,1,0:T(8,128)S(1)}, f32[3,10,128]{2,1,0:T(8,128)S(1)}, u32[]{:S(2)}, u32[]{:S(2)}) %collective-permute-start.11) | collective-permute-done | bytes 15392 | tf_op jit(solution)/shard_map/ppermute | solution.py:372
  42.7 0.0 collective-permute-done.10
  42.7 0.2 shard_map.82
  42.9 9.8 %all_to_all.5 = f32[32,1,128]{2,1,0:T(1,128)S(1)} all-to-all(f32[32,1,128]{2,1,0:T(1,128)S(1)} %bitcast.25), channel_id=1, replica_groups=mesh['lat'=4,'lon'=8] {'lat','lon'}, dimensions={0} | all-to-all | bytes 32768 | tf_op jit(solution)/shard_map/all_to_all | solution.py:443
  52.7 1.4 %shard_map.83 = (f32[2,2]{1,0:T(2,128)}, bf16[32,5120]{1,0:T(8,128)(2,1)}) custom-call(f32[32,128]{1,0:T(8,128)S(1)} %bitcast.24, f32[32,128]{1,0:T(8,128)S(1)} %get-tuple-element.33.y0_ref, f32[32,128]{1,0:T(8,128)S(1)} %get-tuple-element.34.y1_ref, f32[32,128]{1,0:T(8,128)S(1)} %get-tuple-element.37.y2_ref, bf16[32,10240]{1,0:T(8,128)(2,1)S(1)} %bitcast.21, ...), custom_call_target="tpu_custom_call" | custom-call | tf_op jit(solution)/shard_map/pallas_call | solution.py:30
  (10 shorter events, 0.1 us)
Async XLA Ops:
  1.6 6.1 %collective-permute-start = (f32[108,128]{1,0:T(8,128)S(1)}, f32[108,128]{1,0:T(8,128)S(1)}, u32[]{:S(2)}, u32[]{:S(2)}) collective-permute-start(f32[108,128]{1,0:T(8,128)S(1)} %get-tuple-element.21), channel_id=1, source_target_pairs={{0,8},{8,16},{16,24},{24,0},{1,9},{9,17},{17,25},{25,1},{2,10},{10... | collective-permute-start | bytes 165896 | tf_op jit(solution)/shard_map/ppermute | solution.py:375
  4.7 4.4 %collective-permute-start.1 = (f32[108,128]{1,0:T(8,128)S(1)}, f32[108,128]{1,0:T(8,128)S(1)}, u32[]{:S(2)}, u32[]{:S(2)}) collective-permute-start(f32[108,128]{1,0:T(8,128)S(1)} %get-tuple-element.22), channel_id=1, source_target_pairs={{8,0},{16,8},{24,16},{0,24},{9,1},{17,9},{25,17},{1,25},{10,2},{18... | collective-permute-start | bytes 165896 | tf_op jit(solution)/shard_map/ppermute | solution.py:376
  9.1 6.2 %copy-start = (bf16[4,8,10240]{2,1,0:T(8,128)(2,1)S(1)}, bf16[4,8,10240]{2,1,0:T(8,128)(2,1)}, u32[]{:S(2)}) copy-start(bf16[4,8,10240]{2,1,0:T(8,128)(2,1)} %param.6) | copy-start | bytes 1966084
  9.1 3.8 %collective-permute-start.2 = (f32[3,56,128]{2,1,0:T(8,128)S(1)}, f32[3,56,128]{2,1,0:T(8,128)S(1)}, u32[]{:S(2)}, u32[]{:S(2)}) collective-permute-start(f32[3,56,128]{2,1,0:T(8,128)S(1)} %get-tuple-element.40), channel_id=1, source_target_pairs={{0,1},{1,0},{2,3},{3,2},{4,5},{5,4},{6,7},{7,6},{8,9},{9,8},{10,11... | collective-permute-start | bytes 258056 | tf_op jit(solution)/shard_map/ppermute | solution.py:373
  9.2 6.0 %collective-permute-start.3 = (f32[3,56,128]{2,1,0:T(8,128)S(1)}, f32[3,56,128]{2,1,0:T(8,128)S(1)}, u32[]{:S(2)}, u32[]{:S(2)}) collective-permute-start(f32[3,56,128]{2,1,0:T(8,128)S(1)} %get-tuple-element.41), channel_id=1, source_target_pairs={{0,7},{1,2},{2,1},{3,4},{4,3},{5,6},{6,5},{7,0},{8,15},{9,10},{10,... | collective-permute-start | bytes 258056 | tf_op jit(solution)/shard_map/ppermute | solution.py:372
  16.5 4.6 %collective-permute-start.4 = (f32[4,2,128]{2,1,0:T(2,128)S(1)}, f32[4,2,128]{2,1,0:T(2,128)S(1)}, u32[]{:S(2)}, u32[]{:S(2)}) collective-permute-start(f32[4,2,128]{2,1,0:T(2,128)S(1)} %get-tuple-element.52), channel_id=1, source_target_pairs={{0,8},{8,16},{16,24},{24,0},{1,9},{9,17},{17,25},{25,1},{2,10},{10... | collective-permute-start | bytes 12296 | tf_op jit(solution)/shard_map/ppermute | solution.py:375
  19.4 3.6 %collective-permute-start.5 = (f32[4,2,128]{2,1,0:T(2,128)S(1)}, f32[4,2,128]{2,1,0:T(2,128)S(1)}, u32[]{:S(2)}, u32[]{:S(2)}) collective-permute-start(f32[4,2,128]{2,1,0:T(2,128)S(1)} %get-tuple-element.53), channel_id=1, source_target_pairs={{8,0},{16,8},{24,16},{0,24},{9,1},{17,9},{25,17},{1,25},{10,2},{18... | collective-permute-start | bytes 12296 | tf_op jit(solution)/shard_map/ppermute | solution.py:376
  23.7 5.2 %collective-permute-start.7 = (f32[3,12,128]{2,1,0:T(8,128)S(1)}, f32[3,12,128]{2,1,0:T(8,128)S(1)}, u32[]{:S(2)}, u32[]{:S(2)}) collective-permute-start(f32[3,12,128]{2,1,0:T(8,128)S(1)} %get-tuple-element.50), channel_id=1, source_target_pairs={{0,7},{1,2},{2,1},{3,4},{4,3},{5,6},{6,5},{7,0},{8,15},{9,10},{10,... | collective-permute-start | bytes 55304 | tf_op jit(solution)/shard_map/ppermute | solution.py:372
  25.7 3.2 %collective-permute-start.6 = (f32[3,12,128]{2,1,0:T(8,128)S(1)}, f32[3,12,128]{2,1,0:T(8,128)S(1)}, u32[]{:S(2)}, u32[]{:S(2)}) collective-permute-start(f32[3,12,128]{2,1,0:T(8,128)S(1)} %get-tuple-element.51), channel_id=1, source_target_pairs={{0,1},{1,0},{2,3},{3,2},{4,5},{5,4},{6,7},{7,6},{8,9},{9,8},{10,11... | collective-permute-start | bytes 55304 | tf_op jit(solution)/shard_map/ppermute | solution.py:373
  25.9 8.0 %collective-permute-start.8 = (f32[4,10240]{1,0:T(4,128)S(1)}, f32[4,10240]{1,0:T(4,128)S(1)}, u32[]{:S(2)}, u32[]{:S(2)}) collective-permute-start(f32[4,10240]{1,0:T(4,128)S(1)} %get-tuple-element.30), channel_id=1, source_target_pairs={{0,8},{8,16},{16,24},{24,0},{1,9},{9,17},{17,25},{25,1},{2,10},{10... | collective-permute-start | bytes 491528 | tf_op jit(solution)/shard_map/ppermute | solution.py:375
  27.4 8.6 %collective-permute-start.9 = (f32[4,10240]{1,0:T(4,128)S(1)}, f32[4,10240]{1,0:T(4,128)S(1)}, u32[]{:S(2)}, u32[]{:S(2)}) collective-permute-start(f32[4,10240]{1,0:T(4,128)S(1)} %get-tuple-element.31), channel_id=1, source_target_pairs={{8,0},{16,8},{24,16},{0,24},{9,1},{17,9},{25,17},{1,25},{10,2},{18... | collective-permute-start | bytes 491528 | tf_op jit(solution)/shard_map/ppermute | solution.py:376
  37.6 5.1 %collective-permute-start.11 = (f32[3,10,128]{2,1,0:T(8,128)S(1)}, f32[3,10,128]{2,1,0:T(8,128)S(1)}, u32[]{:S(2)}, u32[]{:S(2)}) collective-permute-start(f32[3,10,128]{2,1,0:T(8,128)S(1)} %get-tuple-element.48), channel_id=1, source_target_pairs={{0,7},{1,2},{2,1},{3,4},{4,3},{5,6},{6,5},{7,0},{8,15},{9,10},{10,... | collective-permute-start | bytes 46088 | tf_op jit(solution)/shard_map/ppermute | solution.py:372
  37.9 4.8 %collective-permute-start.10 = (f32[3,10,128]{2,1,0:T(8,128)S(1)}, f32[3,10,128]{2,1,0:T(8,128)S(1)}, u32[]{:S(2)}, u32[]{:S(2)}) collective-permute-start(f32[3,10,128]{2,1,0:T(8,128)S(1)} %get-tuple-element.49), channel_id=1, source_target_pairs={{0,1},{1,0},{2,3},{3,2},{4,5},{5,4},{6,7},{7,6},{8,9},{9,8},{10,11... | collective-permute-start | bytes 46088 | tf_op jit(solution)/shard_map/ppermute | solution.py:373

commit v3 on v2

--- a/solution.py
+++ b/solution.py
@@ -224,7 +224,7 @@
     return jnp.concatenate(blocks, axis=0)
 
 
-def middle(mid_ref, left_ref, right_ref, weight_ref, coefs, dup_ref, spill_ref, sum_ref, rows, halo):
+def middle(mid_ref, left_ref, right_ref, weight_ref, coefs, dup_ref, spill_ref, sum_ref, rows, halo, mask=None):
     cols = mid_ref.shape[0]
     first, count = fine_span(rows, halo)
     given = rows + 2 * halo + 2
@@ -236,6 +236,8 @@
             block = mid_ref[col - 3]
         else:
             block = right_ref[col - cols - 3]
+        if mask is not None:
+            block = block * mask
         dup_ref[col] = jnp.zeros(dup_ref.shape[1:], F32)
         dup_ref[col, pl.ds(PAD, given, stride=2), :] = block
         dup_ref[col, pl.ds(PAD + 1, given, stride=2), :] = block
@@ -275,8 +277,10 @@
     def body(mid_ref, left_ref, right_ref, weight_ref, stencil_ref, flags_ref, ens_ref, ens_low_ref, ens_high_ref,
              widths_ref, scales_ref, coarse_ref, image_ref, padded_ref, dup_ref, spill_ref, sum_ref, rim_ref):
         coefs = lat_coefficients(stencil_ref, rows, 1)
+        row = lax.broadcasted_iota(jnp.int32, (rows + 4, CH), 0)
+        inside = jnp.where(row < 2, flags_ref[0:1, :], jnp.where(row < rows + 2, 1.0, flags_ref[1:2, :]))
         coarse = middle(
-            mid_ref, left_ref, right_ref, weight_ref, coefs, dup_ref, spill_ref, sum_ref, rows, 1
+            mid_ref, left_ref, right_ref, weight_ref, coefs, dup_ref, spill_ref, sum_ref, rows, 1, inside
         )
         coarse_ref[...] = coarse
         end = 2 * rows + 2
@@ -388,7 +392,6 @@
     position = lax.axis_index("lat")
     keeps = jnp.stack([position > 0, position < lat_count - 1]).astype(F32)
     flags = jnp.broadcast_to(keeps[:, None], (2, CH))
-    keep_low, keep_high = keeps[0], keeps[1]
 
     edge_block = pltpu.VMEM(((fine_cols + 1) * 2 * FINE_HALO, CH), F32)
     pair_block = pltpu.VMEM((PAIRS, CH), F32)
@@ -428,7 +431,7 @@
     )
     block = b0.reshape(cols, rows, CH)
     low_rows, high_rows = from_neighbours(block[:, -2:], block[:, :2], "lat", False)
-    mid = jnp.concatenate([low_rows * keep_low, block, high_rows * keep_high], axis=1)
+    mid = jnp.concatenate([low_rows, block, high_rows], axis=1)
     y1, b1, mid1 = kernel_call(
         step_kernel(cols, rows), (cell_block, cell_block, pltpu.VMEM((cols, rows + 2, CH), F32)),
         (mid, *from_neighbours(mid[-3:], mid[:3], "lon", True), weight, stencil, flags,

time: 54.3 us -> 53.1 us (0.978)
  other arithmetic: 1.47 us -> 0.17 us
  waiting for transfers between devices: 19.8 us -> 20.4 us
  local copies, waits for them, and re-layouts: 0.66 us -> 0.08 us
    mul x2 -> x0, other arithmetic: 1.29 us -> none  [the longest x1 0.65 us: per_device(): high_rows * keep_high]
    ppermute x3, waiting for transfers between devices: 8.05 us -> 8.63 us  [from_neighbours(): lax.ppermute(up, axis, [(at, (at + 1) % count) for at in range(count)])]
    slice x1 -> x0, local copies, waits for them, and re-layouts: 0.58 us -> none  [per_device(): keep_low, keep_high = (keeps[0], keeps[1])]
  transfers between devices with their start and end apart: 12 -> 12, of which waited for: 8 -> 8; matrix products, arithmetic and copies ran while one was open for 2% -> 0% of each run, Pallas kernels for 0% -> 0%
where the time goes in v3:
time: 53.1 us; the launch traced here: 52.9 us
  waiting for transfers between devices  20.4 us (38%)
  starting transfers between devices  16.1 us (30%)
  blocking collectives  9.78 us (18%)
  Pallas kernels  5.61 us (11%)
  between operations  0.74 us (1%)
    all_to_all x1, blocking collectives, per_device(): lax.all_to_all(dots.reshape(devices, 1, CH), ('lat', 'lon'), 0, 0)  9.78 us
    ppermute x3, waiting for transfers between devices, from_neighbours(): lax.ppermute(up, axis, [(at, (at + 1) % count) for at in range(count)])  8.63 us
    ppermute x3, waiting for transfers between devices, from_neighbours(): far = lax.ppermute(jnp.where(odd, up, down), axis, outer)  7.14 us
    ppermute x3, starting transfers between devices, from_neighbours(): lax.ppermute(up, axis, [(at, (at + 1) % count) for at in range(count)])  6.83 us
    ppermute x3, starting transfers between devices, from_neighbours(): far = lax.ppermute(jnp.where(odd, up, down), axis, outer)  6.01 us
    ppermute x3, waiting for transfers between devices, from_neighbours(): lax.ppermute(down, axis, [((at + 1) % count, at) for at in range(count)])  4.64 us
    pallas_call x6, Pallas kernels, kernel_call(): pl.pallas_call(body, out_shape=outs, in_specs=[VMEM_SPEC] * len(operands)...  4.62 us
    ppermute x3, starting transfers between devices, from_neighbours(): lax.ppermute(down, axis, [((at + 1) % count, at) for at in range(count)])  3.16 us
  transfers between devices with their start and end apart: 12, of which 8 were waited for; matrix products, arithmetic and copies ran while one was open for 0% of the time, Pallas kernels for 0%

profile of v3, /device:TPU:0, one launch (start us, length us, event | category | flops | bytes accessed | tf_op | source)
XLA Modules:
  0.0 52.9 jit_solution(4144264253225682819)
XLA Ops:
  0.6 1.0 %shard_map.77 = (f32[108,128]{1,0:T(8,128)S(1)}, f32[108,128]{1,0:T(8,128)S(1)}, f32[8,32,128]{2,1,0:T(8,128)S(1)}, f32[32,128]{1,0:T(8,128)S(1)}, f32[40,128]{1,0:T(8,128)S(1)}, /*index=5*/f32[40,128]{1,0:T(8,128)S(1)}) custom-call(f32[8,16,128]{2,1,0:T(8,128)} %weight_ref.1, f32[8,16,128]{2,1,0:T(8,128)} %innovation_ref.1, f32[1,16]{1,0:T(1,128)} %bitcast.20, ...), custom_call_target="tpu_custom_call" | custom-call | tf_op jit(solution)/shard_map/pallas_call | solution.py:398
  1.6 3.0 %collective-permute-start = (f32[108,128]{1,0:T(8,128)S(1)}, f32[108,128]{1,0:T(8,128)S(1)}, u32[]{:S(2)}, u32[]{:S(2)}) collective-permute-start(f32[108,128]{1,0:T(8,128)S(1)} %get-tuple-element.21), channel_id=1, source_target_pairs={{0,8},{8,16},{16,24},{24,0},{1,9},{9,17},{17,25},{25,1},{2,10},{10... | collective-permute-start | bytes 165896 | tf_op jit(solution)/shard_map/ppermute | solution.py:379
  4.7 1.0 %collective-permute-start.1 = (f32[108,128]{1,0:T(8,128)S(1)}, f32[108,128]{1,0:T(8,128)S(1)}, u32[]{:S(2)}, u32[]{:S(2)}) collective-permute-start(f32[108,128]{1,0:T(8,128)S(1)} %get-tuple-element.22), channel_id=1, source_target_pairs={{8,0},{16,8},{24,16},{0,24},{9,1},{17,9},{25,17},{1,25},{10,2},{18... | collective-permute-start | bytes 165896 | tf_op jit(solution)/shard_map/ppermute | solution.py:380
  5.7 0.1 add_convert_fusion
  5.7 2.0 %collective-permute-done.low_ref = f32[108,128]{1,0:T(8,128)S(1)} collective-permute-done((f32[108,128]{1,0:T(8,128)S(1)}, f32[108,128]{1,0:T(8,128)S(1)}, u32[]{:S(2)}, u32[]{:S(2)}) %collective-permute-start) | collective-permute-done | bytes 55328 | tf_op jit(solution)/shard_map/ppermute | solution.py:379
  7.8 1.2 %collective-permute-done.1.high_ref = f32[108,128]{1,0:T(8,128)S(1)} collective-permute-done((f32[108,128]{1,0:T(8,128)S(1)}, f32[108,128]{1,0:T(8,128)S(1)}, u32[]{:S(2)}, u32[]{:S(2)}) %collective-permute-start.1) | collective-permute-done | bytes 55328 | tf_op jit(solution)/shard_map/ppermute | solution.py:380
  9.0 0.1 broadcast_in_dim.18.flags_ref
  9.1 0.0 copy-start
  9.1 0.1 collective-permute-start.2
  9.2 3.7 %collective-permute-start.3 = (f32[3,56,128]{2,1,0:T(8,128)S(1)}, f32[3,56,128]{2,1,0:T(8,128)S(1)}, u32[]{:S(2)}, u32[]{:S(2)}) collective-permute-start(f32[3,56,128]{2,1,0:T(8,128)S(1)} %get-tuple-element.41), channel_id=1, source_target_pairs={{0,7},{1,2},{2,1},{3,4},{4,3},{5,6},{6,5},{7,0},{8,15},{9,10},{10,... | collective-permute-start | bytes 258056 | tf_op jit(solution)/shard_map/ppermute | solution.py:376
  12.9 0.0 collective-permute-done.2
  12.9 2.3 %collective-permute-done.3 = f32[3,56,128]{2,1,0:T(8,128)S(1)} collective-permute-done((f32[3,56,128]{2,1,0:T(8,128)S(1)}, f32[3,56,128]{2,1,0:T(8,128)S(1)}, u32[]{:S(2)}, u32[]{:S(2)}) %collective-permute-start.3) | collective-permute-done | bytes 86048 | tf_op jit(solution)/shard_map/ppermute | solution.py:376
  15.3 0.0 copy-done
  15.3 1.2 %shard_map.79 = (f32[32,128]{1,0:T(8,128)S(1)}, f32[32,128]{1,0:T(8,128)S(1)}) custom-call(f32[14,56,128]{2,1,0:T(8,128)S(1)} %pad_maximum_fusion.weight_ref, f32[56,128]{1,0:T(8,128)S(1)} %get-tuple-element.26.stencil_ref.after_ref, bf16[32,10240]{1,0:T(8,128)(2,1)S(1)} %bitcast.12, f32[40,128]{1,0:T(8,128)S(1)} %get-tuple-element.27.widths_ref, ...), custom_call_target="tpu_custom_call" | custom-call | tf_op jit(solution)/shard_map/pallas_call | solution.py:30
  16.5 2.3 %collective-permute-start.4 = (f32[4,2,128]{2,1,0:T(2,128)S(1)}, f32[4,2,128]{2,1,0:T(2,128)S(1)}, u32[]{:S(2)}, u32[]{:S(2)}) collective-permute-start(f32[4,2,128]{2,1,0:T(2,128)S(1)} %get-tuple-element.52), channel_id=1, source_target_pairs={{0,8},{8,16},{16,24},{24,0},{1,9},{9,17},{17,25},{25,1},{2,10},{10... | collective-permute-start | bytes 12296 | tf_op jit(solution)/shard_map/ppermute | solution.py:379
  18.8 0.7 %collective-permute-start.5 = (f32[4,2,128]{2,1,0:T(2,128)S(1)}, f32[4,2,128]{2,1,0:T(2,128)S(1)}, u32[]{:S(2)}, u32[]{:S(2)}) collective-permute-start(f32[4,2,128]{2,1,0:T(2,128)S(1)} %get-tuple-element.53), channel_id=1, source_target_pairs={{8,0},{16,8},{24,16},{0,24},{9,1},{17,9},{25,17},{1,25},{10,2},{18... | collective-permute-start | bytes 12296 | tf_op jit(solution)/shard_map/ppermute | solution.py:380
  19.5 1.6 %collective-permute-done.4 = f32[4,2,128]{2,1,0:T(2,128)S(1)} collective-permute-done((f32[4,2,128]{2,1,0:T(2,128)S(1)}, f32[4,2,128]{2,1,0:T(2,128)S(1)}, u32[]{:S(2)}, u32[]{:S(2)}) %collective-permute-start.4) | collective-permute-done | bytes 4128 | tf_op jit(solution)/shard_map/ppermute | solution.py:379
  21.1 1.3 %collective-permute-done.5 = f32[4,2,128]{2,1,0:T(2,128)S(1)} collective-permute-done((f32[4,2,128]{2,1,0:T(2,128)S(1)}, f32[4,2,128]{2,1,0:T(2,128)S(1)}, u32[]{:S(2)}, u32[]{:S(2)}) %collective-permute-start.5) | collective-permute-done | bytes 4128 | tf_op jit(solution)/shard_map/ppermute | solution.py:380
  22.4 2.0 %collective-permute-start.7 = (f32[3,12,128]{2,1,0:T(8,128)S(1)}, f32[3,12,128]{2,1,0:T(8,128)S(1)}, u32[]{:S(2)}, u32[]{:S(2)}) collective-permute-start(f32[3,12,128]{2,1,0:T(8,128)S(1)} %get-tuple-element.50), channel_id=1, source_target_pairs={{0,7},{1,2},{2,1},{3,4},{4,3},{5,6},{6,5},{7,0},{8,15},{9,10},{10,... | collective-permute-start | bytes 55304 | tf_op jit(solution)/shard_map/ppermute | solution.py:376
  24.4 0.0 collective-permute-start.6
  24.4 0.2 shard_map.80
  24.6 1.5 %collective-permute-start.8 = (f32[4,10240]{1,0:T(4,128)S(1)}, f32[4,10240]{1,0:T(4,128)S(1)}, u32[]{:S(2)}, u32[]{:S(2)}) collective-permute-start(f32[4,10240]{1,0:T(4,128)S(1)} %get-tuple-element.30), channel_id=1, source_target_pairs={{0,8},{8,16},{16,24},{24,0},{1,9},{9,17},{17,25},{25,1},{2,10},{10... | collective-permute-start | bytes 491528 | tf_op jit(solution)/shard_map/ppermute | solution.py:379
  26.2 1.4 %collective-permute-start.9 = (f32[4,10240]{1,0:T(4,128)S(1)}, f32[4,10240]{1,0:T(4,128)S(1)}, u32[]{:S(2)}, u32[]{:S(2)}) collective-permute-start(f32[4,10240]{1,0:T(4,128)S(1)} %get-tuple-element.31), channel_id=1, source_target_pairs={{8,0},{16,8},{24,16},{0,24},{9,1},{17,9},{25,17},{1,25},{10,2},{18... | collective-permute-start | bytes 491528 | tf_op jit(solution)/shard_map/ppermute | solution.py:380
  27.6 0.0 collective-permute-done.7
  27.6 0.0 collective-permute-done.6
  27.6 5.0 %collective-permute-done.8.ens_low_ref = f32[4,10240]{1,0:T(4,128)S(1)} collective-permute-done((f32[4,10240]{1,0:T(4,128)S(1)}, f32[4,10240]{1,0:T(4,128)S(1)}, u32[]{:S(2)}, u32[]{:S(2)}) %collective-permute-start.8) | collective-permute-done | bytes 163872 | tf_op jit(solution)/shard_map/ppermute | solution.py:379
  32.7 2.1 %collective-permute-done.9.ens_high_ref = f32[4,10240]{1,0:T(4,128)S(1)} collective-permute-done((f32[4,10240]{1,0:T(4,128)S(1)}, f32[4,10240]{1,0:T(4,128)S(1)}, u32[]{:S(2)}, u32[]{:S(2)}) %collective-permute-start.9) | collective-permute-done | bytes 163872 | tf_op jit(solution)/shard_map/ppermute | solution.py:380
  34.8 1.5 %shard_map.81 = (f32[32,128]{1,0:T(8,128)S(1)}, f32[32,128]{1,0:T(8,128)S(1)}, f32[4,10,128]{2,1,0:T(8,128)S(1)}) custom-call(f32[4,12,128]{2,1,0:T(8,128)S(1)} %pad_maximum_fusion.1.mid_ref, f32[3,12,128]{2,1,0:T(8,128)S(1)} %get-tuple-element.47.left_ref, f32[3,12,128]{2,1,0:T(8,128)S(1)} %get-tuple-element.46.right_ref, ...), custom_call_target="tpu_custom_call" | custom-call | tf_op jit(solution)/shard_map/pallas_call | solution.py:30
  36.3 0.3 collective-permute-start.11
  36.6 0.0 collective-permute-start.10
  36.6 4.8 %collective-permute-done.11 = f32[3,10,128]{2,1,0:T(8,128)S(1)} collective-permute-done((f32[3,10,128]{2,1,0:T(8,128)S(1)}, f32[3,10,128]{2,1,0:T(8,128)S(1)}, u32[]{:S(2)}, u32[]{:S(2)}) %collective-permute-start.11) | collective-permute-done | bytes 15392 | tf_op jit(solution)/shard_map/ppermute | solution.py:376
  41.4 0.0 collective-permute-done.10
  41.4 0.2 shard_map.82
  41.7 9.8 %all_to_all.5 = f32[32,1,128]{2,1,0:T(1,128)S(1)} all-to-all(f32[32,1,128]{2,1,0:T(1,128)S(1)} %bitcast.19), channel_id=1, replica_groups=mesh['lat'=4,'lon'=8] {'lat','lon'}, dimensions={0} | all-to-all | bytes 32768 | tf_op jit(solution)/shard_map/all_to_all | solution.py:446
  51.5 1.4 %shard_map.83 = (f32[2,2]{1,0:T(2,128)}, bf16[32,5120]{1,0:T(8,128)(2,1)}) custom-call(f32[32,128]{1,0:T(8,128)S(1)} %bitcast.18, f32[32,128]{1,0:T(8,128)S(1)} %get-tuple-element.33.y0_ref, f32[32,128]{1,0:T(8,128)S(1)} %get-tuple-element.34.y1_ref, f32[32,128]{1,0:T(8,128)S(1)} %get-tuple-element.37.y2_ref, bf16[32,10240]{1,0:T(8,128)(2,1)S(1)} %bitcast.15, ...), custom_call_target="tpu_custom_call" | custom-call | tf_op jit(solution)/shard_map/pallas_call | solution.py:30
  (10 shorter events, 0.1 us)
Async XLA Ops:
  1.6 6.1 %collective-permute-start = (f32[108,128]{1,0:T(8,128)S(1)}, f32[108,128]{1,0:T(8,128)S(1)}, u32[]{:S(2)}, u32[]{:S(2)}) collective-permute-start(f32[108,128]{1,0:T(8,128)S(1)} %get-tuple-element.21), channel_id=1, source_target_pairs={{0,8},{8,16},{16,24},{24,0},{1,9},{9,17},{17,25},{25,1},{2,10},{10... | collective-permute-start | bytes 165896 | tf_op jit(solution)/shard_map/ppermute | solution.py:379
  4.7 4.4 %collective-permute-start.1 = (f32[108,128]{1,0:T(8,128)S(1)}, f32[108,128]{1,0:T(8,128)S(1)}, u32[]{:S(2)}, u32[]{:S(2)}) collective-permute-start(f32[108,128]{1,0:T(8,128)S(1)} %get-tuple-element.22), channel_id=1, source_target_pairs={{8,0},{16,8},{24,16},{0,24},{9,1},{17,9},{25,17},{1,25},{10,2},{18... | collective-permute-start | bytes 165896 | tf_op jit(solution)/shard_map/ppermute | solution.py:380
  9.1 6.2 %copy-start = (bf16[4,8,10240]{2,1,0:T(8,128)(2,1)S(1)}, bf16[4,8,10240]{2,1,0:T(8,128)(2,1)}, u32[]{:S(2)}) copy-start(bf16[4,8,10240]{2,1,0:T(8,128)(2,1)} %param.6) | copy-start | bytes 1966084
  9.1 3.8 %collective-permute-start.2 = (f32[3,56,128]{2,1,0:T(8,128)S(1)}, f32[3,56,128]{2,1,0:T(8,128)S(1)}, u32[]{:S(2)}, u32[]{:S(2)}) collective-permute-start(f32[3,56,128]{2,1,0:T(8,128)S(1)} %get-tuple-element.40), channel_id=1, source_target_pairs={{0,1},{1,0},{2,3},{3,2},{4,5},{5,4},{6,7},{7,6},{8,9},{9,8},{10,11... | collective-permute-start | bytes 258056 | tf_op jit(solution)/shard_map/ppermute | solution.py:377
  9.2 6.0 %collective-permute-start.3 = (f32[3,56,128]{2,1,0:T(8,128)S(1)}, f32[3,56,128]{2,1,0:T(8,128)S(1)}, u32[]{:S(2)}, u32[]{:S(2)}) collective-permute-start(f32[3,56,128]{2,1,0:T(8,128)S(1)} %get-tuple-element.41), channel_id=1, source_target_pairs={{0,7},{1,2},{2,1},{3,4},{4,3},{5,6},{6,5},{7,0},{8,15},{9,10},{10,... | collective-permute-start | bytes 258056 | tf_op jit(solution)/shard_map/ppermute | solution.py:376
  16.5 4.6 %collective-permute-start.4 = (f32[4,2,128]{2,1,0:T(2,128)S(1)}, f32[4,2,128]{2,1,0:T(2,128)S(1)}, u32[]{:S(2)}, u32[]{:S(2)}) collective-permute-start(f32[4,2,128]{2,1,0:T(2,128)S(1)} %get-tuple-element.52), channel_id=1, source_target_pairs={{0,8},{8,16},{16,24},{24,0},{1,9},{9,17},{17,25},{25,1},{2,10},{10... | collective-permute-start | bytes 12296 | tf_op jit(solution)/shard_map/ppermute | solution.py:379
  18.8 3.6 %collective-permute-start.5 = (f32[4,2,128]{2,1,0:T(2,128)S(1)}, f32[4,2,128]{2,1,0:T(2,128)S(1)}, u32[]{:S(2)}, u32[]{:S(2)}) collective-permute-start(f32[4,2,128]{2,1,0:T(2,128)S(1)} %get-tuple-element.53), channel_id=1, source_target_pairs={{8,0},{16,8},{24,16},{0,24},{9,1},{17,9},{25,17},{1,25},{10,2},{18... | collective-permute-start | bytes 12296 | tf_op jit(solution)/shard_map/ppermute | solution.py:380
  22.4 5.2 %collective-permute-start.7 = (f32[3,12,128]{2,1,0:T(8,128)S(1)}, f32[3,12,128]{2,1,0:T(8,128)S(1)}, u32[]{:S(2)}, u32[]{:S(2)}) collective-permute-start(f32[3,12,128]{2,1,0:T(8,128)S(1)} %get-tuple-element.50), channel_id=1, source_target_pairs={{0,7},{1,2},{2,1},{3,4},{4,3},{5,6},{6,5},{7,0},{8,15},{9,10},{10,... | collective-permute-start | bytes 55304 | tf_op jit(solution)/shard_map/ppermute | solution.py:376
  24.4 3.2 %collective-permute-start.6 = (f32[3,12,128]{2,1,0:T(8,128)S(1)}, f32[3,12,128]{2,1,0:T(8,128)S(1)}, u32[]{:S(2)}, u32[]{:S(2)}) collective-permute-start(f32[3,12,128]{2,1,0:T(8,128)S(1)} %get-tuple-element.51), channel_id=1, source_target_pairs={{0,1},{1,0},{2,3},{3,2},{4,5},{5,4},{6,7},{7,6},{8,9},{9,8},{10,11... | collective-permute-start | bytes 55304 | tf_op jit(solution)/shard_map/ppermute | solution.py:377
  24.6 8.0 %collective-permute-start.8 = (f32[4,10240]{1,0:T(4,128)S(1)}, f32[4,10240]{1,0:T(4,128)S(1)}, u32[]{:S(2)}, u32[]{:S(2)}) collective-permute-start(f32[4,10240]{1,0:T(4,128)S(1)} %get-tuple-element.30), channel_id=1, source_target_pairs={{0,8},{8,16},{16,24},{24,0},{1,9},{9,17},{17,25},{25,1},{2,10},{10... | collective-permute-start | bytes 491528 | tf_op jit(solution)/shard_map/ppermute | solution.py:379
  26.2 8.6 %collective-permute-start.9 = (f32[4,10240]{1,0:T(4,128)S(1)}, f32[4,10240]{1,0:T(4,128)S(1)}, u32[]{:S(2)}, u32[]{:S(2)}) collective-permute-start(f32[4,10240]{1,0:T(4,128)S(1)} %get-tuple-element.31), channel_id=1, source_target_pairs={{8,0},{16,8},{24,16},{0,24},{9,1},{17,9},{25,17},{1,25},{10,2},{18... | collective-permute-start | bytes 491528 | tf_op jit(solution)/shard_map/ppermute | solution.py:380
  36.3 5.1 %collective-permute-start.11 = (f32[3,10,128]{2,1,0:T(8,128)S(1)}, f32[3,10,128]{2,1,0:T(8,128)S(1)}, u32[]{:S(2)}, u32[]{:S(2)}) collective-permute-start(f32[3,10,128]{2,1,0:T(8,128)S(1)} %get-tuple-element.48), channel_id=1, source_target_pairs={{0,7},{1,2},{2,1},{3,4},{4,3},{5,6},{6,5},{7,0},{8,15},{9,10},{10,... | collective-permute-start | bytes 46088 | tf_op jit(solution)/shard_map/ppermute | solution.py:376
  36.6 4.8 %collective-permute-start.10 = (f32[3,10,128]{2,1,0:T(8,128)S(1)}, f32[3,10,128]{2,1,0:T(8,128)S(1)}, u32[]{:S(2)}, u32[]{:S(2)}) collective-permute-start(f32[3,10,128]{2,1,0:T(8,128)S(1)} %get-tuple-element.49), channel_id=1, source_target_pairs={{0,1},{1,0},{2,3},{3,2},{4,5},{5,4},{6,7},{7,6},{8,9},{9,8},{10,11... | collective-permute-start | bytes 46088 | tf_op jit(solution)/shard_map/ppermute | solution.py:377

commit v4 on v3

--- a/solution.py
+++ b/solution.py
@@ -20,6 +20,7 @@
 PAD = 8
 FINE_HALO = 6
 VMEM_SPEC = pl.BlockSpec(memory_space=pltpu.VMEM)
+SMALL = pltpu.CompilerParams(vmem_limit_bytes=8 << 20)
 
 
 def in_vmem(value):
@@ -33,6 +34,7 @@
         in_specs=[VMEM_SPEC] * len(operands),
         out_specs=jax.tree.map(lambda _: VMEM_SPEC, outs),
         scratch_shapes=list(scratch),
+        compiler_params=SMALL,
     )(*[in_vmem(operand) for operand in operands])
 
 
@@ -324,8 +326,23 @@
     return body
 
 
-def final_kernel(entries):
-    def body(dots_ref, y0_ref, y1_ref, y2_ref, ens_ref, widths_ref, scales_ref, coef_ref, vector_ref):
+def spread_kernel(cells):
+    def body(y0_ref, y1_ref, y2_ref, ens_ref, widths_ref, scales_ref, spread_ref):
+        distances = pair_distances()
+        low_half = lax.broadcasted_iota(jnp.int32, (cells, CH), 1) < LEV
+        coarse = (y0_ref[...], y1_ref[...], y2_ref[...])
+        for pair in range(PAIRS):
+            matrix = hat(widths_ref, pair, distances)
+            first, second = members((ens_ref,), pair)
+            summed = [field_sum(first, second, part, low_half) for part in coarse]
+            out = product(jnp.concatenate(summed, axis=0), matrix) * scales_ref[pair : pair + 1, :]
+            spread_ref[:, pair * CH : (pair + 1) * CH] = out
+
+    return body
+
+
+def final_kernel(entries, cells):
+    def body(dots_ref, spread_ref, coef_ref, vector_ref):
         sums = jnp.sum(dots_ref[...], axis=0, keepdims=True)
         lane = lax.broadcasted_iota(jnp.int32, (1, CH), 1)
 
@@ -354,15 +371,10 @@
         coef_ref[...] = jnp.where(
             row == 0, jnp.where(col == 0, alpha0, alpha1), jnp.where(col == 0, beta0, beta1)
         )
-        coarse = k0 * y0_ref[...] + k1 * y1_ref[...] + k2 * y2_ref[...]
-        distances = pair_distances()
-        low_half = lax.broadcasted_iota(jnp.int32, coarse.shape, 1) < LEV
         for pair in range(PAIRS):
-            matrix = hat(widths_ref, pair, distances)
-            first, second = members((ens_ref,), pair)
-            summed = field_sum(first, second, coarse, low_half)
-            out = product(summed, matrix) * scales_ref[pair : pair + 1, :]
-            vector_ref[:, pair * CH : (pair + 1) * CH] = out.astype(BF16)
+            lanes = slice(pair * CH, (pair + 1) * CH)
+            out = k0 * spread_ref[0:cells, lanes] + k1 * spread_ref[cells : 2 * cells, lanes]
+            vector_ref[:, lanes] = (out + k2 * spread_ref[2 * cells :, lanes]).astype(BF16)
 
     return body
 
@@ -415,7 +427,9 @@
 
     ens = ensemble.reshape(cells, M * CH)
     edge_rows = pltpu.VMEM((cols, M * CH), F32)
-    ens_up, ens_down = kernel_call(edges_kernel(cols, rows), (edge_rows, edge_rows), (ens, stencil))
+    ens_up, ens_down = kernel_call(
+        edges_kernel(cols, rows), (edge_rows, edge_rows), (ens, own_stencil)
+    )
     ens_low, ens_high = from_neighbours(ens_up, ens_down, "lat", False)
 
     cell_block = pltpu.VMEM((cells, CH), F32)
@@ -444,10 +458,14 @@
         middle_scratch,
     )
     shared = lax.all_to_all(dots.reshape(devices, 1, CH), ("lat", "lon"), 0, 0).reshape(devices, CH)
+    spreads = kernel_call(
+        spread_kernel(cells), pltpu.VMEM((3 * cells, M * LEV), F32),
+        (y0, y1, y2, ens, widths, scales),
+    )
     coefficients, vector = kernel_call(
-        final_kernel(entries),
+        final_kernel(entries, cells),
         (jax.ShapeDtypeStruct((2, 2), F32), jax.ShapeDtypeStruct((cells, M * LEV), BF16)),
-        (shared, y0, y1, y2, ens, widths, scales),
+        (shared, spreads),
     )
     return coefficients, vector.reshape(cols, rows, M * LEV)
 

time: 53.1 us -> 53.5 us (level)
  blocking collectives: 9.78 us -> 0 us
  waiting for transfers between devices: 20.4 us -> 26.5 us
  starting transfers between devices: 16.1 us -> 18.9 us
  Pallas kernels: 5.61 us -> 6.89 us
    all_to_all x1 -> x0, blocking collectives: 9.78 us -> none  [per_device(): lax.all_to_all(dots.reshape(devices, 1, CH), ('lat', 'lon'), 0, 0)]
    all_to_all x0 -> x1, waiting for transfers between devices: none -> 6.06 us  [per_device(): lax.all_to_all(dots.reshape(devices, 1, CH), ('lat', 'lon'), 0, 0)]
    all_to_all x0 -> x1, starting transfers between devices: none -> 2.81 us  [per_device(): lax.all_to_all(dots.reshape(devices, 1, CH), ('lat', 'lon'), 0, 0)]
    pallas_call x6 -> x7, Pallas kernels: 4.62 us -> 5.84 us  [kernel_call(): pl.pallas_call(body, out_shape=outs, in_specs=[VMEM_SPEC] * len(operands)...]
  transfers between devices with their start and end apart: 12 -> 13, of which waited for: 8 -> 9; matrix products, arithmetic and copies ran while one was open for 0% -> 0% of each run, Pallas kernels for 0% -> 2%
where the time goes in v4:
time: 53.5 us; the launch traced here: 53.3 us
  waiting for transfers between devices  26.5 us (50%)
  starting transfers between devices  18.9 us (35%)
  Pallas kernels  6.89 us (13%)
  between operations  0.75 us (1%)
    ppermute x3, waiting for transfers between devices, from_neighbours(): lax.ppermute(up, axis, [(at, (at + 1) % count) for at in range(count)])  8.63 us
    ppermute x3, waiting for transfers between devices, from_neighbours(): far = lax.ppermute(jnp.where(odd, up, down), axis, outer)  7.14 us
    ppermute x3, starting transfers between devices, from_neighbours(): lax.ppermute(up, axis, [(at, (at + 1) % count) for at in range(count)])  6.83 us
    all_to_all x1, waiting for transfers between devices, per_device(): lax.all_to_all(dots.reshape(devices, 1, CH), ('lat', 'lon'), 0, 0)  6.06 us
    ppermute x3, starting transfers between devices, from_neighbours(): far = lax.ppermute(jnp.where(odd, up, down), axis, outer)  6.02 us
    pallas_call x7, Pallas kernels, kernel_call(): pl.pallas_call(body, out_shape=outs, in_specs=[VMEM_SPEC] * len(operands)...  5.84 us
    ppermute x3, waiting for transfers between devices, from_neighbours(): lax.ppermute(down, axis, [((at + 1) % count, at) for at in range(count)])  4.64 us
    ppermute x3, starting transfers between devices, from_neighbours(): lax.ppermute(down, axis, [((at + 1) % count, at) for at in range(count)])  3.16 us
  transfers between devices with their start and end apart: 13, of which 9 were waited for; matrix products, arithmetic and copies ran while one was open for 0% of the time, Pallas kernels for 2%

profile of v4, /device:TPU:0, one launch (start us, length us, event | category | flops | bytes accessed | tf_op | source)
XLA Modules:
  0.0 53.3 jit_solution(6455099835910550130)
XLA Ops:
  0.6 0.0 copy-start
  0.6 1.1 %shard_map.77 = (f32[108,128]{1,0:T(8,128)S(1)}, f32[108,128]{1,0:T(8,128)S(1)}, f32[8,32,128]{2,1,0:T(8,128)S(1)}, f32[32,128]{1,0:T(8,128)S(1)}, f32[40,128]{1,0:T(8,128)S(1)}, /*index=5*/f32[40,128]{1,0:T(8,128)S(1)}) custom-call(f32[8,16,128]{2,1,0:T(8,128)} %weight_ref.1, f32[8,16,128]{2,1,0:T(8,128)} %innovation_ref.1, f32[1,16]{1,0:T(1,128)} %bitcast.19, ...), custom_call_target="tpu_custom_call" | custom-call | tf_op jit(solution)/shard_map/pallas_call | solution.py:410
  1.7 3.0 %collective-permute-start = (f32[108,128]{1,0:T(8,128)S(1)}, f32[108,128]{1,0:T(8,128)S(1)}, u32[]{:S(2)}, u32[]{:S(2)}) collective-permute-start(f32[108,128]{1,0:T(8,128)S(1)} %get-tuple-element.21), channel_id=1, source_target_pairs={{0,8},{8,16},{16,24},{24,0},{1,9},{9,17},{17,25},{25,1},{2,10},{10... | collective-permute-start | bytes 165896 | tf_op jit(solution)/shard_map/ppermute | solution.py:391
  4.7 1.0 %collective-permute-start.1 = (f32[108,128]{1,0:T(8,128)S(1)}, f32[108,128]{1,0:T(8,128)S(1)}, u32[]{:S(2)}, u32[]{:S(2)}) collective-permute-start(f32[108,128]{1,0:T(8,128)S(1)} %get-tuple-element.22), channel_id=1, source_target_pairs={{8,0},{16,8},{24,16},{0,24},{9,1},{17,9},{25,17},{1,25},{10,2},{18... | collective-permute-start | bytes 165896 | tf_op jit(solution)/shard_map/ppermute | solution.py:392
  5.7 0.1 add_convert_fusion
  5.8 2.0 %collective-permute-done.low_ref = f32[108,128]{1,0:T(8,128)S(1)} collective-permute-done((f32[108,128]{1,0:T(8,128)S(1)}, f32[108,128]{1,0:T(8,128)S(1)}, u32[]{:S(2)}, u32[]{:S(2)}) %collective-permute-start) | collective-permute-done | bytes 55328 | tf_op jit(solution)/shard_map/ppermute | solution.py:391
  7.8 1.2 %collective-permute-done.1.high_ref = f32[108,128]{1,0:T(8,128)S(1)} collective-permute-done((f32[108,128]{1,0:T(8,128)S(1)}, f32[108,128]{1,0:T(8,128)S(1)}, u32[]{:S(2)}, u32[]{:S(2)}) %collective-permute-start.1) | collective-permute-done | bytes 55328 | tf_op jit(solution)/shard_map/ppermute | solution.py:392
  9.1 0.1 broadcast_in_dim.18.flags_ref
  9.2 0.1 collective-permute-start.2
  9.3 3.7 %collective-permute-start.3 = (f32[3,56,128]{2,1,0:T(8,128)S(1)}, f32[3,56,128]{2,1,0:T(8,128)S(1)}, u32[]{:S(2)}, u32[]{:S(2)}) collective-permute-start(f32[3,56,128]{2,1,0:T(8,128)S(1)} %get-tuple-element.41), channel_id=1, source_target_pairs={{0,7},{1,2},{2,1},{3,4},{4,3},{5,6},{6,5},{7,0},{8,15},{9,10},{10,... | collective-permute-start | bytes 258056 | tf_op jit(solution)/shard_map/ppermute | solution.py:388
  13.0 0.0 collective-permute-done.2
  13.0 2.3 %collective-permute-done.3 = f32[3,56,128]{2,1,0:T(8,128)S(1)} collective-permute-done((f32[3,56,128]{2,1,0:T(8,128)S(1)}, f32[3,56,128]{2,1,0:T(8,128)S(1)}, u32[]{:S(2)}, u32[]{:S(2)}) %collective-permute-start.3) | collective-permute-done | bytes 86048 | tf_op jit(solution)/shard_map/ppermute | solution.py:388
  15.4 0.0 copy-done
  15.4 1.2 %shard_map.79 = (f32[32,128]{1,0:T(8,128)S(1)}, f32[32,128]{1,0:T(8,128)S(1)}) custom-call(f32[14,56,128]{2,1,0:T(8,128)S(1)} %pad_maximum_fusion.weight_ref, f32[56,128]{1,0:T(8,128)S(1)} %get-tuple-element.26.stencil_ref, bf16[32,10240]{1,0:T(8,128)(2,1)S(1)} %bitcast.12, f32[40,128]{1,0:T(8,128)S(1)} %get-tuple-element.27.widths_ref, ...), custom_call_target="tpu_custom_call" | custom-call | tf_op jit(solution)/shard_map/pallas_call | solution.py:31
  16.6 2.3 %collective-permute-start.4 = (f32[4,2,128]{2,1,0:T(2,128)S(1)}, f32[4,2,128]{2,1,0:T(2,128)S(1)}, u32[]{:S(2)}, u32[]{:S(2)}) collective-permute-start(f32[4,2,128]{2,1,0:T(2,128)S(1)} %get-tuple-element.52), channel_id=1, source_target_pairs={{0,8},{8,16},{16,24},{24,0},{1,9},{9,17},{17,25},{25,1},{2,10},{10... | collective-permute-start | bytes 12296 | tf_op jit(solution)/shard_map/ppermute | solution.py:391
  18.9 0.7 %collective-permute-start.5 = (f32[4,2,128]{2,1,0:T(2,128)S(1)}, f32[4,2,128]{2,1,0:T(2,128)S(1)}, u32[]{:S(2)}, u32[]{:S(2)}) collective-permute-start(f32[4,2,128]{2,1,0:T(2,128)S(1)} %get-tuple-element.53), channel_id=1, source_target_pairs={{8,0},{16,8},{24,16},{0,24},{9,1},{17,9},{25,17},{1,25},{10,2},{18... | collective-permute-start | bytes 12296 | tf_op jit(solution)/shard_map/ppermute | solution.py:392
  19.6 1.6 %collective-permute-done.4 = f32[4,2,128]{2,1,0:T(2,128)S(1)} collective-permute-done((f32[4,2,128]{2,1,0:T(2,128)S(1)}, f32[4,2,128]{2,1,0:T(2,128)S(1)}, u32[]{:S(2)}, u32[]{:S(2)}) %collective-permute-start.4) | collective-permute-done | bytes 4128 | tf_op jit(solution)/shard_map/ppermute | solution.py:391
  21.1 1.3 %collective-permute-done.5 = f32[4,2,128]{2,1,0:T(2,128)S(1)} collective-permute-done((f32[4,2,128]{2,1,0:T(2,128)S(1)}, f32[4,2,128]{2,1,0:T(2,128)S(1)}, u32[]{:S(2)}, u32[]{:S(2)}) %collective-permute-start.5) | collective-permute-done | bytes 4128 | tf_op jit(solution)/shard_map/ppermute | solution.py:392
  22.5 2.0 %collective-permute-start.7 = (f32[3,12,128]{2,1,0:T(8,128)S(1)}, f32[3,12,128]{2,1,0:T(8,128)S(1)}, u32[]{:S(2)}, u32[]{:S(2)}) collective-permute-start(f32[3,12,128]{2,1,0:T(8,128)S(1)} %get-tuple-element.50), channel_id=1, source_target_pairs={{0,7},{1,2},{2,1},{3,4},{4,3},{5,6},{6,5},{7,0},{8,15},{9,10},{10,... | collective-permute-start | bytes 55304 | tf_op jit(solution)/shard_map/ppermute | solution.py:388
  24.5 0.0 collective-permute-start.6
  24.5 0.2 shard_map.80
  24.7 1.5 %collective-permute-start.8 = (f32[4,10240]{1,0:T(4,128)S(1)}, f32[4,10240]{1,0:T(4,128)S(1)}, u32[]{:S(2)}, u32[]{:S(2)}) collective-permute-start(f32[4,10240]{1,0:T(4,128)S(1)} %get-tuple-element.30), channel_id=1, source_target_pairs={{0,8},{8,16},{16,24},{24,0},{1,9},{9,17},{17,25},{25,1},{2,10},{10... | collective-permute-start | bytes 491528 | tf_op jit(solution)/shard_map/ppermute | solution.py:391
  26.3 1.4 %collective-permute-start.9 = (f32[4,10240]{1,0:T(4,128)S(1)}, f32[4,10240]{1,0:T(4,128)S(1)}, u32[]{:S(2)}, u32[]{:S(2)}) collective-permute-start(f32[4,10240]{1,0:T(4,128)S(1)} %get-tuple-element.31), channel_id=1, source_target_pairs={{8,0},{16,8},{24,16},{0,24},{9,1},{17,9},{25,17},{1,25},{10,2},{18... | collective-permute-start | bytes 491528 | tf_op jit(solution)/shard_map/ppermute | solution.py:392
  27.7 0.0 collective-permute-done.7
  27.7 0.0 collective-permute-done.6
  27.7 5.0 %collective-permute-done.8.ens_low_ref = f32[4,10240]{1,0:T(4,128)S(1)} collective-permute-done((f32[4,10240]{1,0:T(4,128)S(1)}, f32[4,10240]{1,0:T(4,128)S(1)}, u32[]{:S(2)}, u32[]{:S(2)}) %collective-permute-start.8) | collective-permute-done | bytes 163872 | tf_op jit(solution)/shard_map/ppermute | solution.py:391
  32.7 2.1 %collective-permute-done.9.ens_high_ref = f32[4,10240]{1,0:T(4,128)S(1)} collective-permute-done((f32[4,10240]{1,0:T(4,128)S(1)}, f32[4,10240]{1,0:T(4,128)S(1)}, u32[]{:S(2)}, u32[]{:S(2)}) %collective-permute-start.9) | collective-permute-done | bytes 163872 | tf_op jit(solution)/shard_map/ppermute | solution.py:392
  34.8 1.5 %shard_map.81 = (f32[32,128]{1,0:T(8,128)S(1)}, f32[32,128]{1,0:T(8,128)S(1)}, f32[4,10,128]{2,1,0:T(8,128)S(1)}) custom-call(f32[4,12,128]{2,1,0:T(8,128)S(1)} %pad_maximum_fusion.1.mid_ref, f32[3,12,128]{2,1,0:T(8,128)S(1)} %get-tuple-element.47.left_ref, f32[3,12,128]{2,1,0:T(8,128)S(1)} %get-tuple-element.46.right_ref, ...), custom_call_target="tpu_custom_call" | custom-call | tf_op jit(solution)/shard_map/pallas_call | solution.py:31
  36.4 0.3 collective-permute-start.11
  36.7 0.0 collective-permute-start.10
  36.7 4.8 %collective-permute-done.11 = f32[3,10,128]{2,1,0:T(8,128)S(1)} collective-permute-done((f32[3,10,128]{2,1,0:T(8,128)S(1)}, f32[3,10,128]{2,1,0:T(8,128)S(1)}, u32[]{:S(2)}, u32[]{:S(2)}) %collective-permute-start.11) | collective-permute-done | bytes 15392 | tf_op jit(solution)/shard_map/ppermute | solution.py:388
  41.5 0.0 collective-permute-done.10
  41.5 0.9 %shard_map.82 = (f32[32,128]{1,0:T(8,128)S(1)}, f32[32,128]{1,0:T(8,128)}) custom-call(f32[4,10,128]{2,1,0:T(8,128)S(1)} %get-tuple-element.32.mid_ref, f32[3,10,128]{2,1,0:T(8,128)S(1)} %get-tuple-element.45.left_ref, f32[3,10,128]{2,1,0:T(8,128)S(1)} %get-tuple-element.44.right_ref, f32[14,56,128]{2,1,0:T(8,128)S(1)} %pad_maximum_fusion.weight_ref, ...), custom_call_target="tpu_custom_call" | custom-call | tf_op jit(solution)/shard_map/pallas_call | solution.py:31
  42.4 2.8 %all-to-all-start = ((f32[32,1,128]{2,1,0:T(1,128)}), f32[32,1,128]{2,1,0:T(1,128)S(1)}, u32[]{:S(2)}, u32[]{:S(2)}) async-start(f32[32,1,128]{2,1,0:T(1,128)} %bitcast.8), calls=%async_computation | async-start | bytes 32768 | tf_op jit(solution)/shard_map/all_to_all | solution.py:460
  45.2 1.0 %shard_map.83.spread_ref = f32[96,5120]{1,0:T(8,128)S(1)} custom-call(f32[32,128]{1,0:T(8,128)S(1)} %get-tuple-element.33.y0_ref, f32[32,128]{1,0:T(8,128)S(1)} %get-tuple-element.34.y1_ref, f32[32,128]{1,0:T(8,128)S(1)} %get-tuple-element.37.y2_ref, bf16[32,10240]{1,0:T(8,128)(2,1)S(1)} %bitcast.15, f32[40,128]{1,0:T(8,128)S(1)} %get-tuple-element.27.widths_ref, ...), custom_call_target="tpu_custom_call" | custom-call | tf_op jit(solution)/shard_map/pallas_call | solution.py:31
  46.2 6.1 %all-to-all-done = f32[32,1,128]{2,1,0:T(1,128)S(1)} async-done(((f32[32,1,128]{2,1,0:T(1,128)}), f32[32,1,128]{2,1,0:T(1,128)S(1)}, u32[]{:S(2)}, u32[]{:S(2)}) %all-to-all-start) | async-done | bytes 16416 | tf_op jit(solution)/shard_map/all_to_all | solution.py:460
  52.3 1.0 %shard_map.84 = (f32[2,2]{1,0:T(2,128)}, bf16[32,5120]{1,0:T(8,128)(2,1)}) custom-call(f32[32,128]{1,0:T(8,128)S(1)} %bitcast.18, f32[96,5120]{1,0:T(8,128)S(1)} %shard_map.83.spread_ref), custom_call_target="tpu_custom_call" | custom-call | tf_op jit(solution)/shard_map/pallas_call | solution.py:31
  (10 shorter events, 0.1 us)
Async XLA Ops:
  0.6 14.8 %copy-start = (bf16[4,8,10240]{2,1,0:T(8,128)(2,1)S(1)}, bf16[4,8,10240]{2,1,0:T(8,128)(2,1)}, u32[]{:S(2)}) copy-start(bf16[4,8,10240]{2,1,0:T(8,128)(2,1)} %param.6) | copy-start | bytes 1966084
  1.7 6.1 %collective-permute-start = (f32[108,128]{1,0:T(8,128)S(1)}, f32[108,128]{1,0:T(8,128)S(1)}, u32[]{:S(2)}, u32[]{:S(2)}) collective-permute-start(f32[108,128]{1,0:T(8,128)S(1)} %get-tuple-element.21), channel_id=1, source_target_pairs={{0,8},{8,16},{16,24},{24,0},{1,9},{9,17},{17,25},{25,1},{2,10},{10... | collective-permute-start | bytes 165896 | tf_op jit(solution)/shard_map/ppermute | solution.py:391
  4.7 4.4 %collective-permute-start.1 = (f32[108,128]{1,0:T(8,128)S(1)}, f32[108,128]{1,0:T(8,128)S(1)}, u32[]{:S(2)}, u32[]{:S(2)}) collective-permute-start(f32[108,128]{1,0:T(8,128)S(1)} %get-tuple-element.22), channel_id=1, source_target_pairs={{8,0},{16,8},{24,16},{0,24},{9,1},{17,9},{25,17},{1,25},{10,2},{18... | collective-permute-start | bytes 165896 | tf_op jit(solution)/shard_map/ppermute | solution.py:392
  9.2 3.8 %collective-permute-start.2 = (f32[3,56,128]{2,1,0:T(8,128)S(1)}, f32[3,56,128]{2,1,0:T(8,128)S(1)}, u32[]{:S(2)}, u32[]{:S(2)}) collective-permute-start(f32[3,56,128]{2,1,0:T(8,128)S(1)} %get-tuple-element.40), channel_id=1, source_target_pairs={{0,1},{1,0},{2,3},{3,2},{4,5},{5,4},{6,7},{7,6},{8,9},{9,8},{10,11... | collective-permute-start | bytes 258056 | tf_op jit(solution)/shard_map/ppermute | solution.py:389
  9.3 6.0 %collective-permute-start.3 = (f32[3,56,128]{2,1,0:T(8,128)S(1)}, f32[3,56,128]{2,1,0:T(8,128)S(1)}, u32[]{:S(2)}, u32[]{:S(2)}) collective-permute-start(f32[3,56,128]{2,1,0:T(8,128)S(1)} %get-tuple-element.41), channel_id=1, source_target_pairs={{0,7},{1,2},{2,1},{3,4},{4,3},{5,6},{6,5},{7,0},{8,15},{9,10},{10,... | collective-permute-start | bytes 258056 | tf_op jit(solution)/shard_map/ppermute | solution.py:388
  16.6 4.6 %collective-permute-start.4 = (f32[4,2,128]{2,1,0:T(2,128)S(1)}, f32[4,2,128]{2,1,0:T(2,128)S(1)}, u32[]{:S(2)}, u32[]{:S(2)}) collective-permute-start(f32[4,2,128]{2,1,0:T(2,128)S(1)} %get-tuple-element.52), channel_id=1, source_target_pairs={{0,8},{8,16},{16,24},{24,0},{1,9},{9,17},{17,25},{25,1},{2,10},{10... | collective-permute-start | bytes 12296 | tf_op jit(solution)/shard_map/ppermute | solution.py:391
  18.9 3.6 %collective-permute-start.5 = (f32[4,2,128]{2,1,0:T(2,128)S(1)}, f32[4,2,128]{2,1,0:T(2,128)S(1)}, u32[]{:S(2)}, u32[]{:S(2)}) collective-permute-start(f32[4,2,128]{2,1,0:T(2,128)S(1)} %get-tuple-element.53), channel_id=1, source_target_pairs={{8,0},{16,8},{24,16},{0,24},{9,1},{17,9},{25,17},{1,25},{10,2},{18... | collective-permute-start | bytes 12296 | tf_op jit(solution)/shard_map/ppermute | solution.py:392
  22.5 5.2 %collective-permute-start.7 = (f32[3,12,128]{2,1,0:T(8,128)S(1)}, f32[3,12,128]{2,1,0:T(8,128)S(1)}, u32[]{:S(2)}, u32[]{:S(2)}) collective-permute-start(f32[3,12,128]{2,1,0:T(8,128)S(1)} %get-tuple-element.50), channel_id=1, source_target_pairs={{0,7},{1,2},{2,1},{3,4},{4,3},{5,6},{6,5},{7,0},{8,15},{9,10},{10,... | collective-permute-start | bytes 55304 | tf_op jit(solution)/shard_map/ppermute | solution.py:388
  24.5 3.2 %collective-permute-start.6 = (f32[3,12,128]{2,1,0:T(8,128)S(1)}, f32[3,12,128]{2,1,0:T(8,128)S(1)}, u32[]{:S(2)}, u32[]{:S(2)}) collective-permute-start(f32[3,12,128]{2,1,0:T(8,128)S(1)} %get-tuple-element.51), channel_id=1, source_target_pairs={{0,1},{1,0},{2,3},{3,2},{4,5},{5,4},{6,7},{7,6},{8,9},{9,8},{10,11... | collective-permute-start | bytes 55304 | tf_op jit(solution)/shard_map/ppermute | solution.py:389
  24.7 8.0 %collective-permute-start.8 = (f32[4,10240]{1,0:T(4,128)S(1)}, f32[4,10240]{1,0:T(4,128)S(1)}, u32[]{:S(2)}, u32[]{:S(2)}) collective-permute-start(f32[4,10240]{1,0:T(4,128)S(1)} %get-tuple-element.30), channel_id=1, source_target_pairs={{0,8},{8,16},{16,24},{24,0},{1,9},{9,17},{17,25},{25,1},{2,10},{10... | collective-permute-start | bytes 491528 | tf_op jit(solution)/shard_map/ppermute | solution.py:391
  26.3 8.6 %collective-permute-start.9 = (f32[4,10240]{1,0:T(4,128)S(1)}, f32[4,10240]{1,0:T(4,128)S(1)}, u32[]{:S(2)}, u32[]{:S(2)}) collective-permute-start(f32[4,10240]{1,0:T(4,128)S(1)} %get-tuple-element.31), channel_id=1, source_target_pairs={{8,0},{16,8},{24,16},{0,24},{9,1},{17,9},{25,17},{1,25},{10,2},{18... | collective-permute-start | bytes 491528 | tf_op jit(solution)/shard_map/ppermute | solution.py:392
  36.4 5.1 %collective-permute-start.11 = (f32[3,10,128]{2,1,0:T(8,128)S(1)}, f32[3,10,128]{2,1,0:T(8,128)S(1)}, u32[]{:S(2)}, u32[]{:S(2)}) collective-permute-start(f32[3,10,128]{2,1,0:T(8,128)S(1)} %get-tuple-element.48), channel_id=1, source_target_pairs={{0,7},{1,2},{2,1},{3,4},{4,3},{5,6},{6,5},{7,0},{8,15},{9,10},{10,... | collective-permute-start | bytes 46088 | tf_op jit(solution)/shard_map/ppermute | solution.py:388
  36.7 4.8 %collective-permute-start.10 = (f32[3,10,128]{2,1,0:T(8,128)S(1)}, f32[3,10,128]{2,1,0:T(8,128)S(1)}, u32[]{:S(2)}, u32[]{:S(2)}) collective-permute-start(f32[3,10,128]{2,1,0:T(8,128)S(1)} %get-tuple-element.49), channel_id=1, source_target_pairs={{0,1},{1,0},{2,3},{3,2},{4,5},{5,4},{6,7},{7,6},{8,9},{9,8},{10,11... | collective-permute-start | bytes 46088 | tf_op jit(solution)/shard_map/ppermute | solution.py:389
  42.4 9.9 %all-to-all-start = ((f32[32,1,128]{2,1,0:T(1,128)}), f32[32,1,128]{2,1,0:T(1,128)S(1)}, u32[]{:S(2)}, u32[]{:S(2)}) async-start(f32[32,1,128]{2,1,0:T(1,128)} %bitcast.8), calls=%async_computation | async-start | bytes 32768 | tf_op jit(solution)/shard_map/all_to_all | solution.py:460

commit v5 on v3

--- a/solution.py
+++ b/solution.py
@@ -12,6 +12,7 @@
 EVEN_TAPS = (-0.0234375, 0.2265625, 0.8671875, -0.0703125)
 ODD_TAPS = (-0.0703125, 0.8671875, 0.2265625, -0.0234375)
 EPSILON = 1e-06
+
 
 F32 = jnp.float32
 BF16 = jnp.bfloat16
@@ -95,22 +96,14 @@
     return total
 
 
-def prepare_kernel():
+def prepare_kernel(cols, rows):
     depth = FINE_HALO
+    fine_cols, fine_rows = 2 * cols, 2 * rows
+    spans = rows + 4
 
     def body(weight_ref, innovation_ref, lat_weight_ref, lat_offset_ref, band_ref,
-             up_ref, down_ref, own_ref, own_stencil_ref, widths_ref, scales_ref):
-        fine_cols, fine_rows = weight_ref.shape[0], weight_ref.shape[1]
-        for col in range(fine_cols):
-            weight = weight_ref[col]
-            weighted = weight * innovation_ref[col]
-            own_ref[col, 0:fine_rows, :] = weight
-            own_ref[col, fine_rows : 2 * fine_rows, :] = weighted
-            at = 2 * depth * col
-            up_ref[at : at + depth, :] = weight[fine_rows - depth :]
-            up_ref[at + depth : at + 2 * depth, :] = weighted[fine_rows - depth :]
-            down_ref[at : at + depth, :] = weight[:depth]
-            down_ref[at + depth : at + 2 * depth, :] = weighted[:depth]
+             up_ref, down_ref, part_ref, wide_up_ref, wide_down_ref, own_ref, own_stencil_ref,
+             widths_ref, scales_ref, spill_ref, sum_ref):
         row = lax.broadcasted_iota(jnp.int32, (fine_rows, fine_rows), 0)
         col = lax.broadcasted_iota(jnp.int32, (fine_rows, fine_rows), 1)
 
@@ -119,15 +112,50 @@
             values = jnp.sum(jnp.where(row == col, spread, 0.0), axis=1, keepdims=True)
             return jnp.broadcast_to(values, (fine_rows, CH))
 
-        weight = column(lat_weight_ref[...])
+        upper = column(lat_weight_ref[...])
         offset = column(lat_offset_ref[...].astype(F32))
-        own_stencil_ref[0:fine_rows, :] = weight
+        weighted = []
+        for at in range(fine_cols):
+            weight = weight_ref[at]
+            own_ref[at] = weight
+            wide_up_ref[depth * at : depth * (at + 1), :] = weight[fine_rows - depth :]
+            wide_down_ref[depth * at : depth * (at + 1), :] = weight[:depth]
+            weighted.append(weight * innovation_ref[at])
+        coefs = stencil_coefficients(upper, offset)
+        blank = jnp.zeros((8, CH), F32)
+        for at in range(cols + 4):
+            folded = None
+            for tap in range(4):
+                for taps, centre in ((EVEN_TAPS, at - tap), (ODD_TAPS, at - 1 - tap)):
+                    if 0 <= centre < cols:
+                        term = taps[tap] * weighted[2 * centre + (taps is ODD_TAPS)]
+                        folded = term if folded is None else folded + term
+            total = None
+            for step in range(5):
+                slot = at * 5 + step
+                spill_ref[slot, 0:8, :] = blank
+                spill_ref[slot, 8 + fine_rows : 16 + fine_rows, :] = blank
+                spill_ref[slot, 8 : 8 + fine_rows, :] = coefs[step] * folded
+                term = spill_ref[slot, 8 - 2 * step : 8 - 2 * step + 2 * spans, :]
+                total = term if total is None else total + term
+            sum_ref[at] = total
+            down_ref[2 * at : 2 * at + 2, :] = (
+                sum_ref[at, pl.ds(0, 2, stride=2), :] + sum_ref[at, pl.ds(1, 2, stride=2), :]
+            )
+            part_ref[at] = (
+                sum_ref[at, pl.ds(4, rows, stride=2), :] + sum_ref[at, pl.ds(5, rows, stride=2), :]
+            )
+            end = 2 * rows + 4
+            up_ref[2 * at : 2 * at + 2, :] = (
+                sum_ref[at, pl.ds(end, 2, stride=2), :] + sum_ref[at, pl.ds(end + 1, 2, stride=2), :]
+            )
+        own_stencil_ref[0:fine_rows, :] = upper
         own_stencil_ref[fine_rows : 2 * fine_rows, :] = offset
-        at = 2 * depth * fine_cols
-        up_ref[at : at + depth, :] = weight[fine_rows - depth :]
-        up_ref[at + depth : at + 2 * depth, :] = offset[fine_rows - depth :]
-        down_ref[at : at + depth, :] = weight[:depth]
-        down_ref[at + depth : at + 2 * depth, :] = offset[:depth]
+        at = depth * fine_cols
+        wide_up_ref[at : at + depth, :] = upper[fine_rows - depth :]
+        wide_up_ref[at + depth : at + 2 * depth, :] = offset[fine_rows - depth :]
+        wide_down_ref[at : at + depth, :] = upper[:depth]
+        wide_down_ref[at + depth : at + 2 * depth, :] = offset[:depth]
         bands = jnp.broadcast_to((band_ref[...] + 1).astype(F32), (PAIRS, M))
         pair = lax.broadcasted_iota(jnp.int32, (PAIRS, M), 0)
         member = lax.broadcasted_iota(jnp.int32, (PAIRS, M), 1)
@@ -141,25 +169,39 @@
     return body
 
 
-def join_kernel():
+def gather_kernel(cols, rows):
+    def body(low_ref, high_ref, part_ref, flags_ref, left_ref, own_ref, right_ref):
+        keep_low, keep_high = flags_ref[0:1, :], flags_ref[1:2, :]
+        middle_rows = jnp.zeros((rows - 4, CH), F32)
+        for at in range(cols + 4):
+            low = low_ref[2 * at : 2 * at + 2, :] * keep_low
+            high = high_ref[2 * at : 2 * at + 2, :] * keep_high
+            block = part_ref[at] + jnp.concatenate([low, middle_rows, high], axis=0)
+            if at < 2:
+                left_ref[at * rows : (at + 1) * rows, :] = block
+            elif at < cols + 2:
+                own_ref[(at - 2) * rows : (at - 1) * rows, :] = block
+            else:
+                right_ref[(at - cols - 2) * rows : (at - cols - 1) * rows, :] = block
+
+    return body
+
+
+def join_kernel(cols, rows):
     depth = FINE_HALO
+    fine_cols, fine_rows = 2 * cols, 2 * rows
 
     def body(low_ref, high_ref, own_ref, own_stencil_ref, flags_ref, tall_ref, stencil_ref):
-        fine_cols, fine_rows = own_ref.shape[0], own_ref.shape[1] // 2
         total = fine_rows + 2 * depth
         keep_low, keep_high = flags_ref[0:1, :], flags_ref[1:2, :]
+        for col in range(fine_cols):
+            edge = slice(depth * col, depth * (col + 1))
+            tall_ref[col, 0:depth, :] = low_ref[edge, :] * keep_low
+            tall_ref[col, depth : depth + fine_rows, :] = own_ref[col]
+            tall_ref[col, depth + fine_rows : total, :] = high_ref[edge, :] * keep_high
         for part in range(2):
             base = part * total
-            for col in range(fine_cols):
-                at = 2 * depth * col + part * depth
-                tall_ref[col, base : base + depth, :] = low_ref[at : at + depth, :] * keep_low
-                tall_ref[col, base + depth : base + depth + fine_rows, :] = own_ref[
-                    col, part * fine_rows : (part + 1) * fine_rows, :
-                ]
-                tall_ref[col, base + depth + fine_rows : base + total, :] = (
-                    high_ref[at : at + depth, :] * keep_high
-                )
-            at = 2 * depth * fine_cols + part * depth
+            at = depth * (fine_cols + part)
             stencil_ref[base : base + depth, :] = low_ref[at : at + depth, :]
             stencil_ref[base + depth : base + depth + fine_rows, :] = own_stencil_ref[
                 part * fine_rows : (part + 1) * fine_rows, :
@@ -192,8 +234,12 @@
 def lat_coefficients(stencil_ref, rows, halo):
     first, count = fine_span(rows, halo)
     total = 2 * rows + 2 * FINE_HALO
-    weight = stencil_ref[first : first + count, :]
-    offset = stencil_ref[total + first : total + first + count, :]
+    return stencil_coefficients(
+        stencil_ref[first : first + count, :], stencil_ref[total + first : total + first + count, :]
+    )
+
+
+def stencil_coefficients(weight, offset):
     result = []
     for step in range(5):
         lower = jnp.where(offset == float(step), 1.0 - weight, 0.0)
@@ -257,16 +303,11 @@
 
 
 def start_kernel(cols, rows):
-    first, count = fine_span(rows, 0)
-    base = 2 * rows + 2 * FINE_HALO + first
-
-    def body(weight_ref, stencil_ref, ens_ref, widths_ref, scales_ref, coarse_ref, image_ref, spill_ref, sum_ref):
-        coefs = lat_coefficients(stencil_ref, rows, 0)
-        even = [weight_ref[2 * at + 1, base : base + count, :] for at in range(cols + 3)]
-        odd = [weight_ref[2 * at, base : base + count, :] for at in range(cols + 3)]
-        coarse = restrict_block(even, odd, coefs, spill_ref, sum_ref, cols, rows, 0)
-        coarse_ref[...] = coarse
-        image_ref[...] = gram((ens_ref,), widths_ref, scales_ref, coarse)
+    def body(own_ref, left_ref, right_ref, ens_ref, widths_ref, scales_ref, coarse_ref, image_ref):
+        coarse_ref[...] = own_ref[...]
+        coarse_ref[0 : 2 * rows, :] += left_ref[...]
+        coarse_ref[(cols - 2) * rows : cols * rows, :] += right_ref[...]
+        image_ref[...] = gram((ens_ref,), widths_ref, scales_ref, coarse_ref[...])
 
     return body
 
@@ -393,32 +434,45 @@
     keeps = jnp.stack([position > 0, position < lat_count - 1]).astype(F32)
     flags = jnp.broadcast_to(keeps[:, None], (2, CH))
 
-    edge_block = pltpu.VMEM(((fine_cols + 1) * 2 * FINE_HALO, CH), F32)
+    cell_block = pltpu.VMEM((cells, CH), F32)
     pair_block = pltpu.VMEM((PAIRS, CH), F32)
-    up, down, own, own_stencil, widths, scales = pl.pallas_call(
-        prepare_kernel(),
+    rim_block = pltpu.VMEM((2 * (cols + 4), CH), F32)
+    wide_block = pltpu.VMEM(((fine_cols + 2) * FINE_HALO, CH), F32)
+    up, down, part, wide_up, wide_down, own, own_stencil, widths, scales = pl.pallas_call(
+        prepare_kernel(cols, rows),
         out_shape=(
-            edge_block, edge_block, pltpu.VMEM((fine_cols, 2 * fine_rows, CH), F32),
+            rim_block, rim_block, pltpu.VMEM((cols + 4, rows, CH), F32), wide_block, wide_block,
+            pltpu.VMEM((fine_cols, fine_rows, CH), F32),
             pltpu.VMEM((2 * fine_rows, CH), F32), pair_block, pair_block,
         ),
         in_specs=[VMEM_SPEC] * 5,
-        out_specs=(VMEM_SPEC,) * 6,
+        out_specs=(VMEM_SPEC,) * 9,
+        scratch_shapes=[
+            pltpu.VMEM(((cols + 4) * 5, fine_rows + 16, CH), F32),
+            pltpu.VMEM((cols + 4, fine_rows + 8, CH), F32),
+        ],
     )(obs_weight, innovation, lat_weight[None], lat_offset[None], band_widths[None])
     low, high = from_neighbours(up, down, "lat", False)
+    wide_low, wide_high = from_neighbours(wide_up, wide_down, "lat", False)
+    side_block = pltpu.VMEM((2 * rows, CH), F32)
+    to_left, own_part, to_right = kernel_call(
+        gather_kernel(cols, rows), (side_block, cell_block, side_block), (low, high, part, flags)
+    )
+    left, right = from_neighbours(to_right, to_left, "lon", True)
+    edge_rows = pltpu.VMEM((cols, M * CH), F32)
+    ens = ensemble.reshape(cells, M * CH)
+    ens_up, ens_down = kernel_call(
+        edges_kernel(cols, rows), (edge_rows, edge_rows), (ens, to_left)
+    )
+    ens_low, ens_high = from_neighbours(ens_up, ens_down, "lat", False)
     tall, stencil = kernel_call(
-        join_kernel(),
-        (pltpu.VMEM((fine_cols, 2 * total, CH), F32), pltpu.VMEM((2 * total, CH), F32)),
-        (low, high, own, own_stencil, flags),
-    )
-    left, right = from_neighbours(tall[-3:], tall[:3], "lon", True)
-    weight = jnp.concatenate([left, tall, right], axis=0)
-
-    ens = ensemble.reshape(cells, M * CH)
-    edge_rows = pltpu.VMEM((cols, M * CH), F32)
-    ens_up, ens_down = kernel_call(edges_kernel(cols, rows), (edge_rows, edge_rows), (ens, stencil))
-    ens_low, ens_high = from_neighbours(ens_up, ens_down, "lat", False)
-
-    cell_block = pltpu.VMEM((cells, CH), F32)
+        join_kernel(cols, rows),
+        (pltpu.VMEM((fine_cols, total, CH), F32), pltpu.VMEM((2 * total, CH), F32)),
+        (wide_low, wide_high, own, own_stencil, flags),
+    )
+    wide_left, wide_right = from_neighbours(tall[-3:], tall[:3], "lon", True)
+    weight = jnp.concatenate([wide_left, tall, wide_right], axis=0)
+
     restrict_scratch = (
         pltpu.VMEM((cols * 5, total, CH), F32),
         pltpu.VMEM((cols, 2 * rows + 8, CH), F32),
@@ -427,14 +481,15 @@
 
     y0, b0 = kernel_call(
         start_kernel(cols, rows), (cell_block, cell_block),
-        (weight, stencil, ens, widths, scales), restrict_scratch,
+        (own_part, left, right, ens, widths, scales),
     )
     block = b0.reshape(cols, rows, CH)
     low_rows, high_rows = from_neighbours(block[:, -2:], block[:, :2], "lat", False)
     mid = jnp.concatenate([low_rows, block, high_rows], axis=1)
+    mid_left, mid_right = from_neighbours(mid[-3:], mid[:3], "lon", True)
     y1, b1, mid1 = kernel_call(
         step_kernel(cols, rows), (cell_block, cell_block, pltpu.VMEM((cols, rows + 2, CH), F32)),
-        (mid, *from_neighbours(mid[-3:], mid[:3], "lon", True), weight, stencil, flags,
+        (mid, mid_left, mid_right, weight, stencil, flags,
          ens, ens_low, ens_high, widths, scales),
         middle_scratch + (pltpu.VMEM((2 * cols, CH), F32),),
     )

time: 53.1 us -> 52.7 us (level)
  local copies, waits for them, and re-layouts: 0.08 us -> 1.16 us
  blocking collectives: 9.78 us -> 8.86 us
  starting transfers between devices: 16.1 us -> 15.5 us
    ppermute x3 -> x4, waiting for transfers between devices: 7.14 us -> 17.8 us  [from_neighbours(): far = lax.ppermute(jnp.where(odd, up, down), axis, outer)]
    ppermute x3 -> x4, waiting for transfers between devices: 8.63 us -> 1.5 us  [from_neighbours(): lax.ppermute(up, axis, [(at, (at + 1) % count) for at in range(count)])]
    ppermute x3 -> x4, starting transfers between devices: 6.01 us -> 1.82 us  [from_neighbours(): far = lax.ppermute(jnp.where(odd, up, down), axis, outer)]
    ppermute x3 -> x4, waiting for transfers between devices: 4.64 us -> 1.07 us  [from_neighbours(): lax.ppermute(down, axis, [((at + 1) % count, at) for at in range(count)])]
    ppermute x3 -> x4, starting transfers between devices: 3.16 us -> 5.32 us  [from_neighbours(): lax.ppermute(down, axis, [((at + 1) % count, at) for at in range(count)])]
    unnamed x2 -> x4, local copies, waits for them, and re-layouts: 0.01 us -> 1.09 us
    all_to_all x1, blocking collectives: 9.78 us -> 8.86 us  [per_device(): lax.all_to_all(dots.reshape(devices, 1, CH), ('lat', 'lon'), 0, 0)]
    ppermute x3 -> x4, starting transfers between devices: 6.83 us -> 7.6 us  [from_neighbours(): lax.ppermute(up, axis, [(at, (at + 1) % count) for at in range(count)])]
  transfers between devices with their start and end apart: 12 -> 16, of which waited for: 8 -> 6; matrix products, arithmetic and copies ran while one was open for 0% -> 0% of each run, Pallas kernels for 0% -> 0%
where the time goes in v5:
time: 52.7 us; the launch traced here: 52.5 us
  waiting for transfers between devices  20.4 us (39%)
  starting transfers between devices  15.5 us (29%)
  blocking collectives  8.86 us (17%)
  Pallas kernels  5.62 us (11%)
  local copies, waits for them, and re-layouts  1.16 us (2%)
  between operations  0.81 us (2%)
    ppermute x4, waiting for transfers between devices, from_neighbours(): far = lax.ppermute(jnp.where(odd, up, down), axis, outer)  17.8 us
    all_to_all x1, blocking collectives, per_device(): lax.all_to_all(dots.reshape(devices, 1, CH), ('lat', 'lon'), 0, 0)  8.86 us
    ppermute x4, starting transfers between devices, from_neighbours(): lax.ppermute(up, axis, [(at, (at + 1) % count) for at in range(count)])  7.6 us
    ppermute x4, starting transfers between devices, from_neighbours(): lax.ppermute(down, axis, [((at + 1) % count, at) for at in range(count)])  5.32 us
    pallas_call x7, Pallas kernels, kernel_call(): pl.pallas_call(body, out_shape=outs, in_specs=[VMEM_SPEC] * len(operands)...  4.58 us
    ppermute x4, starting transfers between devices, from_neighbours(): far = lax.ppermute(jnp.where(odd, up, down), axis, outer)  1.82 us
    ppermute x4, waiting for transfers between devices, from_neighbours(): lax.ppermute(up, axis, [(at, (at + 1) % count) for at in range(count)])  1.5 us
    unnamed x4, local copies, waits for them, and re-layouts  1.09 us
  transfers between devices with their start and end apart: 16, of which 6 were waited for; matrix products, arithmetic and copies ran while one was open for 0% of the time, Pallas kernels for 0%

profile of v5, /device:TPU:0, one launch (start us, length us, event | category | flops | bytes accessed | tf_op | source)
XLA Modules:
  0.0 52.5 jit_solution(12709718135674743911)
XLA Ops:
  0.6 1.0 %shard_map.77 = (f32[16,128]{1,0:T(8,128)S(1)}, f32[16,128]{1,0:T(8,128)S(1)}, f32[8,8,128]{2,1,0:T(8,128)S(1)}, f32[60,128]{1,0:T(8,128)S(1)}, f32[60,128]{1,0:...) custom-call(f32[8,16,128]{2,1,0:T(8,128)} %weight_ref.1, ...), custom_call_target="tpu_custom_call" | custom-call | tf_op jit(solution)/shard_map/pallas_call | solution.py:441
  1.7 3.0 %collective-permute-start = (f32[16,128]{1,0:T(8,128)S(1)}, f32[16,128]{1,0:T(8,128)S(1)}, u32[]{:S(2)}, u32[]{:S(2)}) collective-permute-start(f32[16,128]{1,0:T(8,128)S(1)} %get-tuple-element.27), channel_id=1, source_target_pairs={{0,8},{8,16},{16,24},{24,0},{1,9},{9,17},{17,25},{25,1},{2,10},{10... | collective-permute-start | bytes 24584 | tf_op jit(solution)/shard_map/ppermute | solution.py:420
  4.7 1.0 %collective-permute-start.1 = (f32[16,128]{1,0:T(8,128)S(1)}, f32[16,128]{1,0:T(8,128)S(1)}, u32[]{:S(2)}, u32[]{:S(2)}) collective-permute-start(f32[16,128]{1,0:T(8,128)S(1)} %get-tuple-element.28), channel_id=1, source_target_pairs={{8,0},{16,8},{24,16},{0,24},{9,1},{17,9},{25,17},{1,25},{10,2},{18... | collective-permute-start | bytes 24584 | tf_op jit(solution)/shard_map/ppermute | solution.py:421
  5.7 0.1 add_convert_fusion
  5.8 1.5 %collective-permute-done.low_ref = f32[16,128]{1,0:T(8,128)S(1)} collective-permute-done((f32[16,128]{1,0:T(8,128)S(1)}, f32[16,128]{1,0:T(8,128)S(1)}, u32[]{:S(2)}, u32[]{:S(2)}) %collective-permute-start) | collective-permute-done | bytes 8224 | tf_op jit(solution)/shard_map/ppermute | solution.py:420
  7.3 1.1 %collective-permute-done.1.high_ref = f32[16,128]{1,0:T(8,128)S(1)} collective-permute-done((f32[16,128]{1,0:T(8,128)S(1)}, f32[16,128]{1,0:T(8,128)S(1)}, u32[]{:S(2)}, u32[]{:S(2)}) %collective-permute-start.1) | collective-permute-done | bytes 8224 | tf_op jit(solution)/shard_map/ppermute | solution.py:421
  8.3 0.1 broadcast_in_dim.18.flags_ref
  8.4 1.7 %collective-permute-start.3 = (f32[16,128]{1,0:T(8,128)S(1)}, f32[16,128]{1,0:T(8,128)S(1)}, u32[]{:S(2)}, u32[]{:S(2)}) collective-permute-start(f32[16,128]{1,0:T(8,128)S(1)} %get-tuple-element.68), channel_id=1, source_target_pairs={{0,7},{1,2},{2,1},{3,4},{4,3},{5,6},{6,5},{7,0},{8,15},{9,10},{10,... | collective-permute-start | bytes 24584 | tf_op jit(solution)/shard_map/ppermute | solution.py:417
  10.1 0.1 collective-permute-start.2
  10.2 3.2 %collective-permute-done.3 = f32[16,128]{1,0:T(8,128)S(1)} collective-permute-done((f32[16,128]{1,0:T(8,128)S(1)}, f32[16,128]{1,0:T(8,128)S(1)}, u32[]{:S(2)}, u32[]{:S(2)}) %collective-permute-start.3) | collective-permute-done | bytes 8224 | tf_op jit(solution)/shard_map/ppermute | solution.py:417
  13.4 0.0 collective-permute-done.2
  13.4 0.0 copy-start
  13.4 1.1 %copy-done = bf16[4,8,10240]{2,1,0:T(8,128)(2,1)S(1)} copy-done((bf16[4,8,10240]{2,1,0:T(8,128)(2,1)S(1)}, bf16[4,8,10240]{2,1,0:T(8,128)(2,1)}, u32[]{:S(2)}) %copy-start) | copy-done | bytes 655384
  14.5 0.0 copy-start.1
  14.5 1.1 %shard_map.79 = (f32[32,128]{1,0:T(8,128)S(1)}, f32[32,128]{1,0:T(8,128)S(1)}) custom-call(f32[32,128]{1,0:T(8,128)S(1)} %get-tuple-element.30.own_ref, f32[16,128]{1,0:T(8,128)S(1)} %get-tuple-element.67.left_ref, f32[16,128]{1,0:T(8,128)S(1)} %get-tuple-element.66.right_ref, bf16[32,10240]{1,0:T(8,128)(2,1)S(1)} %bitcast.12, ...), custom_call_target="tpu_custom_call" | custom-call | tf_op jit(solution)/shard_map/pallas_call | solution.py:31
  15.6 2.4 %collective-permute-start.4 = (f32[4,2,128]{2,1,0:T(2,128)S(1)}, f32[4,2,128]{2,1,0:T(2,128)S(1)}, u32[]{:S(2)}, u32[]{:S(2)}) collective-permute-start(f32[4,2,128]{2,1,0:T(2,128)S(1)} %get-tuple-element.64), channel_id=1, source_target_pairs={{0,8},{8,16},{16,24},{24,0},{1,9},{9,17},{17,25},{25,1},{2,10},{10... | collective-permute-start | bytes 12296 | tf_op jit(solution)/shard_map/ppermute | solution.py:420
  18.1 0.5 %collective-permute-start.5 = (f32[4,2,128]{2,1,0:T(2,128)S(1)}, f32[4,2,128]{2,1,0:T(2,128)S(1)}, u32[]{:S(2)}, u32[]{:S(2)}) collective-permute-start(f32[4,2,128]{2,1,0:T(2,128)S(1)} %get-tuple-element.65), channel_id=1, source_target_pairs={{8,0},{16,8},{24,16},{0,24},{9,1},{17,9},{25,17},{1,25},{10,2},{18... | collective-permute-start | bytes 12296 | tf_op jit(solution)/shard_map/ppermute | solution.py:421
  18.6 1.5 %collective-permute-start.8 = (f32[60,128]{1,0:T(8,128)S(1)}, f32[60,128]{1,0:T(8,128)S(1)}, u32[]{:S(2)}, u32[]{:S(2)}) collective-permute-start(f32[60,128]{1,0:T(8,128)S(1)} %get-tuple-element.36), channel_id=1, source_target_pairs={{0,8},{8,16},{16,24},{24,0},{1,9},{9,17},{17,25},{25,1},{2,10},{10... | collective-permute-start | bytes 92168 | tf_op jit(solution)/shard_map/ppermute | solution.py:420
  20.1 1.4 %collective-permute-start.9 = (f32[60,128]{1,0:T(8,128)S(1)}, f32[60,128]{1,0:T(8,128)S(1)}, u32[]{:S(2)}, u32[]{:S(2)}) collective-permute-start(f32[60,128]{1,0:T(8,128)S(1)} %get-tuple-element.37), channel_id=1, source_target_pairs={{8,0},{16,8},{24,16},{0,24},{9,1},{17,9},{25,17},{1,25},{10,2},{18... | collective-permute-start | bytes 92168 | tf_op jit(solution)/shard_map/ppermute | solution.py:421
  21.5 0.0 copy-done.1
  21.5 0.2 shard_map.81
  21.7 0.6 %collective-permute-start.12 = (f32[4,10240]{1,0:T(4,128)S(1)}, f32[4,10240]{1,0:T(4,128)S(1)}, u32[]{:S(2)}, u32[]{:S(2)}) collective-permute-start(f32[4,10240]{1,0:T(4,128)S(1)} %get-tuple-element.42), channel_id=1, source_target_pairs={{0,8},{8,16},{16,24},{24,0},{1,9},{9,17},{17,25},{25,1},{2,10},{10... | collective-permute-start | bytes 491528 | tf_op jit(solution)/shard_map/ppermute | solution.py:420
  22.4 0.0 collective-permute-done.4
  22.4 2.3 %collective-permute-start.13 = (f32[4,10240]{1,0:T(4,128)S(1)}, f32[4,10240]{1,0:T(4,128)S(1)}, u32[]{:S(2)}, u32[]{:S(2)}) collective-permute-start(f32[4,10240]{1,0:T(4,128)S(1)} %get-tuple-element.43), channel_id=1, source_target_pairs={{8,0},{16,8},{24,16},{0,24},{9,1},{17,9},{25,17},{1,25},{10,2},{18... | collective-permute-start | bytes 491528 | tf_op jit(solution)/shard_map/ppermute | solution.py:421
  24.7 0.0 collective-permute-done.5
  24.8 0.1 collective-permute-start.7
  24.8 0.0 collective-permute-done.8.low_ref
  24.8 0.1 collective-permute-start.6
  24.9 0.0 collective-permute-done.9.high_ref
  25.0 0.5 %collective-permute-start.10 = (f32[3,28,128]{2,1,0:T(8,128)S(1)}, f32[3,28,128]{2,1,0:T(8,128)S(1)}, u32[]{:S(2)}, u32[]{:S(2)}) collective-permute-start(f32[3,28,128]{2,1,0:T(8,128)S(1)} %get-tuple-element.52), channel_id=1, source_target_pairs={{0,1},{1,0},{2,3},{3,2},{4,5},{5,4},{6,7},{7,6},{8,9},{9,8},{10,11... | collective-permute-start | bytes 129032 | tf_op jit(solution)/shard_map/ppermute | solution.py:418
  25.5 4.4 %collective-permute-done.7 = f32[3,12,128]{2,1,0:T(8,128)S(1)} collective-permute-done((f32[3,12,128]{2,1,0:T(8,128)S(1)}, f32[3,12,128]{2,1,0:T(8,128)S(1)}, u32[]{:S(2)}, u32[]{:S(2)}) %collective-permute-start.7) | collective-permute-done | bytes 18464 | tf_op jit(solution)/shard_map/ppermute | solution.py:417
  29.9 0.0 collective-permute-start.11
  29.9 0.0 collective-permute-done.6
  29.9 0.0 collective-permute-done.10
  29.9 5.3 %collective-permute-done.11 = f32[3,28,128]{2,1,0:T(8,128)S(1)} collective-permute-done((f32[3,28,128]{2,1,0:T(8,128)S(1)}, f32[3,28,128]{2,1,0:T(8,128)S(1)}, u32[]{:S(2)}, u32[]{:S(2)}) %collective-permute-start.11) | collective-permute-done | bytes 43040 | tf_op jit(solution)/shard_map/ppermute | solution.py:417
  35.2 0.0 collective-permute-done.12.ens_low_ref
  35.3 0.0 collective-permute-done.13.ens_high_ref
  35.3 1.6 %shard_map.82 = (f32[32,128]{1,0:T(8,128)S(1)}, f32[32,128]{1,0:T(8,128)S(1)}, f32[4,10,128]{2,1,0:T(8,128)S(1)}) custom-call(f32[4,12,128]{2,1,0:T(8,128)S(1)} %pad_maximum_fusion.1.mid_ref, f32[3,12,128]{2,1,0:T(8,128)S(1)} %get-tuple-element.59.left_ref, f32[3,12,128]{2,1,0:T(8,128)S(1)} %get-tuple-element.58.right_ref, ...), custom_call_target="tpu_custom_call" | custom-call | tf_op jit(solution)/shard_map/pallas_call | solution.py:31
  36.8 0.1 collective-permute-start.15
  36.9 0.1 collective-permute-start.14
  37.0 5.0 %collective-permute-done.15 = f32[3,10,128]{2,1,0:T(8,128)S(1)} collective-permute-done((f32[3,10,128]{2,1,0:T(8,128)S(1)}, f32[3,10,128]{2,1,0:T(8,128)S(1)}, u32[]{:S(2)}, u32[]{:S(2)}) %collective-permute-start.15) | collective-permute-done | bytes 15392 | tf_op jit(solution)/shard_map/ppermute | solution.py:417
  42.0 0.0 collective-permute-done.14
  42.0 0.2 shard_map.83
  42.2 8.9 %all_to_all.5 = f32[32,1,128]{2,1,0:T(1,128)S(1)} all-to-all(f32[32,1,128]{2,1,0:T(1,128)S(1)} %bitcast.19), channel_id=1, replica_groups=mesh['lat'=4,'lon'=8] {'lat','lon'}, dimensions={0} | all-to-all | bytes 32768 | tf_op jit(solution)/shard_map/all_to_all | solution.py:501
  51.1 1.4 %shard_map.84 = (f32[2,2]{1,0:T(2,128)}, bf16[32,5120]{1,0:T(8,128)(2,1)}) custom-call(f32[32,128]{1,0:T(8,128)S(1)} %bitcast.18, f32[32,128]{1,0:T(8,128)S(1)} %get-tuple-element.45.y0_ref, f32[32,128]{1,0:T(8,128)S(1)} %get-tuple-element.46.y1_ref, f32[32,128]{1,0:T(8,128)S(1)} %get-tuple-element.49.y2_ref, bf16[32,10240]{1,0:T(8,128)(2,1)S(1)} %bitcast.15, ...), custom_call_target="tpu_custom_call" | custom-call | tf_op jit(solution)/shard_map/pallas_call | solution.py:31
  (13 shorter events, 0.1 us)
Async XLA Ops:
  1.7 5.6 %collective-permute-start = (f32[16,128]{1,0:T(8,128)S(1)}, f32[16,128]{1,0:T(8,128)S(1)}, u32[]{:S(2)}, u32[]{:S(2)}) collective-permute-start(f32[16,128]{1,0:T(8,128)S(1)} %get-tuple-element.27), channel_id=1, source_target_pairs={{0,8},{8,16},{16,24},{24,0},{1,9},{9,17},{17,25},{25,1},{2,10},{10... | collective-permute-start | bytes 24584 | tf_op jit(solution)/shard_map/ppermute | solution.py:420
  4.7 3.7 %collective-permute-start.1 = (f32[16,128]{1,0:T(8,128)S(1)}, f32[16,128]{1,0:T(8,128)S(1)}, u32[]{:S(2)}, u32[]{:S(2)}) collective-permute-start(f32[16,128]{1,0:T(8,128)S(1)} %get-tuple-element.28), channel_id=1, source_target_pairs={{8,0},{16,8},{24,16},{0,24},{9,1},{17,9},{25,17},{1,25},{10,2},{18... | collective-permute-start | bytes 24584 | tf_op jit(solution)/shard_map/ppermute | solution.py:421
  8.4 4.9 %collective-permute-start.3 = (f32[16,128]{1,0:T(8,128)S(1)}, f32[16,128]{1,0:T(8,128)S(1)}, u32[]{:S(2)}, u32[]{:S(2)}) collective-permute-start(f32[16,128]{1,0:T(8,128)S(1)} %get-tuple-element.68), channel_id=1, source_target_pairs={{0,7},{1,2},{2,1},{3,4},{4,3},{5,6},{6,5},{7,0},{8,15},{9,10},{10,... | collective-permute-start | bytes 24584 | tf_op jit(solution)/shard_map/ppermute | solution.py:417
  10.1 3.3 %collective-permute-start.2 = (f32[16,128]{1,0:T(8,128)S(1)}, f32[16,128]{1,0:T(8,128)S(1)}, u32[]{:S(2)}, u32[]{:S(2)}) collective-permute-start(f32[16,128]{1,0:T(8,128)S(1)} %get-tuple-element.69), channel_id=1, source_target_pairs={{0,1},{1,0},{2,3},{3,2},{4,5},{5,4},{6,7},{7,6},{8,9},{9,8},{10,11... | collective-permute-start | bytes 24584 | tf_op jit(solution)/shard_map/ppermute | solution.py:418
  13.4 1.1 %copy-start = (bf16[4,8,10240]{2,1,0:T(8,128)(2,1)S(1)}, bf16[4,8,10240]{2,1,0:T(8,128)(2,1)}, u32[]{:S(2)}) copy-start(bf16[4,8,10240]{2,1,0:T(8,128)(2,1)} %param.6) | copy-start | bytes 1966084
  14.5 7.0 %copy-start.1 = (bf16[4,8,10240]{2,1,0:T(8,128)(2,1)S(1)}, bf16[4,8,10240]{2,1,0:T(8,128)(2,1)}, u32[]{:S(2)}) copy-start(bf16[4,8,10240]{2,1,0:T(8,128)(2,1)} %param.6) | copy-start | bytes 1966084
  15.6 6.8 %collective-permute-start.4 = (f32[4,2,128]{2,1,0:T(2,128)S(1)}, f32[4,2,128]{2,1,0:T(2,128)S(1)}, u32[]{:S(2)}, u32[]{:S(2)}) collective-permute-start(f32[4,2,128]{2,1,0:T(2,128)S(1)} %get-tuple-element.64), channel_id=1, source_target_pairs={{0,8},{8,16},{16,24},{24,0},{1,9},{9,17},{17,25},{25,1},{2,10},{10... | collective-permute-start | bytes 12296 | tf_op jit(solution)/shard_map/ppermute | solution.py:420
  18.1 6.7 %collective-permute-start.5 = (f32[4,2,128]{2,1,0:T(2,128)S(1)}, f32[4,2,128]{2,1,0:T(2,128)S(1)}, u32[]{:S(2)}, u32[]{:S(2)}) collective-permute-start(f32[4,2,128]{2,1,0:T(2,128)S(1)} %get-tuple-element.65), channel_id=1, source_target_pairs={{8,0},{16,8},{24,16},{0,24},{9,1},{17,9},{25,17},{1,25},{10,2},{18... | collective-permute-start | bytes 12296 | tf_op jit(solution)/shard_map/ppermute | solution.py:421
  18.6 6.2 %collective-permute-start.8 = (f32[60,128]{1,0:T(8,128)S(1)}, f32[60,128]{1,0:T(8,128)S(1)}, u32[]{:S(2)}, u32[]{:S(2)}) collective-permute-start(f32[60,128]{1,0:T(8,128)S(1)} %get-tuple-element.36), channel_id=1, source_target_pairs={{0,8},{8,16},{16,24},{24,0},{1,9},{9,17},{17,25},{25,1},{2,10},{10... | collective-permute-start | bytes 92168 | tf_op jit(solution)/shard_map/ppermute | solution.py:420
  20.1 4.8 %collective-permute-start.9 = (f32[60,128]{1,0:T(8,128)S(1)}, f32[60,128]{1,0:T(8,128)S(1)}, u32[]{:S(2)}, u32[]{:S(2)}) collective-permute-start(f32[60,128]{1,0:T(8,128)S(1)} %get-tuple-element.37), channel_id=1, source_target_pairs={{8,0},{16,8},{24,16},{0,24},{9,1},{17,9},{25,17},{1,25},{10,2},{18... | collective-permute-start | bytes 92168 | tf_op jit(solution)/shard_map/ppermute | solution.py:421
  21.7 13.5 %collective-permute-start.12 = (f32[4,10240]{1,0:T(4,128)S(1)}, f32[4,10240]{1,0:T(4,128)S(1)}, u32[]{:S(2)}, u32[]{:S(2)}) collective-permute-start(f32[4,10240]{1,0:T(4,128)S(1)} %get-tuple-element.42), channel_id=1, source_target_pairs={{0,8},{8,16},{16,24},{24,0},{1,9},{9,17},{17,25},{25,1},{2,10},{10... | collective-permute-start | bytes 491528 | tf_op jit(solution)/shard_map/ppermute | solution.py:420
  22.4 12.9 %collective-permute-start.13 = (f32[4,10240]{1,0:T(4,128)S(1)}, f32[4,10240]{1,0:T(4,128)S(1)}, u32[]{:S(2)}, u32[]{:S(2)}) collective-permute-start(f32[4,10240]{1,0:T(4,128)S(1)} %get-tuple-element.43), channel_id=1, source_target_pairs={{8,0},{16,8},{24,16},{0,24},{9,1},{17,9},{25,17},{1,25},{10,2},{18... | collective-permute-start | bytes 491528 | tf_op jit(solution)/shard_map/ppermute | solution.py:421
  24.8 5.1 %collective-permute-start.7 = (f32[3,12,128]{2,1,0:T(8,128)S(1)}, f32[3,12,128]{2,1,0:T(8,128)S(1)}, u32[]{:S(2)}, u32[]{:S(2)}) collective-permute-start(f32[3,12,128]{2,1,0:T(8,128)S(1)} %get-tuple-element.62), channel_id=1, source_target_pairs={{0,7},{1,2},{2,1},{3,4},{4,3},{5,6},{6,5},{7,0},{8,15},{9,10},{10,... | collective-permute-start | bytes 55304 | tf_op jit(solution)/shard_map/ppermute | solution.py:417
  24.8 5.0 %collective-permute-start.6 = (f32[3,12,128]{2,1,0:T(8,128)S(1)}, f32[3,12,128]{2,1,0:T(8,128)S(1)}, u32[]{:S(2)}, u32[]{:S(2)}) collective-permute-start(f32[3,12,128]{2,1,0:T(8,128)S(1)} %get-tuple-element.63), channel_id=1, source_target_pairs={{0,1},{1,0},{2,3},{3,2},{4,5},{5,4},{6,7},{7,6},{8,9},{9,8},{10,11... | collective-permute-start | bytes 55304 | tf_op jit(solution)/shard_map/ppermute | solution.py:418
  25.0 4.9 %collective-permute-start.10 = (f32[3,28,128]{2,1,0:T(8,128)S(1)}, f32[3,28,128]{2,1,0:T(8,128)S(1)}, u32[]{:S(2)}, u32[]{:S(2)}) collective-permute-start(f32[3,28,128]{2,1,0:T(8,128)S(1)} %get-tuple-element.52), channel_id=1, source_target_pairs={{0,1},{1,0},{2,3},{3,2},{4,5},{5,4},{6,7},{7,6},{8,9},{9,8},{10,11... | collective-permute-start | bytes 129032 | tf_op jit(solution)/shard_map/ppermute | solution.py:418
  29.9 5.3 %collective-permute-start.11 = (f32[3,28,128]{2,1,0:T(8,128)S(1)}, f32[3,28,128]{2,1,0:T(8,128)S(1)}, u32[]{:S(2)}, u32[]{:S(2)}) collective-permute-start(f32[3,28,128]{2,1,0:T(8,128)S(1)} %get-tuple-element.53), channel_id=1, source_target_pairs={{0,7},{1,2},{2,1},{3,4},{4,3},{5,6},{6,5},{7,0},{8,15},{9,10},{10,... | collective-permute-start | bytes 129032 | tf_op jit(solution)/shard_map/ppermute | solution.py:417
  36.8 5.1 %collective-permute-start.15 = (f32[3,10,128]{2,1,0:T(8,128)S(1)}, f32[3,10,128]{2,1,0:T(8,128)S(1)}, u32[]{:S(2)}, u32[]{:S(2)}) collective-permute-start(f32[3,10,128]{2,1,0:T(8,128)S(1)} %get-tuple-element.60), channel_id=1, source_target_pairs={{0,7},{1,2},{2,1},{3,4},{4,3},{5,6},{6,5},{7,0},{8,15},{9,10},{10,... | collective-permute-start | bytes 46088 | tf_op jit(solution)/shard_map/ppermute | solution.py:417
  36.9 5.0 %collective-permute-start.14 = (f32[3,10,128]{2,1,0:T(8,128)S(1)}, f32[3,10,128]{2,1,0:T(8,128)S(1)}, u32[]{:S(2)}, u32[]{:S(2)}) collective-permute-start(f32[3,10,128]{2,1,0:T(8,128)S(1)} %get-tuple-element.61), channel_id=1, source_target_pairs={{0,1},{1,0},{2,3},{3,2},{4,5},{5,4},{6,7},{7,6},{8,9},{9,8},{10,11... | collective-permute-start | bytes 46088 | tf_op jit(solution)/shard_map/ppermute | solution.py:418

commit v6 on v5

--- a/solution.py
+++ b/solution.py
@@ -100,10 +100,13 @@
     depth = FINE_HALO
     fine_cols, fine_rows = 2 * cols, 2 * rows
     spans = rows + 4
-
-    def body(weight_ref, innovation_ref, lat_weight_ref, lat_offset_ref, band_ref,
-             up_ref, down_ref, part_ref, wide_up_ref, wide_down_ref, own_ref, own_stencil_ref,
-             widths_ref, scales_ref, spill_ref, sum_ref):
+    wide = 2 * (cols + 4)
+
+    def body(weight_ref, innovation_ref, lat_weight_ref, lat_offset_ref, band_ref, ens_ref,
+             up_ref, down_ref, part_ref, own_ref, own_stencil_ref, widths_ref, scales_ref, local_ref,
+             spill_ref, sum_ref, done_ref):
+        copy = pltpu.make_async_copy(ens_ref, local_ref, done_ref)
+        copy.start()
         row = lax.broadcasted_iota(jnp.int32, (fine_rows, fine_rows), 0)
         col = lax.broadcasted_iota(jnp.int32, (fine_rows, fine_rows), 1)
 
@@ -118,8 +121,8 @@
         for at in range(fine_cols):
             weight = weight_ref[at]
             own_ref[at] = weight
-            wide_up_ref[depth * at : depth * (at + 1), :] = weight[fine_rows - depth :]
-            wide_down_ref[depth * at : depth * (at + 1), :] = weight[:depth]
+            up_ref[wide + depth * at : wide + depth * (at + 1), :] = weight[fine_rows - depth :]
+            down_ref[wide + depth * at : wide + depth * (at + 1), :] = weight[:depth]
             weighted.append(weight * innovation_ref[at])
         coefs = stencil_coefficients(upper, offset)
         blank = jnp.zeros((8, CH), F32)
@@ -151,11 +154,11 @@
             )
         own_stencil_ref[0:fine_rows, :] = upper
         own_stencil_ref[fine_rows : 2 * fine_rows, :] = offset
-        at = depth * fine_cols
-        wide_up_ref[at : at + depth, :] = upper[fine_rows - depth :]
-        wide_up_ref[at + depth : at + 2 * depth, :] = offset[fine_rows - depth :]
-        wide_down_ref[at : at + depth, :] = upper[:depth]
-        wide_down_ref[at + depth : at + 2 * depth, :] = offset[:depth]
+        at = wide + depth * fine_cols
+        up_ref[at : at + depth, :] = upper[fine_rows - depth :]
+        up_ref[at + depth : at + 2 * depth, :] = offset[fine_rows - depth :]
+        down_ref[at : at + depth, :] = upper[:depth]
+        down_ref[at + depth : at + 2 * depth, :] = offset[:depth]
         bands = jnp.broadcast_to((band_ref[...] + 1).astype(F32), (PAIRS, M))
         pair = lax.broadcasted_iota(jnp.int32, (PAIRS, M), 0)
         member = lax.broadcasted_iota(jnp.int32, (PAIRS, M), 1)
@@ -165,12 +168,19 @@
         widths = jnp.where(lane < LEV, first, second)
         widths_ref[...] = widths
         scales_ref[...] = 1.0 / (widths * widths)
-
-    return body
-
-
-def gather_kernel(cols, rows):
-    def body(low_ref, high_ref, part_ref, flags_ref, left_ref, own_ref, right_ref):
+        copy.wait()
+
+    return body
+
+
+def join_kernel(cols, rows):
+    depth = FINE_HALO
+    fine_cols, fine_rows = 2 * cols, 2 * rows
+    wide = 2 * (cols + 4)
+    total = fine_rows + 2 * depth
+
+    def body(low_ref, high_ref, part_ref, own_ref, own_stencil_ref, flags_ref,
+             left_ref, right_ref, coarse_ref, tall_ref, stencil_ref):
         keep_low, keep_high = flags_ref[0:1, :], flags_ref[1:2, :]
         middle_rows = jnp.zeros((rows - 4, CH), F32)
         for at in range(cols + 4):
@@ -180,28 +190,28 @@
             if at < 2:
                 left_ref[at * rows : (at + 1) * rows, :] = block
             elif at < cols + 2:
-                own_ref[(at - 2) * rows : (at - 1) * rows, :] = block
+                coarse_ref[(at - 2) * rows : (at - 1) * rows, :] = block
             else:
                 right_ref[(at - cols - 2) * rows : (at - cols - 1) * rows, :] = block
-
-    return body
-
-
-def join_kernel(cols, rows):
-    depth = FINE_HALO
-    fine_cols, fine_rows = 2 * cols, 2 * rows
-
-    def body(low_ref, high_ref, own_ref, own_stencil_ref, flags_ref, tall_ref, stencil_ref):
-        total = fine_rows + 2 * depth
-        keep_low, keep_high = flags_ref[0:1, :], flags_ref[1:2, :]
         for col in range(fine_cols):
-            edge = slice(depth * col, depth * (col + 1))
-            tall_ref[col, 0:depth, :] = low_ref[edge, :] * keep_low
-            tall_ref[col, depth : depth + fine_rows, :] = own_ref[col]
-            tall_ref[col, depth + fine_rows : total, :] = high_ref[edge, :] * keep_high
+            edge = slice(wide + depth * col, wide + depth * (col + 1))
+            pieces = (
+                (0, low_ref[edge, :] * keep_low),
+                (depth, own_ref[col]),
+                (depth + fine_rows, high_ref[edge, :] * keep_high),
+            )
+            for first, piece in pieces:
+                last = first + piece.shape[0]
+                tall_ref[col, first:last, :] = piece
+                if col < 3:
+                    base = 2 * rows + total * col
+                    left_ref[base + first : base + last, :] = piece
+                if col >= fine_cols - 3:
+                    base = 2 * rows + total * (col - fine_cols + 3)
+                    right_ref[base + first : base + last, :] = piece
         for part in range(2):
             base = part * total
-            at = depth * (fine_cols + part)
+            at = wide + depth * (fine_cols + part)
             stencil_ref[base : base + depth, :] = low_ref[at : at + depth, :]
             stencil_ref[base + depth : base + depth + fine_rows, :] = own_stencil_ref[
                 part * fine_rows : (part + 1) * fine_rows, :
@@ -270,7 +280,17 @@
     return jnp.concatenate(blocks, axis=0)
 
 
-def middle(mid_ref, left_ref, right_ref, weight_ref, coefs, dup_ref, spill_ref, sum_ref, rows, halo, mask=None):
+def weight_column(weight_refs, at, rows, first, count):
+    west_ref, tall_ref, east_ref = weight_refs
+    fine_cols = tall_ref.shape[0]
+    if 3 <= at < fine_cols + 3:
+        return tall_ref[at - 3, first : first + count, :]
+    ref, col = (west_ref, at) if at < 3 else (east_ref, at - fine_cols - 3)
+    base = 2 * rows + tall_ref.shape[1] * col + first
+    return ref[base : base + count, :]
+
+
+def middle(mid_ref, left_ref, right_ref, weight_refs, coefs, dup_ref, spill_ref, sum_ref, rows, halo, mask=None):
     cols = mid_ref.shape[0]
     first, count = fine_span(rows, halo)
     given = rows + 2 * halo + 2
@@ -297,16 +317,16 @@
     for at in range(cols + 3):
         left = sum(EVEN_TAPS[tap] * lat[at + tap] for tap in range(4))
         right = sum(ODD_TAPS[tap] * lat[at + tap] for tap in range(4))
-        even.append(left * weight_ref[2 * at + 1, first : first + count, :])
-        odd.append(right * weight_ref[2 * at, first : first + count, :])
+        even.append(left * weight_column(weight_refs, 2 * at + 1, rows, first, count))
+        odd.append(right * weight_column(weight_refs, 2 * at, rows, first, count))
     return restrict_block(even, odd, coefs, spill_ref, sum_ref, cols, rows, halo)
 
 
 def start_kernel(cols, rows):
     def body(own_ref, left_ref, right_ref, ens_ref, widths_ref, scales_ref, coarse_ref, image_ref):
         coarse_ref[...] = own_ref[...]
-        coarse_ref[0 : 2 * rows, :] += left_ref[...]
-        coarse_ref[(cols - 2) * rows : cols * rows, :] += right_ref[...]
+        coarse_ref[0 : 2 * rows, :] += left_ref[0 : 2 * rows, :]
+        coarse_ref[(cols - 2) * rows : cols * rows, :] += right_ref[0 : 2 * rows, :]
         image_ref[...] = gram((ens_ref,), widths_ref, scales_ref, coarse_ref[...])
 
     return body
@@ -315,13 +335,13 @@
 def step_kernel(cols, rows):
     cells = cols * rows
 
-    def body(mid_ref, left_ref, right_ref, weight_ref, stencil_ref, flags_ref, ens_ref, ens_low_ref, ens_high_ref,
+    def body(mid_ref, left_ref, right_ref, west_ref, tall_ref, east_ref, stencil_ref, flags_ref, ens_ref, ens_low_ref, ens_high_ref,
              widths_ref, scales_ref, coarse_ref, image_ref, padded_ref, dup_ref, spill_ref, sum_ref, rim_ref):
         coefs = lat_coefficients(stencil_ref, rows, 1)
         row = lax.broadcasted_iota(jnp.int32, (rows + 4, CH), 0)
         inside = jnp.where(row < 2, flags_ref[0:1, :], jnp.where(row < rows + 2, 1.0, flags_ref[1:2, :]))
         coarse = middle(
-            mid_ref, left_ref, right_ref, weight_ref, coefs, dup_ref, spill_ref, sum_ref, rows, 1, inside
+            mid_ref, left_ref, right_ref, (west_ref, tall_ref, east_ref), coefs, dup_ref, spill_ref, sum_ref, rows, 1, inside
         )
         coarse_ref[...] = coarse
         end = 2 * rows + 2
@@ -346,11 +366,11 @@
 
 
 def last_kernel(rows, devices):
-    def body(mid_ref, left_ref, right_ref, weight_ref, stencil_ref, y0_ref, b0_ref, y1_ref, b1_ref,
+    def body(mid_ref, left_ref, right_ref, west_ref, tall_ref, east_ref, stencil_ref, y0_ref, b0_ref, y1_ref, b1_ref,
              coarse_ref, dots_ref, dup_ref, spill_ref, sum_ref):
         coefs = lat_coefficients(stencil_ref, rows, 0)
         coarse = middle(
-            mid_ref, left_ref, right_ref, weight_ref, coefs, dup_ref, spill_ref, sum_ref, rows, 0
+            mid_ref, left_ref, right_ref, (west_ref, tall_ref, east_ref), coefs, dup_ref, spill_ref, sum_ref, rows, 0
         )
         coarse_ref[...] = coarse
         lane = lax.broadcasted_iota(jnp.int32, (1, CH), 1)
@@ -436,42 +456,38 @@
 
     cell_block = pltpu.VMEM((cells, CH), F32)
     pair_block = pltpu.VMEM((PAIRS, CH), F32)
-    rim_block = pltpu.VMEM((2 * (cols + 4), CH), F32)
-    wide_block = pltpu.VMEM(((fine_cols + 2) * FINE_HALO, CH), F32)
-    up, down, part, wide_up, wide_down, own, own_stencil, widths, scales = pl.pallas_call(
+    message = pltpu.VMEM((2 * (cols + 4) + (fine_cols + 2) * FINE_HALO, CH), F32)
+    ens_block = pltpu.VMEM((cells, M * CH), BF16)
+    up, down, part, own, own_stencil, widths, scales, ens = pl.pallas_call(
         prepare_kernel(cols, rows),
         out_shape=(
-            rim_block, rim_block, pltpu.VMEM((cols + 4, rows, CH), F32), wide_block, wide_block,
+            message, message, pltpu.VMEM((cols + 4, rows, CH), F32),
             pltpu.VMEM((fine_cols, fine_rows, CH), F32),
-            pltpu.VMEM((2 * fine_rows, CH), F32), pair_block, pair_block,
+            pltpu.VMEM((2 * fine_rows, CH), F32), pair_block, pair_block, ens_block,
         ),
-        in_specs=[VMEM_SPEC] * 5,
-        out_specs=(VMEM_SPEC,) * 9,
+        in_specs=[VMEM_SPEC] * 5 + [pl.BlockSpec(memory_space=pltpu.HBM)],
+        out_specs=(VMEM_SPEC,) * 8,
         scratch_shapes=[
             pltpu.VMEM(((cols + 4) * 5, fine_rows + 16, CH), F32),
             pltpu.VMEM((cols + 4, fine_rows + 8, CH), F32),
+            pltpu.SemaphoreType.DMA,
         ],
-    )(obs_weight, innovation, lat_weight[None], lat_offset[None], band_widths[None])
+    )(obs_weight, innovation, lat_weight[None], lat_offset[None], band_widths[None],
+      ensemble.reshape(cells, M * CH))
     low, high = from_neighbours(up, down, "lat", False)
-    wide_low, wide_high = from_neighbours(wide_up, wide_down, "lat", False)
-    side_block = pltpu.VMEM((2 * rows, CH), F32)
-    to_left, own_part, to_right = kernel_call(
-        gather_kernel(cols, rows), (side_block, cell_block, side_block), (low, high, part, flags)
-    )
-    left, right = from_neighbours(to_right, to_left, "lon", True)
+    side_block = pltpu.VMEM((2 * rows + 3 * total, CH), F32)
+    to_left, to_right, own_part, tall, stencil = kernel_call(
+        join_kernel(cols, rows),
+        (side_block, side_block, cell_block,
+         pltpu.VMEM((fine_cols, total, CH), F32), pltpu.VMEM((2 * total, CH), F32)),
+        (low, high, part, own, own_stencil, flags),
+    )
+    west, east = from_neighbours(to_right, to_left, "lon", True)
     edge_rows = pltpu.VMEM((cols, M * CH), F32)
-    ens = ensemble.reshape(cells, M * CH)
     ens_up, ens_down = kernel_call(
         edges_kernel(cols, rows), (edge_rows, edge_rows), (ens, to_left)
     )
     ens_low, ens_high = from_neighbours(ens_up, ens_down, "lat", False)
-    tall, stencil = kernel_call(
-        join_kernel(cols, rows),
-        (pltpu.VMEM((fine_cols, total, CH), F32), pltpu.VMEM((2 * total, CH), F32)),
-        (wide_low, wide_high, own, own_stencil, flags),
-    )
-    wide_left, wide_right = from_neighbours(tall[-3:], tall[:3], "lon", True)
-    weight = jnp.concatenate([wide_left, tall, wide_right], axis=0)
 
     restrict_scratch = (
         pltpu.VMEM((cols * 5, total, CH), F32),
@@ -481,7 +497,7 @@
 
     y0, b0 = kernel_call(
         start_kernel(cols, rows), (cell_block, cell_block),
-        (own_part, left, right, ens, widths, scales),
+        (own_part, west, east, ens, widths, scales),
     )
     block = b0.reshape(cols, rows, CH)
     low_rows, high_rows = from_neighbours(block[:, -2:], block[:, :2], "lat", False)
@@ -489,13 +505,13 @@
     mid_left, mid_right = from_neighbours(mid[-3:], mid[:3], "lon", True)
     y1, b1, mid1 = kernel_call(
         step_kernel(cols, rows), (cell_block, cell_block, pltpu.VMEM((cols, rows + 2, CH), F32)),
-        (mid, mid_left, mid_right, weight, stencil, flags,
+        (mid, mid_left, mid_right, west, tall, east, stencil, flags,
          ens, ens_low, ens_high, widths, scales),
         middle_scratch + (pltpu.VMEM((2 * cols, CH), F32),),
     )
     y2, dots = kernel_call(
         last_kernel(rows, devices), (cell_block, pltpu.VMEM((devices, CH), F32)),
-        (mid1, *from_neighbours(mid1[-3:], mid1[:3], "lon", True), weight, stencil, y0, b0, y1, b1),
+        (mid1, *from_neighbours(mid1[-3:], mid1[:3], "lon", True), west, tall, east, stencil, y0, b0, y1, b1),
         middle_scratch,
     )
     shared = lax.all_to_all(dots.reshape(devices, 1, CH), ("lat", "lon"), 0, 0).reshape(devices, CH)

time: 52.7 us -> 53 us (level)
  blocking collectives: 8.86 us -> 10.7 us
  starting transfers between devices: 15.5 us -> 14 us
  local copies, waits for them, and re-layouts: 1.16 us -> 0.08 us
  Pallas kernels: 5.62 us -> 6.56 us
    ppermute x4 -> x3, waiting for transfers between devices: 17.8 us -> 8.69 us  [from_neighbours(): far = lax.ppermute(jnp.where(odd, up, down), axis, outer)]
    ppermute x4 -> x3, waiting for transfers between devices: 1.5 us -> 7 us  [from_neighbours(): lax.ppermute(up, axis, [(at, (at + 1) % count) for at in range(count)])]
    ppermute x4 -> x3, waiting for transfers between devices: 1.07 us -> 4.94 us  [from_neighbours(): lax.ppermute(down, axis, [((at + 1) % count, at) for at in range(count)])]
    ppermute x4 -> x3, starting transfers between devices: 5.32 us -> 3.1 us  [from_neighbours(): lax.ppermute(down, axis, [((at + 1) % count, at) for at in range(count)])]
    ppermute x4 -> x3, starting transfers between devices: 1.82 us -> 3.97 us  [from_neighbours(): far = lax.ppermute(jnp.where(odd, up, down), axis, outer)]
    all_to_all x1, blocking collectives: 8.86 us -> 10.7 us  [per_device(): lax.all_to_all(dots.reshape(devices, 1, CH), ('lat', 'lon'), 0, 0)]
    unnamed x4 -> x0, local copies, waits for them, and re-layouts: 1.09 us -> none
    pallas_call x1, Pallas kernels: 1.04 us -> 2 us  [per_device(): pl.pallas_call(prepare_kernel(cols, rows), out_shape=(message, message, p...]
  transfers between devices with their start and end apart: 16 -> 12, of which waited for: 6 -> 9; matrix products, arithmetic and copies ran while one was open for 0% -> 0% of each run, Pallas kernels for 0% -> 0%
where the time goes in v6:
time: 53 us; the launch traced here: 52.8 us
  waiting for transfers between devices  20.6 us (39%)
  starting transfers between devices  14 us (26%)
  blocking collectives  10.7 us (20%)
  Pallas kernels  6.56 us (12%)
  between operations  0.71 us (1%)
    all_to_all x1, blocking collectives, per_device(): lax.all_to_all(dots.reshape(devices, 1, CH), ('lat', 'lon'), 0, 0)  10.7 us
    ppermute x3, waiting for transfers between devices, from_neighbours(): far = lax.ppermute(jnp.where(odd, up, down), axis, outer)  8.69 us
    ppermute x3, waiting for transfers between devices, from_neighbours(): lax.ppermute(up, axis, [(at, (at + 1) % count) for at in range(count)])  7 us
    ppermute x3, starting transfers between devices, from_neighbours(): lax.ppermute(up, axis, [(at, (at + 1) % count) for at in range(count)])  6.89 us
    ppermute x3, waiting for transfers between devices, from_neighbours(): lax.ppermute(down, axis, [((at + 1) % count, at) for at in range(count)])  4.94 us
    pallas_call x6, Pallas kernels, kernel_call(): pl.pallas_call(body, out_shape=outs, in_specs=[VMEM_SPEC] * len(operands)...  4.56 us
    ppermute x3, starting transfers between devices, from_neighbours(): far = lax.ppermute(jnp.where(odd, up, down), axis, outer)  3.97 us
    ppermute x3, starting transfers between devices, from_neighbours(): lax.ppermute(down, axis, [((at + 1) % count, at) for at in range(count)])  3.1 us
  transfers between devices with their start and end apart: 12, of which 9 were waited for; matrix products, arithmetic and copies ran while one was open for 0% of the time, Pallas kernels for 0%

profile of v6, /device:TPU:0, one launch (start us, length us, event | category | flops | bytes accessed | tf_op | source)
XLA Modules:
  0.0 52.8 jit_solution(13078756822048821782)
XLA Ops:
  0.6 2.0 %shard_map.77 = (f32[76,128]{1,0:T(8,128)S(1)}, f32[76,128]{1,0:T(8,128)S(1)}, f32[8,8,128]{2,1,0:T(8,128)S(1)}, f32[8,16,128]{2,1,0:T(8,128)S(1)}, f32[32,128]{...) custom-call(f32[8,16,128]{2,1,0:T(8,128)} %weight_ref.1, ...), custom_call_target="tpu_custom_call" | custom-call | tf_op jit(solution)/shard_map/pallas_call | solution.py:461
  2.6 3.0 %collective-permute-start = (f32[76,128]{1,0:T(8,128)S(1)}, f32[76,128]{1,0:T(8,128)S(1)}, u32[]{:S(2)}, u32[]{:S(2)}) collective-permute-start(f32[76,128]{1,0:T(8,128)S(1)} %get-tuple-element.26), channel_id=1, source_target_pairs={{0,8},{8,16},{16,24},{24,0},{1,9},{9,17},{17,25},{25,1},{2,10},{10... | collective-permute-start | bytes 116744 | tf_op jit(solution)/shard_map/ppermute | solution.py:440
  5.7 1.0 %collective-permute-start.1 = (f32[76,128]{1,0:T(8,128)S(1)}, f32[76,128]{1,0:T(8,128)S(1)}, u32[]{:S(2)}, u32[]{:S(2)}) collective-permute-start(f32[76,128]{1,0:T(8,128)S(1)} %get-tuple-element.27), channel_id=1, source_target_pairs={{8,0},{16,8},{24,16},{0,24},{9,1},{17,9},{25,17},{1,25},{10,2},{18... | collective-permute-start | bytes 116744 | tf_op jit(solution)/shard_map/ppermute | solution.py:441
  6.7 0.1 add_convert_fusion
  6.8 1.8 %collective-permute-done.low_ref = f32[76,128]{1,0:T(8,128)S(1)} collective-permute-done((f32[76,128]{1,0:T(8,128)S(1)}, f32[76,128]{1,0:T(8,128)S(1)}, u32[]{:S(2)}, u32[]{:S(2)}) %collective-permute-start) | collective-permute-done | bytes 38944 | tf_op jit(solution)/shard_map/ppermute | solution.py:440
  8.6 1.1 %collective-permute-done.1.high_ref = f32[76,128]{1,0:T(8,128)S(1)} collective-permute-done((f32[76,128]{1,0:T(8,128)S(1)}, f32[76,128]{1,0:T(8,128)S(1)}, u32[]{:S(2)}, u32[]{:S(2)}) %collective-permute-start.1) | collective-permute-done | bytes 38944 | tf_op jit(solution)/shard_map/ppermute | solution.py:441
  9.7 0.1 broadcast_in_dim.18.flags_ref
  9.8 1.9 %collective-permute-start.3 = (f32[100,128]{1,0:T(8,128)S(1)}, f32[100,128]{1,0:T(8,128)S(1)}, u32[]{:S(2)}, u32[]{:S(2)}) collective-permute-start(f32[100,128]{1,0:T(8,128)S(1)} %get-tuple-element.52), channel_id=1, source_target_pairs={{0,7},{1,2},{2,1},{3,4},{4,3},{5,6},{6,5},{7,0},{8,15},{9,10},{10,... | collective-permute-start | bytes 153608 | tf_op jit(solution)/shard_map/ppermute | solution.py:437
  11.6 0.0 collective-permute-start.2
  11.6 3.8 %collective-permute-done.3 = f32[100,128]{1,0:T(8,128)S(1)} collective-permute-done((f32[100,128]{1,0:T(8,128)S(1)}, f32[100,128]{1,0:T(8,128)S(1)}, u32[]{:S(2)}, u32[]{:S(2)}) %collective-permute-start.3) | collective-permute-done | bytes 51232 | tf_op jit(solution)/shard_map/ppermute | solution.py:437
  15.4 0.0 collective-permute-done.2
  15.4 1.1 %shard_map.79 = (f32[32,128]{1,0:T(8,128)S(1)}, f32[32,128]{1,0:T(8,128)S(1)}) custom-call(f32[32,128]{1,0:T(8,128)S(1)} %get-tuple-element.31.own_ref, f32[100,128]{1,0:T(8,128)S(1)} %get-tuple-element.51.left_ref.west_ref, f32[100,128]{1,0:T(8,128)S(1)} %get-tuple-element.50.right_ref.east_ref, bf16[32,10240]{1,0:T(8,128)(2,1)S(1)} %get-tuple-element.34.ens_ref, ...), custom_call_target="tpu_custom_call" | custom-call | tf_op jit(solution)/shard_map/pallas_call | solution.py:31
  16.6 2.4 %collective-permute-start.4 = (f32[4,2,128]{2,1,0:T(2,128)S(1)}, f32[4,2,128]{2,1,0:T(2,128)S(1)}, u32[]{:S(2)}, u32[]{:S(2)}) collective-permute-start(f32[4,2,128]{2,1,0:T(2,128)S(1)} %get-tuple-element.62), channel_id=1, source_target_pairs={{0,8},{8,16},{16,24},{24,0},{1,9},{9,17},{17,25},{25,1},{2,10},{10... | collective-permute-start | bytes 12296 | tf_op jit(solution)/shard_map/ppermute | solution.py:440
  19.0 0.5 %collective-permute-start.5 = (f32[4,2,128]{2,1,0:T(2,128)S(1)}, f32[4,2,128]{2,1,0:T(2,128)S(1)}, u32[]{:S(2)}, u32[]{:S(2)}) collective-permute-start(f32[4,2,128]{2,1,0:T(2,128)S(1)} %get-tuple-element.63), channel_id=1, source_target_pairs={{8,0},{16,8},{24,16},{0,24},{9,1},{17,9},{25,17},{1,25},{10,2},{18... | collective-permute-start | bytes 12296 | tf_op jit(solution)/shard_map/ppermute | solution.py:441
  19.5 1.6 %collective-permute-done.4 = f32[4,2,128]{2,1,0:T(2,128)S(1)} collective-permute-done((f32[4,2,128]{2,1,0:T(2,128)S(1)}, f32[4,2,128]{2,1,0:T(2,128)S(1)}, u32[]{:S(2)}, u32[]{:S(2)}) %collective-permute-start.4) | collective-permute-done | bytes 4128 | tf_op jit(solution)/shard_map/ppermute | solution.py:440
  21.1 1.5 %collective-permute-done.5 = f32[4,2,128]{2,1,0:T(2,128)S(1)} collective-permute-done((f32[4,2,128]{2,1,0:T(2,128)S(1)}, f32[4,2,128]{2,1,0:T(2,128)S(1)}, u32[]{:S(2)}, u32[]{:S(2)}) %collective-permute-start.5) | collective-permute-done | bytes 4128 | tf_op jit(solution)/shard_map/ppermute | solution.py:441
  22.6 0.5 collective-permute-start.7
  23.1 0.0 collective-permute-start.6
  23.1 0.2 shard_map.80
  23.3 1.4 %collective-permute-start.8 = (f32[4,10240]{1,0:T(4,128)S(1)}, f32[4,10240]{1,0:T(4,128)S(1)}, u32[]{:S(2)}, u32[]{:S(2)}) collective-permute-start(f32[4,10240]{1,0:T(4,128)S(1)} %get-tuple-element.40), channel_id=1, source_target_pairs={{0,8},{8,16},{16,24},{24,0},{1,9},{9,17},{17,25},{25,1},{2,10},{10... | collective-permute-start | bytes 491528 | tf_op jit(solution)/shard_map/ppermute | solution.py:440
  24.7 1.5 %collective-permute-start.9 = (f32[4,10240]{1,0:T(4,128)S(1)}, f32[4,10240]{1,0:T(4,128)S(1)}, u32[]{:S(2)}, u32[]{:S(2)}) collective-permute-start(f32[4,10240]{1,0:T(4,128)S(1)} %get-tuple-element.41), channel_id=1, source_target_pairs={{8,0},{16,8},{24,16},{0,24},{9,1},{17,9},{25,17},{1,25},{10,2},{18... | collective-permute-start | bytes 491528 | tf_op jit(solution)/shard_map/ppermute | solution.py:441
  26.3 1.5 %collective-permute-done.7 = f32[3,12,128]{2,1,0:T(8,128)S(1)} collective-permute-done((f32[3,12,128]{2,1,0:T(8,128)S(1)}, f32[3,12,128]{2,1,0:T(8,128)S(1)}, u32[]{:S(2)}, u32[]{:S(2)}) %collective-permute-start.7) | collective-permute-done | bytes 18464 | tf_op jit(solution)/shard_map/ppermute | solution.py:437
  27.8 0.0 collective-permute-done.6
  27.8 3.6 %collective-permute-done.8.ens_low_ref = f32[4,10240]{1,0:T(4,128)S(1)} collective-permute-done((f32[4,10240]{1,0:T(4,128)S(1)}, f32[4,10240]{1,0:T(4,128)S(1)}, u32[]{:S(2)}, u32[]{:S(2)}) %collective-permute-start.8) | collective-permute-done | bytes 163872 | tf_op jit(solution)/shard_map/ppermute | solution.py:440
  31.3 2.4 %collective-permute-done.9.ens_high_ref = f32[4,10240]{1,0:T(4,128)S(1)} collective-permute-done((f32[4,10240]{1,0:T(4,128)S(1)}, f32[4,10240]{1,0:T(4,128)S(1)}, u32[]{:S(2)}, u32[]{:S(2)}) %collective-permute-start.9) | collective-permute-done | bytes 163872 | tf_op jit(solution)/shard_map/ppermute | solution.py:441
  33.7 1.5 %shard_map.81 = (f32[32,128]{1,0:T(8,128)S(1)}, f32[32,128]{1,0:T(8,128)S(1)}, f32[4,10,128]{2,1,0:T(8,128)S(1)}) custom-call(f32[4,12,128]{2,1,0:T(8,128)S(1)} %pad_maximum_fusion.mid_ref, f32[3,12,128]{2,1,0:T(8,128)S(1)} %get-tuple-element.57.left_ref, f32[3,12,128]{2,1,0:T(8,128)S(1)} %get-tuple-element.56.right_ref, ...), custom_call_target="tpu_custom_call" | custom-call | tf_op jit(solution)/shard_map/pallas_call | solution.py:31
  35.3 1.6 %collective-permute-start.11 = (f32[3,10,128]{2,1,0:T(8,128)S(1)}, f32[3,10,128]{2,1,0:T(8,128)S(1)}, u32[]{:S(2)}, u32[]{:S(2)}) collective-permute-start(f32[3,10,128]{2,1,0:T(8,128)S(1)} %get-tuple-element.58), channel_id=1, source_target_pairs={{0,7},{1,2},{2,1},{3,4},{4,3},{5,6},{6,5},{7,0},{8,15},{9,10},{10,... | collective-permute-start | bytes 46088 | tf_op jit(solution)/shard_map/ppermute | solution.py:437
  36.9 0.0 collective-permute-start.10
  36.9 3.5 %collective-permute-done.11 = f32[3,10,128]{2,1,0:T(8,128)S(1)} collective-permute-done((f32[3,10,128]{2,1,0:T(8,128)S(1)}, f32[3,10,128]{2,1,0:T(8,128)S(1)}, u32[]{:S(2)}, u32[]{:S(2)}) %collective-permute-start.11) | collective-permute-done | bytes 15392 | tf_op jit(solution)/shard_map/ppermute | solution.py:437
  40.4 0.0 collective-permute-done.10
  40.4 0.2 shard_map.82
  40.7 10.7 %all_to_all.5 = f32[32,1,128]{2,1,0:T(1,128)S(1)} all-to-all(f32[32,1,128]{2,1,0:T(1,128)S(1)} %bitcast.15), channel_id=1, replica_groups=mesh['lat'=4,'lon'=8] {'lat','lon'}, dimensions={0} | all-to-all | bytes 32768 | tf_op jit(solution)/shard_map/all_to_all | solution.py:517
  51.4 1.4 %shard_map.83 = (f32[2,2]{1,0:T(2,128)}, bf16[32,5120]{1,0:T(8,128)(2,1)}) custom-call(f32[32,128]{1,0:T(8,128)S(1)} %bitcast.14, f32[32,128]{1,0:T(8,128)S(1)} %get-tuple-element.43.y0_ref, f32[32,128]{1,0:T(8,128)S(1)} %get-tuple-element.44.y1_ref, f32[32,128]{1,0:T(8,128)S(1)} %get-tuple-element.47.y2_ref, ...), custom_call_target="tpu_custom_call" | custom-call | tf_op jit(solution)/shard_map/pallas_call | solution.py:31
  (9 shorter events, 0.1 us)
Async XLA Ops:
  2.6 6.0 %collective-permute-start = (f32[76,128]{1,0:T(8,128)S(1)}, f32[76,128]{1,0:T(8,128)S(1)}, u32[]{:S(2)}, u32[]{:S(2)}) collective-permute-start(f32[76,128]{1,0:T(8,128)S(1)} %get-tuple-element.26), channel_id=1, source_target_pairs={{0,8},{8,16},{16,24},{24,0},{1,9},{9,17},{17,25},{25,1},{2,10},{10... | collective-permute-start | bytes 116744 | tf_op jit(solution)/shard_map/ppermute | solution.py:440
  5.7 4.0 %collective-permute-start.1 = (f32[76,128]{1,0:T(8,128)S(1)}, f32[76,128]{1,0:T(8,128)S(1)}, u32[]{:S(2)}, u32[]{:S(2)}) collective-permute-start(f32[76,128]{1,0:T(8,128)S(1)} %get-tuple-element.27), channel_id=1, source_target_pairs={{8,0},{16,8},{24,16},{0,24},{9,1},{17,9},{25,17},{1,25},{10,2},{18... | collective-permute-start | bytes 116744 | tf_op jit(solution)/shard_map/ppermute | solution.py:441
  9.8 5.6 %collective-permute-start.3 = (f32[100,128]{1,0:T(8,128)S(1)}, f32[100,128]{1,0:T(8,128)S(1)}, u32[]{:S(2)}, u32[]{:S(2)}) collective-permute-start(f32[100,128]{1,0:T(8,128)S(1)} %get-tuple-element.52), channel_id=1, source_target_pairs={{0,7},{1,2},{2,1},{3,4},{4,3},{5,6},{6,5},{7,0},{8,15},{9,10},{10,... | collective-permute-start | bytes 153608 | tf_op jit(solution)/shard_map/ppermute | solution.py:437
  11.6 3.8 %collective-permute-start.2 = (f32[100,128]{1,0:T(8,128)S(1)}, f32[100,128]{1,0:T(8,128)S(1)}, u32[]{:S(2)}, u32[]{:S(2)}) collective-permute-start(f32[100,128]{1,0:T(8,128)S(1)} %get-tuple-element.53), channel_id=1, source_target_pairs={{0,1},{1,0},{2,3},{3,2},{4,5},{5,4},{6,7},{7,6},{8,9},{9,8},{10,11... | collective-permute-start | bytes 153608 | tf_op jit(solution)/shard_map/ppermute | solution.py:438
  16.6 4.6 %collective-permute-start.4 = (f32[4,2,128]{2,1,0:T(2,128)S(1)}, f32[4,2,128]{2,1,0:T(2,128)S(1)}, u32[]{:S(2)}, u32[]{:S(2)}) collective-permute-start(f32[4,2,128]{2,1,0:T(2,128)S(1)} %get-tuple-element.62), channel_id=1, source_target_pairs={{0,8},{8,16},{16,24},{24,0},{1,9},{9,17},{17,25},{25,1},{2,10},{10... | collective-permute-start | bytes 12296 | tf_op jit(solution)/shard_map/ppermute | solution.py:440
  19.0 3.6 %collective-permute-start.5 = (f32[4,2,128]{2,1,0:T(2,128)S(1)}, f32[4,2,128]{2,1,0:T(2,128)S(1)}, u32[]{:S(2)}, u32[]{:S(2)}) collective-permute-start(f32[4,2,128]{2,1,0:T(2,128)S(1)} %get-tuple-element.63), channel_id=1, source_target_pairs={{8,0},{16,8},{24,16},{0,24},{9,1},{17,9},{25,17},{1,25},{10,2},{18... | collective-permute-start | bytes 12296 | tf_op jit(solution)/shard_map/ppermute | solution.py:441
  22.6 5.1 %collective-permute-start.7 = (f32[3,12,128]{2,1,0:T(8,128)S(1)}, f32[3,12,128]{2,1,0:T(8,128)S(1)}, u32[]{:S(2)}, u32[]{:S(2)}) collective-permute-start(f32[3,12,128]{2,1,0:T(8,128)S(1)} %get-tuple-element.60), channel_id=1, source_target_pairs={{0,7},{1,2},{2,1},{3,4},{4,3},{5,6},{6,5},{7,0},{8,15},{9,10},{10,... | collective-permute-start | bytes 55304 | tf_op jit(solution)/shard_map/ppermute | solution.py:437
  23.1 4.7 %collective-permute-start.6 = (f32[3,12,128]{2,1,0:T(8,128)S(1)}, f32[3,12,128]{2,1,0:T(8,128)S(1)}, u32[]{:S(2)}, u32[]{:S(2)}) collective-permute-start(f32[3,12,128]{2,1,0:T(8,128)S(1)} %get-tuple-element.61), channel_id=1, source_target_pairs={{0,1},{1,0},{2,3},{3,2},{4,5},{5,4},{6,7},{7,6},{8,9},{9,8},{10,11... | collective-permute-start | bytes 55304 | tf_op jit(solution)/shard_map/ppermute | solution.py:438
  23.3 8.0 %collective-permute-start.8 = (f32[4,10240]{1,0:T(4,128)S(1)}, f32[4,10240]{1,0:T(4,128)S(1)}, u32[]{:S(2)}, u32[]{:S(2)}) collective-permute-start(f32[4,10240]{1,0:T(4,128)S(1)} %get-tuple-element.40), channel_id=1, source_target_pairs={{0,8},{8,16},{16,24},{24,0},{1,9},{9,17},{17,25},{25,1},{2,10},{10... | collective-permute-start | bytes 491528 | tf_op jit(solution)/shard_map/ppermute | solution.py:440
  24.7 9.0 %collective-permute-start.9 = (f32[4,10240]{1,0:T(4,128)S(1)}, f32[4,10240]{1,0:T(4,128)S(1)}, u32[]{:S(2)}, u32[]{:S(2)}) collective-permute-start(f32[4,10240]{1,0:T(4,128)S(1)} %get-tuple-element.41), channel_id=1, source_target_pairs={{8,0},{16,8},{24,16},{0,24},{9,1},{17,9},{25,17},{1,25},{10,2},{18... | collective-permute-start | bytes 491528 | tf_op jit(solution)/shard_map/ppermute | solution.py:441
  35.3 5.1 %collective-permute-start.11 = (f32[3,10,128]{2,1,0:T(8,128)S(1)}, f32[3,10,128]{2,1,0:T(8,128)S(1)}, u32[]{:S(2)}, u32[]{:S(2)}) collective-permute-start(f32[3,10,128]{2,1,0:T(8,128)S(1)} %get-tuple-element.58), channel_id=1, source_target_pairs={{0,7},{1,2},{2,1},{3,4},{4,3},{5,6},{6,5},{7,0},{8,15},{9,10},{10,... | collective-permute-start | bytes 46088 | tf_op jit(solution)/shard_map/ppermute | solution.py:437
  36.9 3.5 %collective-permute-start.10 = (f32[3,10,128]{2,1,0:T(8,128)S(1)}, f32[3,10,128]{2,1,0:T(8,128)S(1)}, u32[]{:S(2)}, u32[]{:S(2)}) collective-permute-start(f32[3,10,128]{2,1,0:T(8,128)S(1)} %get-tuple-element.59), channel_id=1, source_target_pairs={{0,1},{1,0},{2,3},{3,2},{4,5},{5,4},{6,7},{7,6},{8,9},{9,8},{10,11... | collective-permute-start | bytes 46088 | tf_op jit(solution)/shard_map/ppermute | solution.py:438

commit v7 on v6

--- a/solution.py
+++ b/solution.py
@@ -78,17 +78,30 @@
     return jnp.where(low_half, left, right) + swap_halves(jnp.where(low_half, right, left))
 
 
-def gram(ens_refs, widths_ref, scales_ref, coarse):
+def gram(ens_refs, widths_ref, scales_ref, coarse, once_ref, twice_ref):
     distances = pair_distances()
+    cells = coarse.shape[0]
     low_half = lax.broadcasted_iota(jnp.int32, coarse.shape, 1) < LEV
+
+    def put(ref, pair, value):
+        ref[pair, 0:cells, :], ref[pair, cells : 2 * cells, :] = split(value)
+
+    def apply(ref, pair):
+        matrix = hat(widths_ref, pair, distances)
+        both = jnp.dot(ref[pair], matrix, preferred_element_type=F32)
+        return both[:cells] + both[cells:]
+
+    for pair in range(PAIRS):
+        first, second = members(ens_refs, pair)
+        put(once_ref, pair, field_sum(first, second, coarse, low_half))
+    for pair in range(PAIRS):
+        put(twice_ref, pair, apply(once_ref, pair))
     total = jnp.zeros(coarse.shape, F32)
     for pair in range(PAIRS):
-        matrix = hat(widths_ref, pair, distances)
+        scale = scales_ref[pair : pair + 1, :]
+        twice = apply(twice_ref, pair) * (scale * scale)
+        swapped = swap_halves(twice)
         first, second = members(ens_refs, pair)
-        summed = field_sum(first, second, coarse, low_half)
-        scale = scales_ref[pair : pair + 1, :]
-        twice = product(product(summed, matrix), matrix) * (scale * scale)
-        swapped = swap_halves(twice)
         total = total + (
             first * jnp.where(low_half, twice, swapped)
             + second * jnp.where(low_half, swapped, twice)
@@ -102,11 +115,9 @@
     spans = rows + 4
     wide = 2 * (cols + 4)
 
-    def body(weight_ref, innovation_ref, lat_weight_ref, lat_offset_ref, band_ref, ens_ref,
-             up_ref, down_ref, part_ref, own_ref, own_stencil_ref, widths_ref, scales_ref, local_ref,
-             spill_ref, sum_ref, done_ref):
-        copy = pltpu.make_async_copy(ens_ref, local_ref, done_ref)
-        copy.start()
+    def body(weight_ref, innovation_ref, lat_weight_ref, lat_offset_ref, band_ref,
+             up_ref, down_ref, part_ref, own_ref, own_stencil_ref, widths_ref, scales_ref,
+             spill_ref, sum_ref):
         row = lax.broadcasted_iota(jnp.int32, (fine_rows, fine_rows), 0)
         col = lax.broadcasted_iota(jnp.int32, (fine_rows, fine_rows), 1)
 
@@ -168,7 +179,6 @@
         widths = jnp.where(lane < LEV, first, second)
         widths_ref[...] = widths
         scales_ref[...] = 1.0 / (widths * widths)
-        copy.wait()
 
     return body
 
@@ -180,7 +190,7 @@
     total = fine_rows + 2 * depth
 
     def body(low_ref, high_ref, part_ref, own_ref, own_stencil_ref, flags_ref,
-             left_ref, right_ref, coarse_ref, tall_ref, stencil_ref):
+             left_ref, right_ref, coarse_ref, west_ref, east_ref, tall_ref, stencil_ref):
         keep_low, keep_high = flags_ref[0:1, :], flags_ref[1:2, :]
         middle_rows = jnp.zeros((rows - 4, CH), F32)
         for at in range(cols + 4):
@@ -204,11 +214,9 @@
                 last = first + piece.shape[0]
                 tall_ref[col, first:last, :] = piece
                 if col < 3:
-                    base = 2 * rows + total * col
-                    left_ref[base + first : base + last, :] = piece
+                    west_ref[col, first:last, :] = piece
                 if col >= fine_cols - 3:
-                    base = 2 * rows + total * (col - fine_cols + 3)
-                    right_ref[base + first : base + last, :] = piece
+                    east_ref[col - fine_cols + 3, first:last, :] = piece
         for part in range(2):
             base = part * total
             at = wide + depth * (fine_cols + part)
@@ -280,14 +288,13 @@
     return jnp.concatenate(blocks, axis=0)
 
 
-def weight_column(weight_refs, at, rows, first, count):
+def weight_column(weight_refs, at, first, count):
     west_ref, tall_ref, east_ref = weight_refs
     fine_cols = tall_ref.shape[0]
     if 3 <= at < fine_cols + 3:
         return tall_ref[at - 3, first : first + count, :]
     ref, col = (west_ref, at) if at < 3 else (east_ref, at - fine_cols - 3)
-    base = 2 * rows + tall_ref.shape[1] * col + first
-    return ref[base : base + count, :]
+    return ref[col, first : first + count, :]
 
 
 def middle(mid_ref, left_ref, right_ref, weight_refs, coefs, dup_ref, spill_ref, sum_ref, rows, halo, mask=None):
@@ -317,17 +324,19 @@
     for at in range(cols + 3):
         left = sum(EVEN_TAPS[tap] * lat[at + tap] for tap in range(4))
         right = sum(ODD_TAPS[tap] * lat[at + tap] for tap in range(4))
-        even.append(left * weight_column(weight_refs, 2 * at + 1, rows, first, count))
-        odd.append(right * weight_column(weight_refs, 2 * at, rows, first, count))
+        even.append(left * weight_column(weight_refs, 2 * at + 1, first, count))
+        odd.append(right * weight_column(weight_refs, 2 * at, first, count))
     return restrict_block(even, odd, coefs, spill_ref, sum_ref, cols, rows, halo)
 
 
 def start_kernel(cols, rows):
-    def body(own_ref, left_ref, right_ref, ens_ref, widths_ref, scales_ref, coarse_ref, image_ref):
+    def body(own_ref, left_ref, right_ref, ens_ref, widths_ref, scales_ref, coarse_ref, image_ref, once_ref, twice_ref):
         coarse_ref[...] = own_ref[...]
-        coarse_ref[0 : 2 * rows, :] += left_ref[0 : 2 * rows, :]
-        coarse_ref[(cols - 2) * rows : cols * rows, :] += right_ref[0 : 2 * rows, :]
-        image_ref[...] = gram((ens_ref,), widths_ref, scales_ref, coarse_ref[...])
+        coarse_ref[0 : 2 * rows, :] += left_ref[...]
+        coarse_ref[(cols - 2) * rows : cols * rows, :] += right_ref[...]
+        image_ref[...] = gram(
+            (ens_ref,), widths_ref, scales_ref, coarse_ref[...], once_ref, twice_ref
+        )
 
     return body
 
@@ -336,7 +345,7 @@
     cells = cols * rows
 
     def body(mid_ref, left_ref, right_ref, west_ref, tall_ref, east_ref, stencil_ref, flags_ref, ens_ref, ens_low_ref, ens_high_ref,
-             widths_ref, scales_ref, coarse_ref, image_ref, padded_ref, dup_ref, spill_ref, sum_ref, rim_ref):
+             widths_ref, scales_ref, coarse_ref, image_ref, padded_ref, dup_ref, spill_ref, sum_ref, rim_ref, once_ref, twice_ref):
         coefs = lat_coefficients(stencil_ref, rows, 1)
         row = lax.broadcasted_iota(jnp.int32, (rows + 4, CH), 0)
         inside = jnp.where(row < 2, flags_ref[0:1, :], jnp.where(row < rows + 2, 1.0, flags_ref[1:2, :]))
@@ -352,7 +361,7 @@
             rim_ref[cols + col : cols + col + 1, :] = high * flags_ref[1:2, :]
         image = gram(
             (ens_ref, ens_low_ref, ens_high_ref), widths_ref, scales_ref,
-            jnp.concatenate([coarse, rim_ref[...]], axis=0),
+            jnp.concatenate([coarse, rim_ref[...]], axis=0), once_ref, twice_ref,
         )
         image_ref[...] = image[:cells]
         for col in range(cols):
@@ -394,22 +403,19 @@
             return jnp.sum(jnp.where(lane == place, sums, 0.0), axis=1, keepdims=True)
 
         m00, m01, m11, m12 = (pick(place) for place in range(4))
-        beta0 = jnp.sqrt(m00 / entries + EPSILON)
-        alpha0 = (m00 + m01) / (entries * beta0 * beta0)
-        s1 = 1.0 / beta0
-        s0 = (1.0 - alpha0) * s1
-        u1u1 = s0 * s0 * m00 + 2.0 * s0 * s1 * m01 + s1 * s1 * m11
-        beta1 = jnp.sqrt(u1u1 / entries + EPSILON)
-        u0u1 = s0 * m00 + s1 * m01
-        u0lu1 = s0 * m01 + s1 * m11
-        u1lu1 = s0 * s0 * m01 + 2.0 * s0 * s1 * m11 + s1 * s1 * m12
-        c0 = (u0u1 + u0lu1) / (entries * beta0 * beta1)
-        alpha1 = (u1u1 + u1lu1) / (entries * beta1 * beta1)
-        r1 = 1.0 / beta1
-        keep = (1.0 - alpha1) * r1
-        k0 = keep * s0 - c0 / beta0
-        k1 = keep * s1 + s0 * r1
-        k2 = s1 * r1
+        square0 = m00 / entries + EPSILON
+        inverse0 = 1.0 / square0
+        alpha0 = ((m00 + m01) / entries) * inverse0
+        g = 1.0 - alpha0
+        u1u1 = (g * (g * m00 + 2.0 * m01) + m11) * inverse0
+        u1lu1 = (g * (g * m01 + 2.0 * m11) + m12) * inverse0
+        cross = ((g * (m00 + m01) + m01 + m11) / entries) * inverse0
+        square1 = u1u1 / entries + EPSILON
+        alpha1 = ((u1u1 + u1lu1) / entries) / square1
+        beta0, beta1 = jnp.sqrt(square0), jnp.sqrt(square1)
+        k2 = lax.rsqrt(square0) * lax.rsqrt(square1)
+        k1 = k2 * (1.0 - alpha1 + g)
+        k0 = k2 * ((1.0 - alpha1) * g - cross)
         row = lax.broadcasted_iota(jnp.int32, (2, 2), 0)
         col = lax.broadcasted_iota(jnp.int32, (2, 2), 1)
         coef_ref[...] = jnp.where(
@@ -428,6 +434,10 @@
     return body
 
 
+def gram_scratch(cells):
+    return (pltpu.VMEM((PAIRS, 2 * cells, CH), BF16),) * 2
+
+
 def from_neighbours(up, down, axis, paired):
     count = lax.axis_size(axis)
     if paired and count % 2 == 0:
@@ -457,37 +467,38 @@
     cell_block = pltpu.VMEM((cells, CH), F32)
     pair_block = pltpu.VMEM((PAIRS, CH), F32)
     message = pltpu.VMEM((2 * (cols + 4) + (fine_cols + 2) * FINE_HALO, CH), F32)
-    ens_block = pltpu.VMEM((cells, M * CH), BF16)
-    up, down, part, own, own_stencil, widths, scales, ens = pl.pallas_call(
+    ens = ensemble.reshape(cells, M * CH)
+    up, down, part, own, own_stencil, widths, scales = pl.pallas_call(
         prepare_kernel(cols, rows),
         out_shape=(
             message, message, pltpu.VMEM((cols + 4, rows, CH), F32),
             pltpu.VMEM((fine_cols, fine_rows, CH), F32),
-            pltpu.VMEM((2 * fine_rows, CH), F32), pair_block, pair_block, ens_block,
+            pltpu.VMEM((2 * fine_rows, CH), F32), pair_block, pair_block,
         ),
-        in_specs=[VMEM_SPEC] * 5 + [pl.BlockSpec(memory_space=pltpu.HBM)],
-        out_specs=(VMEM_SPEC,) * 8,
+        in_specs=[VMEM_SPEC] * 5,
+        out_specs=(VMEM_SPEC,) * 7,
         scratch_shapes=[
             pltpu.VMEM(((cols + 4) * 5, fine_rows + 16, CH), F32),
             pltpu.VMEM((cols + 4, fine_rows + 8, CH), F32),
-            pltpu.SemaphoreType.DMA,
         ],
-    )(obs_weight, innovation, lat_weight[None], lat_offset[None], band_widths[None],
-      ensemble.reshape(cells, M * CH))
+        cost_estimate=pl.CostEstimate(flops=1 << 29, bytes_accessed=1 << 21, transcendentals=0),
+    )(obs_weight, innovation, lat_weight[None], lat_offset[None], band_widths[None])
     low, high = from_neighbours(up, down, "lat", False)
-    side_block = pltpu.VMEM((2 * rows + 3 * total, CH), F32)
-    to_left, to_right, own_part, tall, stencil = kernel_call(
+    edge_rows = pltpu.VMEM((cols, M * CH), F32)
+    ens_up, ens_down = kernel_call(
+        edges_kernel(cols, rows), (edge_rows, edge_rows), (ens, own_stencil)
+    )
+    ens_low, ens_high = from_neighbours(ens_up, ens_down, "lat", False)
+    side_block = pltpu.VMEM((2 * rows, CH), F32)
+    wide_block = pltpu.VMEM((3, total, CH), F32)
+    to_left, to_right, own_part, to_west, to_east, tall, stencil = kernel_call(
         join_kernel(cols, rows),
-        (side_block, side_block, cell_block,
+        (side_block, side_block, cell_block, wide_block, wide_block,
          pltpu.VMEM((fine_cols, total, CH), F32), pltpu.VMEM((2 * total, CH), F32)),
         (low, high, part, own, own_stencil, flags),
     )
-    west, east = from_neighbours(to_right, to_left, "lon", True)
-    edge_rows = pltpu.VMEM((cols, M * CH), F32)
-    ens_up, ens_down = kernel_call(
-        edges_kernel(cols, rows), (edge_rows, edge_rows), (ens, to_left)
-    )
-    ens_low, ens_high = from_neighbours(ens_up, ens_down, "lat", False)
+    left, right = from_neighbours(to_right, to_left, "lon", True)
+    west, east = from_neighbours(to_east, to_west, "lon", True)
 
     restrict_scratch = (
         pltpu.VMEM((cols * 5, total, CH), F32),
@@ -497,7 +508,7 @@
 
     y0, b0 = kernel_call(
         start_kernel(cols, rows), (cell_block, cell_block),
-        (own_part, west, east, ens, widths, scales),
+        (own_part, left, right, ens, widths, scales), gram_scratch(cells),
     )
     block = b0.reshape(cols, rows, CH)
     low_rows, high_rows = from_neighbours(block[:, -2:], block[:, :2], "lat", False)
@@ -507,7 +518,7 @@
         step_kernel(cols, rows), (cell_block, cell_block, pltpu.VMEM((cols, rows + 2, CH), F32)),
         (mid, mid_left, mid_right, west, tall, east, stencil, flags,
          ens, ens_low, ens_high, widths, scales),
-        middle_scratch + (pltpu.VMEM((2 * cols, CH), F32),),
+        middle_scratch + (pltpu.VMEM((2 * cols, CH), F32),) + gram_scratch(cells + 2 * cols),
     )
     y2, dots = kernel_call(
         last_kernel(rows, devices), (cell_block, pltpu.VMEM((devices, CH), F32)),

time: 53 us -> 46.9 us (0.88)
  waiting for transfers between devices: 20.6 us -> 11.6 us
  starting transfers between devices: 14 us -> 18 us
  Pallas kernels: 6.56 us -> 5.47 us
    ppermute x3, waiting for transfers between devices: 7 us -> 1.84 us  [from_neighbours(): lax.ppermute(up, axis, [(at, (at + 1) % count) for at in range(count)])]
    ppermute x3 -> x4, starting transfers between devices: 3.97 us -> 7.96 us  [from_neighbours(): far = lax.ppermute(jnp.where(odd, up, down), axis, outer)]
    ppermute x3, waiting for transfers between devices: 4.94 us -> 1.07 us  [from_neighbours(): lax.ppermute(down, axis, [((at + 1) % count, at) for at in range(count)])]
    pallas_call x1, Pallas kernels: 2 us -> 1.1 us  [per_device(): pl.pallas_call(prepare_kernel(cols, rows), out_shape=(message, message, p...]
    ppermute x3 -> x4, waiting for transfers between devices: 8.69 us -> 8.7 us  [from_neighbours(): far = lax.ppermute(jnp.where(odd, up, down), axis, outer)]
  transfers between devices with their start and end apart: 12 -> 14, of which waited for: 9 -> 6; matrix products, arithmetic and copies ran while one was open for 0% -> 0% of each run, Pallas kernels for 0% -> 0%
where the time goes in v7:
time: 46.9 us; the launch traced here: 46.7 us
  starting transfers between devices  18 us (38%)
  waiting for transfers between devices  11.6 us (25%)
  blocking collectives  10.6 us (23%)
  Pallas kernels  5.47 us (12%)
  between operations  0.75 us (2%)
    all_to_all x1, blocking collectives, per_device(): lax.all_to_all(dots.reshape(devices, 1, CH), ('lat', 'lon'), 0, 0)  10.6 us
    ppermute x4, waiting for transfers between devices, from_neighbours(): far = lax.ppermute(jnp.where(odd, up, down), axis, outer)  8.7 us
    ppermute x4, starting transfers between devices, from_neighbours(): far = lax.ppermute(jnp.where(odd, up, down), axis, outer)  7.96 us
    ppermute x3, starting transfers between devices, from_neighbours(): lax.ppermute(up, axis, [(at, (at + 1) % count) for at in range(count)])  7 us
    pallas_call x6, Pallas kernels, kernel_call(): pl.pallas_call(body, out_shape=outs, in_specs=[VMEM_SPEC] * len(operands)...  4.37 us
    ppermute x3, starting transfers between devices, from_neighbours(): lax.ppermute(down, axis, [((at + 1) % count, at) for at in range(count)])  2.99 us
    ppermute x3, waiting for transfers between devices, from_neighbours(): lax.ppermute(up, axis, [(at, (at + 1) % count) for at in range(count)])  1.84 us
    pallas_call x1, Pallas kernels, per_device(): pl.pallas_call(prepare_kernel(cols, rows), out_shape=(message, message, p...  1.1 us
  transfers between devices with their start and end apart: 14, of which 6 were waited for; matrix products, arithmetic and copies ran while one was open for 0% of the time, Pallas kernels for 0%

profile of v7, /device:TPU:0, one launch (start us, length us, event | category | flops | bytes accessed | tf_op | source)
XLA Modules:
  0.0 46.7 jit_solution(12676640270379991881)
XLA Ops:
  0.6 0.0 copy-start
  0.6 1.1 %shard_map.77 = (f32[76,128]{1,0:T(8,128)S(1)}, f32[76,128]{1,0:T(8,128)S(1)}, f32[8,8,128]{2,1,0:T(8,128)S(1)}, f32[8,16,128]{2,1,0:T(8,128)S(1)}, f32[32,128]{...) custom-call(f32[8,16,128]{2,1,0:T(8,128)} %weight_ref.1, f32[8,16,128]{2,1,0:T(8,128)} %innovation_ref.1, ...), custom_call_target="tpu_custom_call" | custom-call | flops 536870912 | bytes 2097152 | tf_op jit(solution)/shard_map/pallas_call | solution.py:471
  1.8 3.0 %collective-permute-start = (f32[76,128]{1,0:T(8,128)S(1)}, f32[76,128]{1,0:T(8,128)S(1)}, u32[]{:S(2)}, u32[]{:S(2)}) collective-permute-start(f32[76,128]{1,0:T(8,128)S(1)} %get-tuple-element.27), channel_id=1, source_target_pairs={{0,8},{8,16},{16,24},{24,0},{1,9},{9,17},{17,25},{25,1},{2,10},{10... | collective-permute-start | bytes 116744 | tf_op jit(solution)/shard_map/ppermute | solution.py:450
  4.8 1.0 %collective-permute-start.1 = (f32[76,128]{1,0:T(8,128)S(1)}, f32[76,128]{1,0:T(8,128)S(1)}, u32[]{:S(2)}, u32[]{:S(2)}) collective-permute-start(f32[76,128]{1,0:T(8,128)S(1)} %get-tuple-element.28), channel_id=1, source_target_pairs={{8,0},{16,8},{24,16},{0,24},{9,1},{17,9},{25,17},{1,25},{10,2},{18... | collective-permute-start | bytes 116744 | tf_op jit(solution)/shard_map/ppermute | solution.py:451
  5.8 0.1 add_convert_fusion
  5.9 1.8 %collective-permute-done.low_ref = f32[76,128]{1,0:T(8,128)S(1)} collective-permute-done((f32[76,128]{1,0:T(8,128)S(1)}, f32[76,128]{1,0:T(8,128)S(1)}, u32[]{:S(2)}, u32[]{:S(2)}) %collective-permute-start) | collective-permute-done | bytes 38944 | tf_op jit(solution)/shard_map/ppermute | solution.py:450
  7.7 1.1 %collective-permute-done.1.high_ref = f32[76,128]{1,0:T(8,128)S(1)} collective-permute-done((f32[76,128]{1,0:T(8,128)S(1)}, f32[76,128]{1,0:T(8,128)S(1)}, u32[]{:S(2)}, u32[]{:S(2)}) %collective-permute-start.1) | collective-permute-done | bytes 38944 | tf_op jit(solution)/shard_map/ppermute | solution.py:451
  8.8 0.1 broadcast_in_dim.18.flags_ref
  8.9 1.9 %collective-permute-start.3 = (f32[16,128]{1,0:T(8,128)S(1)}, f32[16,128]{1,0:T(8,128)S(1)}, u32[]{:S(2)}, u32[]{:S(2)}) collective-permute-start(f32[16,128]{1,0:T(8,128)S(1)} %get-tuple-element.68), channel_id=1, source_target_pairs={{0,7},{1,2},{2,1},{3,4},{4,3},{5,6},{6,5},{7,0},{8,15},{9,10},{10,... | collective-permute-start | bytes 24584 | tf_op jit(solution)/shard_map/ppermute | solution.py:447
  10.8 0.0 collective-permute-start.2
  10.8 3.1 %collective-permute-done.3 = f32[16,128]{1,0:T(8,128)S(1)} collective-permute-done((f32[16,128]{1,0:T(8,128)S(1)}, f32[16,128]{1,0:T(8,128)S(1)}, u32[]{:S(2)}, u32[]{:S(2)}) %collective-permute-start.3) | collective-permute-done | bytes 8224 | tf_op jit(solution)/shard_map/ppermute | solution.py:447
  13.8 0.0 collective-permute-done.2
  13.8 0.0 copy-done
  13.8 1.0 %shard_map.79 = (f32[32,128]{1,0:T(8,128)S(1)}, f32[32,128]{1,0:T(8,128)S(1)}) custom-call(f32[32,128]{1,0:T(8,128)S(1)} %get-tuple-element.32.own_ref, f32[16,128]{1,0:T(8,128)S(1)} %get-tuple-element.67.left_ref, f32[16,128]{1,0:T(8,128)S(1)} %get-tuple-element.66.right_ref, bf16[32,10240]{1,0:T(8,128)(2,1)S(1)} %bitcast.12, ...), custom_call_target="tpu_custom_call" | custom-call | tf_op jit(solution)/shard_map/pallas_call | solution.py:31
  14.9 2.4 %collective-permute-start.4 = (f32[4,2,128]{2,1,0:T(2,128)S(1)}, f32[4,2,128]{2,1,0:T(2,128)S(1)}, u32[]{:S(2)}, u32[]{:S(2)}) collective-permute-start(f32[4,2,128]{2,1,0:T(2,128)S(1)} %get-tuple-element.64), channel_id=1, source_target_pairs={{0,8},{8,16},{16,24},{24,0},{1,9},{9,17},{17,25},{25,1},{2,10},{10... | collective-permute-start | bytes 12296 | tf_op jit(solution)/shard_map/ppermute | solution.py:450
  17.3 0.5 %collective-permute-start.5 = (f32[4,2,128]{2,1,0:T(2,128)S(1)}, f32[4,2,128]{2,1,0:T(2,128)S(1)}, u32[]{:S(2)}, u32[]{:S(2)}) collective-permute-start(f32[4,2,128]{2,1,0:T(2,128)S(1)} %get-tuple-element.65), channel_id=1, source_target_pairs={{8,0},{16,8},{24,16},{0,24},{9,1},{17,9},{25,17},{1,25},{10,2},{18... | collective-permute-start | bytes 12296 | tf_op jit(solution)/shard_map/ppermute | solution.py:451
  17.9 0.2 shard_map.80
  18.1 1.5 %collective-permute-start.10 = (f32[4,10240]{1,0:T(4,128)S(1)}, f32[4,10240]{1,0:T(4,128)S(1)}, u32[]{:S(2)}, u32[]{:S(2)}) collective-permute-start(f32[4,10240]{1,0:T(4,128)S(1)} %get-tuple-element.42), channel_id=1, source_target_pairs={{0,8},{8,16},{16,24},{24,0},{1,9},{9,17},{17,25},{25,1},{2,10},{10... | collective-permute-start | bytes 491528 | tf_op jit(solution)/shard_map/ppermute | solution.py:450
  19.6 1.4 %collective-permute-start.11 = (f32[4,10240]{1,0:T(4,128)S(1)}, f32[4,10240]{1,0:T(4,128)S(1)}, u32[]{:S(2)}, u32[]{:S(2)}) collective-permute-start(f32[4,10240]{1,0:T(4,128)S(1)} %get-tuple-element.43), channel_id=1, source_target_pairs={{8,0},{16,8},{24,16},{0,24},{9,1},{17,9},{25,17},{1,25},{10,2},{18... | collective-permute-start | bytes 491528 | tf_op jit(solution)/shard_map/ppermute | solution.py:451
  21.0 0.0 collective-permute-done.4
  21.1 0.0 collective-permute-done.5
  21.1 0.7 %collective-permute-start.7 = (f32[3,12,128]{2,1,0:T(8,128)S(1)}, f32[3,12,128]{2,1,0:T(8,128)S(1)}, u32[]{:S(2)}, u32[]{:S(2)}) collective-permute-start(f32[3,12,128]{2,1,0:T(8,128)S(1)} %get-tuple-element.62), channel_id=1, source_target_pairs={{0,7},{1,2},{2,1},{3,4},{4,3},{5,6},{6,5},{7,0},{8,15},{9,10},{10,... | collective-permute-start | bytes 55304 | tf_op jit(solution)/shard_map/ppermute | solution.py:447
  21.8 0.0 collective-permute-start.6
  21.8 2.9 %collective-permute-start.9 = (f32[3,28,128]{2,1,0:T(8,128)S(1)}, f32[3,28,128]{2,1,0:T(8,128)S(1)}, u32[]{:S(2)}, u32[]{:S(2)}) collective-permute-start(f32[3,28,128]{2,1,0:T(8,128)S(1)} %get-tuple-element.54), channel_id=1, source_target_pairs={{0,7},{1,2},{2,1},{3,4},{4,3},{5,6},{6,5},{7,0},{8,15},{9,10},{10,... | collective-permute-start | bytes 129032 | tf_op jit(solution)/shard_map/ppermute | solution.py:447
  24.8 1.5 %collective-permute-done.7 = f32[3,12,128]{2,1,0:T(8,128)S(1)} collective-permute-done((f32[3,12,128]{2,1,0:T(8,128)S(1)}, f32[3,12,128]{2,1,0:T(8,128)S(1)}, u32[]{:S(2)}, u32[]{:S(2)}) %collective-permute-start.7) | collective-permute-done | bytes 18464 | tf_op jit(solution)/shard_map/ppermute | solution.py:447
  26.3 0.0 collective-permute-start.8
  26.3 0.0 collective-permute-done.6
  26.3 1.4 %collective-permute-done.9 = f32[3,28,128]{2,1,0:T(8,128)S(1)} collective-permute-done((f32[3,28,128]{2,1,0:T(8,128)S(1)}, f32[3,28,128]{2,1,0:T(8,128)S(1)}, u32[]{:S(2)}, u32[]{:S(2)}) %collective-permute-start.9) | collective-permute-done | bytes 43040 | tf_op jit(solution)/shard_map/ppermute | solution.py:447
  27.7 0.0 collective-permute-done.8
  27.7 0.0 collective-permute-done.10.ens_low_ref
  27.8 0.0 collective-permute-done.11.ens_high_ref
  27.8 1.5 %shard_map.81 = (f32[32,128]{1,0:T(8,128)S(1)}, f32[32,128]{1,0:T(8,128)S(1)}, f32[4,10,128]{2,1,0:T(8,128)S(1)}) custom-call(f32[4,12,128]{2,1,0:T(8,128)S(1)} %pad_maximum_fusion.mid_ref, f32[3,12,128]{2,1,0:T(8,128)S(1)} %get-tuple-element.59.left_ref, f32[3,12,128]{2,1,0:T(8,128)S(1)} %get-tuple-element.58.right_ref, ...), custom_call_target="tpu_custom_call" | custom-call | tf_op jit(solution)/shard_map/pallas_call | solution.py:31
  29.3 2.4 %collective-permute-start.13 = (f32[3,10,128]{2,1,0:T(8,128)S(1)}, f32[3,10,128]{2,1,0:T(8,128)S(1)}, u32[]{:S(2)}, u32[]{:S(2)}) collective-permute-start(f32[3,10,128]{2,1,0:T(8,128)S(1)} %get-tuple-element.60), channel_id=1, source_target_pairs={{0,7},{1,2},{2,1},{3,4},{4,3},{5,6},{6,5},{7,0},{8,15},{9,10},{10,... | collective-permute-start | bytes 46088 | tf_op jit(solution)/shard_map/ppermute | solution.py:447
  31.7 0.0 collective-permute-start.12
  31.7 2.7 %collective-permute-done.13 = f32[3,10,128]{2,1,0:T(8,128)S(1)} collective-permute-done((f32[3,10,128]{2,1,0:T(8,128)S(1)}, f32[3,10,128]{2,1,0:T(8,128)S(1)}, u32[]{:S(2)}, u32[]{:S(2)}) %collective-permute-start.13) | collective-permute-done | bytes 15392 | tf_op jit(solution)/shard_map/ppermute | solution.py:447
  34.4 0.0 collective-permute-done.12
  34.4 0.2 shard_map.82
  34.6 10.6 %all_to_all.5 = f32[32,1,128]{2,1,0:T(1,128)S(1)} all-to-all(f32[32,1,128]{2,1,0:T(1,128)S(1)} %bitcast.19), channel_id=1, replica_groups=mesh['lat'=4,'lon'=8] {'lat','lon'}, dimensions={0} | all-to-all | bytes 32768 | tf_op jit(solution)/shard_map/all_to_all | solution.py:528
  45.3 1.4 %shard_map.83 = (f32[2,2]{1,0:T(2,128)}, bf16[32,5120]{1,0:T(8,128)(2,1)}) custom-call(f32[32,128]{1,0:T(8,128)S(1)} %bitcast.18, f32[32,128]{1,0:T(8,128)S(1)} %get-tuple-element.45.y0_ref, f32[32,128]{1,0:T(8,128)S(1)} %get-tuple-element.46.y1_ref, f32[32,128]{1,0:T(8,128)S(1)} %get-tuple-element.49.y2_ref, bf16[32,10240]{1,0:T(8,128)(2,1)S(1)} %bitcast.15, ...), custom_call_target="tpu_custom_call" | custom-call | tf_op jit(solution)/shard_map/pallas_call | solution.py:31
  (11 shorter events, 0.1 us)
Async XLA Ops:
  0.6 13.2 %copy-start = (bf16[4,8,10240]{2,1,0:T(8,128)(2,1)S(1)}, bf16[4,8,10240]{2,1,0:T(8,128)(2,1)}, u32[]{:S(2)}) copy-start(bf16[4,8,10240]{2,1,0:T(8,128)(2,1)} %param.6) | copy-start | bytes 1966084
  1.8 6.0 %collective-permute-start = (f32[76,128]{1,0:T(8,128)S(1)}, f32[76,128]{1,0:T(8,128)S(1)}, u32[]{:S(2)}, u32[]{:S(2)}) collective-permute-start(f32[76,128]{1,0:T(8,128)S(1)} %get-tuple-element.27), channel_id=1, source_target_pairs={{0,8},{8,16},{16,24},{24,0},{1,9},{9,17},{17,25},{25,1},{2,10},{10... | collective-permute-start | bytes 116744 | tf_op jit(solution)/shard_map/ppermute | solution.py:450
  4.8 4.0 %collective-permute-start.1 = (f32[76,128]{1,0:T(8,128)S(1)}, f32[76,128]{1,0:T(8,128)S(1)}, u32[]{:S(2)}, u32[]{:S(2)}) collective-permute-start(f32[76,128]{1,0:T(8,128)S(1)} %get-tuple-element.28), channel_id=1, source_target_pairs={{8,0},{16,8},{24,16},{0,24},{9,1},{17,9},{25,17},{1,25},{10,2},{18... | collective-permute-start | bytes 116744 | tf_op jit(solution)/shard_map/ppermute | solution.py:451
  8.9 4.9 %collective-permute-start.3 = (f32[16,128]{1,0:T(8,128)S(1)}, f32[16,128]{1,0:T(8,128)S(1)}, u32[]{:S(2)}, u32[]{:S(2)}) collective-permute-start(f32[16,128]{1,0:T(8,128)S(1)} %get-tuple-element.68), channel_id=1, source_target_pairs={{0,7},{1,2},{2,1},{3,4},{4,3},{5,6},{6,5},{7,0},{8,15},{9,10},{10,... | collective-permute-start | bytes 24584 | tf_op jit(solution)/shard_map/ppermute | solution.py:447
  10.8 3.1 %collective-permute-start.2 = (f32[16,128]{1,0:T(8,128)S(1)}, f32[16,128]{1,0:T(8,128)S(1)}, u32[]{:S(2)}, u32[]{:S(2)}) collective-permute-start(f32[16,128]{1,0:T(8,128)S(1)} %get-tuple-element.69), channel_id=1, source_target_pairs={{0,1},{1,0},{2,3},{3,2},{4,5},{5,4},{6,7},{7,6},{8,9},{9,8},{10,11... | collective-permute-start | bytes 24584 | tf_op jit(solution)/shard_map/ppermute | solution.py:448
  14.9 6.2 %collective-permute-start.4 = (f32[4,2,128]{2,1,0:T(2,128)S(1)}, f32[4,2,128]{2,1,0:T(2,128)S(1)}, u32[]{:S(2)}, u32[]{:S(2)}) collective-permute-start(f32[4,2,128]{2,1,0:T(2,128)S(1)} %get-tuple-element.64), channel_id=1, source_target_pairs={{0,8},{8,16},{16,24},{24,0},{1,9},{9,17},{17,25},{25,1},{2,10},{10... | collective-permute-start | bytes 12296 | tf_op jit(solution)/shard_map/ppermute | solution.py:450
  17.3 3.7 %collective-permute-start.5 = (f32[4,2,128]{2,1,0:T(2,128)S(1)}, f32[4,2,128]{2,1,0:T(2,128)S(1)}, u32[]{:S(2)}, u32[]{:S(2)}) collective-permute-start(f32[4,2,128]{2,1,0:T(2,128)S(1)} %get-tuple-element.65), channel_id=1, source_target_pairs={{8,0},{16,8},{24,16},{0,24},{9,1},{17,9},{25,17},{1,25},{10,2},{18... | collective-permute-start | bytes 12296 | tf_op jit(solution)/shard_map/ppermute | solution.py:451
  18.1 9.7 %collective-permute-start.10 = (f32[4,10240]{1,0:T(4,128)S(1)}, f32[4,10240]{1,0:T(4,128)S(1)}, u32[]{:S(2)}, u32[]{:S(2)}) collective-permute-start(f32[4,10240]{1,0:T(4,128)S(1)} %get-tuple-element.42), channel_id=1, source_target_pairs={{0,8},{8,16},{16,24},{24,0},{1,9},{9,17},{17,25},{25,1},{2,10},{10... | collective-permute-start | bytes 491528 | tf_op jit(solution)/shard_map/ppermute | solution.py:450
  19.6 8.1 %collective-permute-start.11 = (f32[4,10240]{1,0:T(4,128)S(1)}, f32[4,10240]{1,0:T(4,128)S(1)}, u32[]{:S(2)}, u32[]{:S(2)}) collective-permute-start(f32[4,10240]{1,0:T(4,128)S(1)} %get-tuple-element.43), channel_id=1, source_target_pairs={{8,0},{16,8},{24,16},{0,24},{9,1},{17,9},{25,17},{1,25},{10,2},{18... | collective-permute-start | bytes 491528 | tf_op jit(solution)/shard_map/ppermute | solution.py:451
  21.1 5.2 %collective-permute-start.7 = (f32[3,12,128]{2,1,0:T(8,128)S(1)}, f32[3,12,128]{2,1,0:T(8,128)S(1)}, u32[]{:S(2)}, u32[]{:S(2)}) collective-permute-start(f32[3,12,128]{2,1,0:T(8,128)S(1)} %get-tuple-element.62), channel_id=1, source_target_pairs={{0,7},{1,2},{2,1},{3,4},{4,3},{5,6},{6,5},{7,0},{8,15},{9,10},{10,... | collective-permute-start | bytes 55304 | tf_op jit(solution)/shard_map/ppermute | solution.py:447
  21.8 4.5 %collective-permute-start.6 = (f32[3,12,128]{2,1,0:T(8,128)S(1)}, f32[3,12,128]{2,1,0:T(8,128)S(1)}, u32[]{:S(2)}, u32[]{:S(2)}) collective-permute-start(f32[3,12,128]{2,1,0:T(8,128)S(1)} %get-tuple-element.63), channel_id=1, source_target_pairs={{0,1},{1,0},{2,3},{3,2},{4,5},{5,4},{6,7},{7,6},{8,9},{9,8},{10,11... | collective-permute-start | bytes 55304 | tf_op jit(solution)/shard_map/ppermute | solution.py:448
  21.8 5.9 %collective-permute-start.9 = (f32[3,28,128]{2,1,0:T(8,128)S(1)}, f32[3,28,128]{2,1,0:T(8,128)S(1)}, u32[]{:S(2)}, u32[]{:S(2)}) collective-permute-start(f32[3,28,128]{2,1,0:T(8,128)S(1)} %get-tuple-element.54), channel_id=1, source_target_pairs={{0,7},{1,2},{2,1},{3,4},{4,3},{5,6},{6,5},{7,0},{8,15},{9,10},{10,... | collective-permute-start | bytes 129032 | tf_op jit(solution)/shard_map/ppermute | solution.py:447
  26.3 1.4 %collective-permute-start.8 = (f32[3,28,128]{2,1,0:T(8,128)S(1)}, f32[3,28,128]{2,1,0:T(8,128)S(1)}, u32[]{:S(2)}, u32[]{:S(2)}) collective-permute-start(f32[3,28,128]{2,1,0:T(8,128)S(1)} %get-tuple-element.55), channel_id=1, source_target_pairs={{0,1},{1,0},{2,3},{3,2},{4,5},{5,4},{6,7},{7,6},{8,9},{9,8},{10,11... | collective-permute-start | bytes 129032 | tf_op jit(solution)/shard_map/ppermute | solution.py:448
  29.3 5.1 %collective-permute-start.13 = (f32[3,10,128]{2,1,0:T(8,128)S(1)}, f32[3,10,128]{2,1,0:T(8,128)S(1)}, u32[]{:S(2)}, u32[]{:S(2)}) collective-permute-start(f32[3,10,128]{2,1,0:T(8,128)S(1)} %get-tuple-element.60), channel_id=1, source_target_pairs={{0,7},{1,2},{2,1},{3,4},{4,3},{5,6},{6,5},{7,0},{8,15},{9,10},{10,... | collective-permute-start | bytes 46088 | tf_op jit(solution)/shard_map/ppermute | solution.py:447
  31.7 2.7 %collective-permute-start.12 = (f32[3,10,128]{2,1,0:T(8,128)S(1)}, f32[3,10,128]{2,1,0:T(8,128)S(1)}, u32[]{:S(2)}, u32[]{:S(2)}) collective-permute-start(f32[3,10,128]{2,1,0:T(8,128)S(1)} %get-tuple-element.61), channel_id=1, source_target_pairs={{0,1},{1,0},{2,3},{3,2},{4,5},{5,4},{6,7},{7,6},{8,9},{9,8},{10,11... | collective-permute-start | bytes 46088 | tf_op jit(solution)/shard_map/ppermute | solution.py:448

commit v8 on v7

--- a/solution.py
+++ b/solution.py
@@ -65,23 +65,37 @@
     return pltpu.roll(value, LEV, 1)
 
 
-def members(ens_refs, pair):
-    result = []
-    for member in (2 * pair, 2 * pair + 1):
-        parts = [ref[:, member * CH : (member + 1) * CH].astype(F32) for ref in ens_refs]
-        result.append(parts[0] if len(parts) == 1 else jnp.concatenate(parts, axis=0))
-    return result
-
-
-def field_sum(first, second, coarse, low_half):
-    left, right = first * coarse, second * coarse
-    return jnp.where(low_half, left, right) + swap_halves(jnp.where(low_half, right, left))
-
-
-def gram(ens_refs, widths_ref, scales_ref, coarse, once_ref, twice_ref):
+def by_field(value, low_half):
+    swapped = swap_halves(value)
+    return jnp.where(low_half, value, swapped), jnp.where(low_half, swapped, value)
+
+
+def arrange_kernel(body_rows):
+    def body(*refs):
+        ens_refs, (one_ref, two_ref) = refs[:-2], refs[-2:]
+        low_half = lax.broadcasted_iota(jnp.int32, (body_rows, CH), 1) < LEV
+        for pair in range(PAIRS):
+            both = []
+            for member in (2 * pair, 2 * pair + 1):
+                parts = [ref[:, member * CH : (member + 1) * CH].astype(F32) for ref in ens_refs]
+                both.append(parts[0] if len(parts) == 1 else jnp.concatenate(parts, axis=0))
+            first, second = both
+            one_ref[pair] = jnp.where(low_half, first, swap_halves(second))
+            two_ref[pair] = jnp.where(low_half, swap_halves(first), second)
+
+    return body
+
+
+def pair_members(ens_refs, pair):
+    parts = [ref[pair] for ref in ens_refs]
+    return parts[0] if len(parts) == 1 else jnp.concatenate(parts, axis=0)
+
+
+def gram(ones, twos, widths_ref, scales_ref, coarse, once_ref, twice_ref):
     distances = pair_distances()
     cells = coarse.shape[0]
     low_half = lax.broadcasted_iota(jnp.int32, coarse.shape, 1) < LEV
+    field_one, field_two = by_field(coarse, low_half)
 
     def put(ref, pair, value):
         ref[pair, 0:cells, :], ref[pair, cells : 2 * cells, :] = split(value)
@@ -92,21 +106,20 @@
         return both[:cells] + both[cells:]
 
     for pair in range(PAIRS):
-        first, second = members(ens_refs, pair)
-        put(once_ref, pair, field_sum(first, second, coarse, low_half))
+        summed = pair_members(ones, pair) * field_one + pair_members(twos, pair) * field_two
+        put(once_ref, pair, summed)
     for pair in range(PAIRS):
         put(twice_ref, pair, apply(once_ref, pair))
-    total = jnp.zeros(coarse.shape, F32)
+    total_one = jnp.zeros(coarse.shape, F32)
+    total_two = jnp.zeros(coarse.shape, F32)
     for pair in range(PAIRS):
         scale = scales_ref[pair : pair + 1, :]
         twice = apply(twice_ref, pair) * (scale * scale)
-        swapped = swap_halves(twice)
-        first, second = members(ens_refs, pair)
-        total = total + (
-            first * jnp.where(low_half, twice, swapped)
-            + second * jnp.where(low_half, swapped, twice)
-        )
-    return total
+        total_one = total_one + pair_members(ones, pair) * twice
+        total_two = total_two + pair_members(twos, pair) * twice
+    return jnp.where(
+        low_half, total_one + swap_halves(total_one), total_two + swap_halves(total_two)
+    )
 
 
 def prepare_kernel(cols, rows):
@@ -330,12 +343,12 @@
 
 
 def start_kernel(cols, rows):
-    def body(own_ref, left_ref, right_ref, ens_ref, widths_ref, scales_ref, coarse_ref, image_ref, once_ref, twice_ref):
+    def body(own_ref, left_ref, right_ref, one_ref, two_ref, widths_ref, scales_ref, coarse_ref, image_ref, once_ref, twice_ref):
         coarse_ref[...] = own_ref[...]
         coarse_ref[0 : 2 * rows, :] += left_ref[...]
         coarse_ref[(cols - 2) * rows : cols * rows, :] += right_ref[...]
         image_ref[...] = gram(
-            (ens_ref,), widths_ref, scales_ref, coarse_ref[...], once_ref, twice_ref
+            (one_ref,), (two_ref,), widths_ref, scales_ref, coarse_ref[...], once_ref, twice_ref
         )
 
     return body
@@ -344,7 +357,7 @@
 def step_kernel(cols, rows):
     cells = cols * rows
 
-    def body(mid_ref, left_ref, right_ref, west_ref, tall_ref, east_ref, stencil_ref, flags_ref, ens_ref, ens_low_ref, ens_high_ref,
+    def body(mid_ref, left_ref, right_ref, west_ref, tall_ref, east_ref, stencil_ref, flags_ref, one_ref, two_ref, rim_one_ref, rim_two_ref,
              widths_ref, scales_ref, coarse_ref, image_ref, padded_ref, dup_ref, spill_ref, sum_ref, rim_ref, once_ref, twice_ref):
         coefs = lat_coefficients(stencil_ref, rows, 1)
         row = lax.broadcasted_iota(jnp.int32, (rows + 4, CH), 0)
@@ -360,7 +373,7 @@
             rim_ref[col : col + 1, :] = low * flags_ref[0:1, :]
             rim_ref[cols + col : cols + col + 1, :] = high * flags_ref[1:2, :]
         image = gram(
-            (ens_ref, ens_low_ref, ens_high_ref), widths_ref, scales_ref,
+            (one_ref, rim_one_ref), (two_ref, rim_two_ref), widths_ref, scales_ref,
             jnp.concatenate([coarse, rim_ref[...]], axis=0), once_ref, twice_ref,
         )
         image_ref[...] = image[:cells]
@@ -395,7 +408,7 @@
 
 
 def final_kernel(entries):
-    def body(dots_ref, y0_ref, y1_ref, y2_ref, ens_ref, widths_ref, scales_ref, coef_ref, vector_ref):
+    def body(dots_ref, y0_ref, y1_ref, y2_ref, one_ref, two_ref, widths_ref, scales_ref, coef_ref, vector_ref):
         sums = jnp.sum(dots_ref[...], axis=0, keepdims=True)
         lane = lax.broadcasted_iota(jnp.int32, (1, CH), 1)
 
@@ -424,10 +437,10 @@
         coarse = k0 * y0_ref[...] + k1 * y1_ref[...] + k2 * y2_ref[...]
         distances = pair_distances()
         low_half = lax.broadcasted_iota(jnp.int32, coarse.shape, 1) < LEV
+        field_one, field_two = by_field(coarse, low_half)
         for pair in range(PAIRS):
             matrix = hat(widths_ref, pair, distances)
-            first, second = members((ens_ref,), pair)
-            summed = field_sum(first, second, coarse, low_half)
+            summed = one_ref[pair] * field_one + two_ref[pair] * field_two
             out = product(summed, matrix) * scales_ref[pair : pair + 1, :]
             vector_ref[:, pair * CH : (pair + 1) * CH] = out.astype(BF16)
 
@@ -500,6 +513,11 @@
     left, right = from_neighbours(to_right, to_left, "lon", True)
     west, east = from_neighbours(to_east, to_west, "lon", True)
 
+    arranged = (pltpu.VMEM((PAIRS, cells, CH), F32),) * 2
+    one, two = kernel_call(arrange_kernel(cells), arranged, (ens,))
+    rim = (pltpu.VMEM((PAIRS, 2 * cols, CH), F32),) * 2
+    rim_one, rim_two = kernel_call(arrange_kernel(2 * cols), rim, (ens_low, ens_high))
+
     restrict_scratch = (
         pltpu.VMEM((cols * 5, total, CH), F32),
         pltpu.VMEM((cols, 2 * rows + 8, CH), F32),
@@ -508,7 +526,7 @@
 
     y0, b0 = kernel_call(
         start_kernel(cols, rows), (cell_block, cell_block),
-        (own_part, left, right, ens, widths, scales), gram_scratch(cells),
+        (own_part, left, right, one, two, widths, scales), gram_scratch(cells),
     )
     block = b0.reshape(cols, rows, CH)
     low_rows, high_rows = from_neighbours(block[:, -2:], block[:, :2], "lat", False)
@@ -517,7 +535,7 @@
     y1, b1, mid1 = kernel_call(
         step_kernel(cols, rows), (cell_block, cell_block, pltpu.VMEM((cols, rows + 2, CH), F32)),
         (mid, mid_left, mid_right, west, tall, east, stencil, flags,
-         ens, ens_low, ens_high, widths, scales),
+         one, two, rim_one, rim_two, widths, scales),
         middle_scratch + (pltpu.VMEM((2 * cols, CH), F32),) + gram_scratch(cells + 2 * cols),
     )
     y2, dots = kernel_call(
@@ -529,7 +547,7 @@
     coefficients, vector = kernel_call(
         final_kernel(entries),
         (jax.ShapeDtypeStruct((2, 2), F32), jax.ShapeDtypeStruct((cells, M * LEV), BF16)),
-        (shared, y0, y1, y2, ens, widths, scales),
+        (shared, y0, y1, y2, one, two, widths, scales),
     )
     return coefficients, vector.reshape(cols, rows, M * LEV)
 

time: 46.9 us -> 46.9 us (level)
    pallas_call x6 -> x8, Pallas kernels: 4.37 us -> 4.7 us  [kernel_call(): pl.pallas_call(body, out_shape=outs, in_specs=[VMEM_SPEC] * len(operands)...]
  transfers between devices with their start and end apart: 14 -> 14, of which waited for: 6 -> 6; matrix products, arithmetic and copies ran while one was open for 0% -> 0% of each run, Pallas kernels for 0% -> 1%
where the time goes in v8:
time: 46.9 us; the launch traced here: 46.7 us
  starting transfers between devices  18 us (38%)
  waiting for transfers between devices  11.3 us (24%)
  blocking collectives  10.6 us (23%)
  Pallas kernels  5.8 us (12%)
  between operations  0.76 us (2%)
    all_to_all x1, blocking collectives, per_device(): lax.all_to_all(dots.reshape(devices, 1, CH), ('lat', 'lon'), 0, 0)  10.6 us
    ppermute x4, waiting for transfers between devices, from_neighbours(): far = lax.ppermute(jnp.where(odd, up, down), axis, outer)  8.42 us
    ppermute x4, starting transfers between devices, from_neighbours(): far = lax.ppermute(jnp.where(odd, up, down), axis, outer)  7.96 us
    ppermute x3, starting transfers between devices, from_neighbours(): lax.ppermute(up, axis, [(at, (at + 1) % count) for at in range(count)])  7 us
    pallas_call x8, Pallas kernels, kernel_call(): pl.pallas_call(body, out_shape=outs, in_specs=[VMEM_SPEC] * len(operands)...  4.7 us
    ppermute x3, starting transfers between devices, from_neighbours(): lax.ppermute(down, axis, [((at + 1) % count, at) for at in range(count)])  2.99 us
    ppermute x3, waiting for transfers between devices, from_neighbours(): lax.ppermute(up, axis, [(at, (at + 1) % count) for at in range(count)])  1.84 us
    pallas_call x1, Pallas kernels, per_device(): pl.pallas_call(prepare_kernel(cols, rows), out_shape=(message, message, p...  1.1 us
  transfers between devices with their start and end apart: 14, of which 6 were waited for; matrix products, arithmetic and copies ran while one was open for 0% of the time, Pallas kernels for 1%

profile of v8, /device:TPU:0, one launch (start us, length us, event | category | flops | bytes accessed | tf_op | source)
XLA Modules:
  0.0 46.7 jit_solution(7137131846046524801)
XLA Ops:
  0.6 0.0 copy-start
  0.6 1.1 %shard_map.77 = (f32[76,128]{1,0:T(8,128)S(1)}, f32[76,128]{1,0:T(8,128)S(1)}, f32[8,8,128]{2,1,0:T(8,128)S(1)}, f32[8,16,128]{2,1,0:T(8,128)S(1)}, f32[32,128]{...) custom-call(f32[8,16,128]{2,1,0:T(8,128)} %weight_ref.1, f32[8,16,128]{2,1,0:T(8,128)} %innovation_ref.1, ...), custom_call_target="tpu_custom_call" | custom-call | flops 536870912 | bytes 2097152 | tf_op jit(solution)/shard_map/pallas_call | solution.py:484
  1.8 3.0 %collective-permute-start = (f32[76,128]{1,0:T(8,128)S(1)}, f32[76,128]{1,0:T(8,128)S(1)}, u32[]{:S(2)}, u32[]{:S(2)}) collective-permute-start(f32[76,128]{1,0:T(8,128)S(1)} %get-tuple-element.31), channel_id=1, source_target_pairs={{0,8},{8,16},{16,24},{24,0},{1,9},{9,17},{17,25},{25,1},{2,10},{10... | collective-permute-start | bytes 116744 | tf_op jit(solution)/shard_map/ppermute | solution.py:463
  4.8 1.0 %collective-permute-start.1 = (f32[76,128]{1,0:T(8,128)S(1)}, f32[76,128]{1,0:T(8,128)S(1)}, u32[]{:S(2)}, u32[]{:S(2)}) collective-permute-start(f32[76,128]{1,0:T(8,128)S(1)} %get-tuple-element.32), channel_id=1, source_target_pairs={{8,0},{16,8},{24,16},{0,24},{9,1},{17,9},{25,17},{1,25},{10,2},{18... | collective-permute-start | bytes 116744 | tf_op jit(solution)/shard_map/ppermute | solution.py:464
  5.8 0.1 add_convert_fusion
  5.9 1.8 %collective-permute-done.low_ref = f32[76,128]{1,0:T(8,128)S(1)} collective-permute-done((f32[76,128]{1,0:T(8,128)S(1)}, f32[76,128]{1,0:T(8,128)S(1)}, u32[]{:S(2)}, u32[]{:S(2)}) %collective-permute-start) | collective-permute-done | bytes 38944 | tf_op jit(solution)/shard_map/ppermute | solution.py:463
  7.7 1.1 %collective-permute-done.1.high_ref = f32[76,128]{1,0:T(8,128)S(1)} collective-permute-done((f32[76,128]{1,0:T(8,128)S(1)}, f32[76,128]{1,0:T(8,128)S(1)}, u32[]{:S(2)}, u32[]{:S(2)}) %collective-permute-start.1) | collective-permute-done | bytes 38944 | tf_op jit(solution)/shard_map/ppermute | solution.py:464
  8.8 0.1 broadcast_in_dim.18.flags_ref
  8.9 1.9 %collective-permute-start.3 = (f32[16,128]{1,0:T(8,128)S(1)}, f32[16,128]{1,0:T(8,128)S(1)}, u32[]{:S(2)}, u32[]{:S(2)}) collective-permute-start(f32[16,128]{1,0:T(8,128)S(1)} %get-tuple-element.76), channel_id=1, source_target_pairs={{0,7},{1,2},{2,1},{3,4},{4,3},{5,6},{6,5},{7,0},{8,15},{9,10},{10,... | collective-permute-start | bytes 24584 | tf_op jit(solution)/shard_map/ppermute | solution.py:460
  10.8 0.0 collective-permute-start.2
  10.8 0.0 copy-done
  10.8 0.3 shard_map.79
  11.0 2.8 %collective-permute-done.3 = f32[16,128]{1,0:T(8,128)S(1)} collective-permute-done((f32[16,128]{1,0:T(8,128)S(1)}, f32[16,128]{1,0:T(8,128)S(1)}, u32[]{:S(2)}, u32[]{:S(2)}) %collective-permute-start.3) | collective-permute-done | bytes 8224 | tf_op jit(solution)/shard_map/ppermute | solution.py:460
  13.8 0.0 collective-permute-done.2
  13.8 1.0 %shard_map.80 = (f32[32,128]{1,0:T(8,128)S(1)}, f32[32,128]{1,0:T(8,128)S(1)}) custom-call(f32[32,128]{1,0:T(8,128)S(1)} %get-tuple-element.36.own_ref, f32[16,128]{1,0:T(8,128)S(1)} %get-tuple-element.75.left_ref, f32[16,128]{1,0:T(8,128)S(1)} %get-tuple-element.74.right_ref, f32[40,32,128]{2,1,0:T(8,128)S(1)} %get-tuple-element.39.one_ref, ...), custom_call_target="tpu_custom_call" | custom-call | tf_op jit(solution)/shard_map/pallas_call | solution.py:31
  14.8 2.4 %collective-permute-start.4 = (f32[4,2,128]{2,1,0:T(2,128)S(1)}, f32[4,2,128]{2,1,0:T(2,128)S(1)}, u32[]{:S(2)}, u32[]{:S(2)}) collective-permute-start(f32[4,2,128]{2,1,0:T(2,128)S(1)} %get-tuple-element.72), channel_id=1, source_target_pairs={{0,8},{8,16},{16,24},{24,0},{1,9},{9,17},{17,25},{25,1},{2,10},{10... | collective-permute-start | bytes 12296 | tf_op jit(solution)/shard_map/ppermute | solution.py:463
  17.3 0.5 %collective-permute-start.5 = (f32[4,2,128]{2,1,0:T(2,128)S(1)}, f32[4,2,128]{2,1,0:T(2,128)S(1)}, u32[]{:S(2)}, u32[]{:S(2)}) collective-permute-start(f32[4,2,128]{2,1,0:T(2,128)S(1)} %get-tuple-element.73), channel_id=1, source_target_pairs={{8,0},{16,8},{24,16},{0,24},{9,1},{17,9},{25,17},{1,25},{10,2},{18... | collective-permute-start | bytes 12296 | tf_op jit(solution)/shard_map/ppermute | solution.py:464
  17.8 0.2 shard_map.81
  18.0 1.5 %collective-permute-start.10 = (f32[4,10240]{1,0:T(4,128)S(1)}, f32[4,10240]{1,0:T(4,128)S(1)}, u32[]{:S(2)}, u32[]{:S(2)}) collective-permute-start(f32[4,10240]{1,0:T(4,128)S(1)} %get-tuple-element.48), channel_id=1, source_target_pairs={{0,8},{8,16},{16,24},{24,0},{1,9},{9,17},{17,25},{25,1},{2,10},{10... | collective-permute-start | bytes 491528 | tf_op jit(solution)/shard_map/ppermute | solution.py:463
  19.6 1.4 %collective-permute-start.11 = (f32[4,10240]{1,0:T(4,128)S(1)}, f32[4,10240]{1,0:T(4,128)S(1)}, u32[]{:S(2)}, u32[]{:S(2)}) collective-permute-start(f32[4,10240]{1,0:T(4,128)S(1)} %get-tuple-element.49), channel_id=1, source_target_pairs={{8,0},{16,8},{24,16},{0,24},{9,1},{17,9},{25,17},{1,25},{10,2},{18... | collective-permute-start | bytes 491528 | tf_op jit(solution)/shard_map/ppermute | solution.py:464
  21.0 0.0 collective-permute-done.4
  21.0 0.0 collective-permute-done.5
  21.1 0.7 %collective-permute-start.7 = (f32[3,12,128]{2,1,0:T(8,128)S(1)}, f32[3,12,128]{2,1,0:T(8,128)S(1)}, u32[]{:S(2)}, u32[]{:S(2)}) collective-permute-start(f32[3,12,128]{2,1,0:T(8,128)S(1)} %get-tuple-element.70), channel_id=1, source_target_pairs={{0,7},{1,2},{2,1},{3,4},{4,3},{5,6},{6,5},{7,0},{8,15},{9,10},{10,... | collective-permute-start | bytes 55304 | tf_op jit(solution)/shard_map/ppermute | solution.py:460
  21.8 0.0 collective-permute-start.6
  21.8 2.9 %collective-permute-start.9 = (f32[3,28,128]{2,1,0:T(8,128)S(1)}, f32[3,28,128]{2,1,0:T(8,128)S(1)}, u32[]{:S(2)}, u32[]{:S(2)}) collective-permute-start(f32[3,28,128]{2,1,0:T(8,128)S(1)} %get-tuple-element.62), channel_id=1, source_target_pairs={{0,7},{1,2},{2,1},{3,4},{4,3},{5,6},{6,5},{7,0},{8,15},{9,10},{10,... | collective-permute-start | bytes 129032 | tf_op jit(solution)/shard_map/ppermute | solution.py:460
  24.7 1.5 %collective-permute-done.7 = f32[3,12,128]{2,1,0:T(8,128)S(1)} collective-permute-done((f32[3,12,128]{2,1,0:T(8,128)S(1)}, f32[3,12,128]{2,1,0:T(8,128)S(1)}, u32[]{:S(2)}, u32[]{:S(2)}) %collective-permute-start.7) | collective-permute-done | bytes 18464 | tf_op jit(solution)/shard_map/ppermute | solution.py:460
  26.3 0.0 collective-permute-start.8
  26.3 0.0 collective-permute-done.6
  26.3 1.4 %collective-permute-done.9 = f32[3,28,128]{2,1,0:T(8,128)S(1)} collective-permute-done((f32[3,28,128]{2,1,0:T(8,128)S(1)}, f32[3,28,128]{2,1,0:T(8,128)S(1)}, u32[]{:S(2)}, u32[]{:S(2)}) %collective-permute-start.9) | collective-permute-done | bytes 43040 | tf_op jit(solution)/shard_map/ppermute | solution.py:460
  27.7 0.0 collective-permute-done.8
  27.7 0.0 collective-permute-done.10.refs_0_
  27.7 0.0 collective-permute-done.11.refs_1_
  27.7 0.1 shard_map.82
  27.9 1.4 %shard_map.83 = (f32[32,128]{1,0:T(8,128)S(1)}, f32[32,128]{1,0:T(8,128)S(1)}, f32[4,10,128]{2,1,0:T(8,128)S(1)}) custom-call(f32[4,12,128]{2,1,0:T(8,128)S(1)} %pad_maximum_fusion.mid_ref, f32[3,12,128]{2,1,0:T(8,128)S(1)} %get-tuple-element.67.left_ref, f32[3,12,128]{2,1,0:T(8,128)S(1)} %get-tuple-element.66.right_ref, ...), custom_call_target="tpu_custom_call" | custom-call | tf_op jit(solution)/shard_map/pallas_call | solution.py:31
  29.3 2.4 %collective-permute-start.13 = (f32[3,10,128]{2,1,0:T(8,128)S(1)}, f32[3,10,128]{2,1,0:T(8,128)S(1)}, u32[]{:S(2)}, u32[]{:S(2)}) collective-permute-start(f32[3,10,128]{2,1,0:T(8,128)S(1)} %get-tuple-element.68), channel_id=1, source_target_pairs={{0,7},{1,2},{2,1},{3,4},{4,3},{5,6},{6,5},{7,0},{8,15},{9,10},{10,... | collective-permute-start | bytes 46088 | tf_op jit(solution)/shard_map/ppermute | solution.py:460
  31.8 0.0 collective-permute-start.12
  31.8 2.7 %collective-permute-done.13 = f32[3,10,128]{2,1,0:T(8,128)S(1)} collective-permute-done((f32[3,10,128]{2,1,0:T(8,128)S(1)}, f32[3,10,128]{2,1,0:T(8,128)S(1)}, u32[]{:S(2)}, u32[]{:S(2)}) %collective-permute-start.13) | collective-permute-done | bytes 15392 | tf_op jit(solution)/shard_map/ppermute | solution.py:460
  34.4 0.0 collective-permute-done.12
  34.5 0.2 shard_map.84
  34.7 10.6 %all_to_all.5 = f32[32,1,128]{2,1,0:T(1,128)S(1)} all-to-all(f32[32,1,128]{2,1,0:T(1,128)S(1)} %bitcast.17), channel_id=1, replica_groups=mesh['lat'=4,'lon'=8] {'lat','lon'}, dimensions={0} | all-to-all | bytes 32768 | tf_op jit(solution)/shard_map/all_to_all | solution.py:546
  45.4 1.4 %shard_map.85 = (f32[2,2]{1,0:T(2,128)}, bf16[32,5120]{1,0:T(8,128)(2,1)}) custom-call(f32[32,128]{1,0:T(8,128)S(1)} %bitcast.16, f32[32,128]{1,0:T(8,128)S(1)} %get-tuple-element.53.y0_ref, f32[32,128]{1,0:T(8,128)S(1)} %get-tuple-element.54.y1_ref, f32[32,128]{1,0:T(8,128)S(1)} %get-tuple-element.57.y2_ref, f32[40,32,128]{2,1,0:T(8,128)S(1)} %get-tuple-element.39.one_ref, ...), custom_call_target="tpu_custom_call" | custom-call | tf_op jit(solution)/shard_map/pallas_call | solution.py:31
  (11 shorter events, 0.1 us)
Async XLA Ops:
  0.6 10.1 %copy-start = (bf16[4,8,10240]{2,1,0:T(8,128)(2,1)S(1)}, bf16[4,8,10240]{2,1,0:T(8,128)(2,1)}, u32[]{:S(2)}) copy-start(bf16[4,8,10240]{2,1,0:T(8,128)(2,1)} %param.6) | copy-start | bytes 1966084
  1.8 6.0 %collective-permute-start = (f32[76,128]{1,0:T(8,128)S(1)}, f32[76,128]{1,0:T(8,128)S(1)}, u32[]{:S(2)}, u32[]{:S(2)}) collective-permute-start(f32[76,128]{1,0:T(8,128)S(1)} %get-tuple-element.31), channel_id=1, source_target_pairs={{0,8},{8,16},{16,24},{24,0},{1,9},{9,17},{17,25},{25,1},{2,10},{10... | collective-permute-start | bytes 116744 | tf_op jit(solution)/shard_map/ppermute | solution.py:463
  4.8 4.0 %collective-permute-start.1 = (f32[76,128]{1,0:T(8,128)S(1)}, f32[76,128]{1,0:T(8,128)S(1)}, u32[]{:S(2)}, u32[]{:S(2)}) collective-permute-start(f32[76,128]{1,0:T(8,128)S(1)} %get-tuple-element.32), channel_id=1, source_target_pairs={{8,0},{16,8},{24,16},{0,24},{9,1},{17,9},{25,17},{1,25},{10,2},{18... | collective-permute-start | bytes 116744 | tf_op jit(solution)/shard_map/ppermute | solution.py:464
  8.9 4.9 %collective-permute-start.3 = (f32[16,128]{1,0:T(8,128)S(1)}, f32[16,128]{1,0:T(8,128)S(1)}, u32[]{:S(2)}, u32[]{:S(2)}) collective-permute-start(f32[16,128]{1,0:T(8,128)S(1)} %get-tuple-element.76), channel_id=1, source_target_pairs={{0,7},{1,2},{2,1},{3,4},{4,3},{5,6},{6,5},{7,0},{8,15},{9,10},{10,... | collective-permute-start | bytes 24584 | tf_op jit(solution)/shard_map/ppermute | solution.py:460
  10.8 3.1 %collective-permute-start.2 = (f32[16,128]{1,0:T(8,128)S(1)}, f32[16,128]{1,0:T(8,128)S(1)}, u32[]{:S(2)}, u32[]{:S(2)}) collective-permute-start(f32[16,128]{1,0:T(8,128)S(1)} %get-tuple-element.77), channel_id=1, source_target_pairs={{0,1},{1,0},{2,3},{3,2},{4,5},{5,4},{6,7},{7,6},{8,9},{9,8},{10,11... | collective-permute-start | bytes 24584 | tf_op jit(solution)/shard_map/ppermute | solution.py:461
  14.8 6.2 %collective-permute-start.4 = (f32[4,2,128]{2,1,0:T(2,128)S(1)}, f32[4,2,128]{2,1,0:T(2,128)S(1)}, u32[]{:S(2)}, u32[]{:S(2)}) collective-permute-start(f32[4,2,128]{2,1,0:T(2,128)S(1)} %get-tuple-element.72), channel_id=1, source_target_pairs={{0,8},{8,16},{16,24},{24,0},{1,9},{9,17},{17,25},{25,1},{2,10},{10... | collective-permute-start | bytes 12296 | tf_op jit(solution)/shard_map/ppermute | solution.py:463
  17.3 3.7 %collective-permute-start.5 = (f32[4,2,128]{2,1,0:T(2,128)S(1)}, f32[4,2,128]{2,1,0:T(2,128)S(1)}, u32[]{:S(2)}, u32[]{:S(2)}) collective-permute-start(f32[4,2,128]{2,1,0:T(2,128)S(1)} %get-tuple-element.73), channel_id=1, source_target_pairs={{8,0},{16,8},{24,16},{0,24},{9,1},{17,9},{25,17},{1,25},{10,2},{18... | collective-permute-start | bytes 12296 | tf_op jit(solution)/shard_map/ppermute | solution.py:464
  18.0 9.7 %collective-permute-start.10 = (f32[4,10240]{1,0:T(4,128)S(1)}, f32[4,10240]{1,0:T(4,128)S(1)}, u32[]{:S(2)}, u32[]{:S(2)}) collective-permute-start(f32[4,10240]{1,0:T(4,128)S(1)} %get-tuple-element.48), channel_id=1, source_target_pairs={{0,8},{8,16},{16,24},{24,0},{1,9},{9,17},{17,25},{25,1},{2,10},{10... | collective-permute-start | bytes 491528 | tf_op jit(solution)/shard_map/ppermute | solution.py:463
  19.6 8.1 %collective-permute-start.11 = (f32[4,10240]{1,0:T(4,128)S(1)}, f32[4,10240]{1,0:T(4,128)S(1)}, u32[]{:S(2)}, u32[]{:S(2)}) collective-permute-start(f32[4,10240]{1,0:T(4,128)S(1)} %get-tuple-element.49), channel_id=1, source_target_pairs={{8,0},{16,8},{24,16},{0,24},{9,1},{17,9},{25,17},{1,25},{10,2},{18... | collective-permute-start | bytes 491528 | tf_op jit(solution)/shard_map/ppermute | solution.py:464
  21.1 5.2 %collective-permute-start.7 = (f32[3,12,128]{2,1,0:T(8,128)S(1)}, f32[3,12,128]{2,1,0:T(8,128)S(1)}, u32[]{:S(2)}, u32[]{:S(2)}) collective-permute-start(f32[3,12,128]{2,1,0:T(8,128)S(1)} %get-tuple-element.70), channel_id=1, source_target_pairs={{0,7},{1,2},{2,1},{3,4},{4,3},{5,6},{6,5},{7,0},{8,15},{9,10},{10,... | collective-permute-start | bytes 55304 | tf_op jit(solution)/shard_map/ppermute | solution.py:460
  21.8 4.5 %collective-permute-start.6 = (f32[3,12,128]{2,1,0:T(8,128)S(1)}, f32[3,12,128]{2,1,0:T(8,128)S(1)}, u32[]{:S(2)}, u32[]{:S(2)}) collective-permute-start(f32[3,12,128]{2,1,0:T(8,128)S(1)} %get-tuple-element.71), channel_id=1, source_target_pairs={{0,1},{1,0},{2,3},{3,2},{4,5},{5,4},{6,7},{7,6},{8,9},{9,8},{10,11... | collective-permute-start | bytes 55304 | tf_op jit(solution)/shard_map/ppermute | solution.py:461
  21.8 5.9 %collective-permute-start.9 = (f32[3,28,128]{2,1,0:T(8,128)S(1)}, f32[3,28,128]{2,1,0:T(8,128)S(1)}, u32[]{:S(2)}, u32[]{:S(2)}) collective-permute-start(f32[3,28,128]{2,1,0:T(8,128)S(1)} %get-tuple-element.62), channel_id=1, source_target_pairs={{0,7},{1,2},{2,1},{3,4},{4,3},{5,6},{6,5},{7,0},{8,15},{9,10},{10,... | collective-permute-start | bytes 129032 | tf_op jit(solution)/shard_map/ppermute | solution.py:460
  26.3 1.4 %collective-permute-start.8 = (f32[3,28,128]{2,1,0:T(8,128)S(1)}, f32[3,28,128]{2,1,0:T(8,128)S(1)}, u32[]{:S(2)}, u32[]{:S(2)}) collective-permute-start(f32[3,28,128]{2,1,0:T(8,128)S(1)} %get-tuple-element.63), channel_id=1, source_target_pairs={{0,1},{1,0},{2,3},{3,2},{4,5},{5,4},{6,7},{7,6},{8,9},{9,8},{10,11... | collective-permute-start | bytes 129032 | tf_op jit(solution)/shard_map/ppermute | solution.py:461
  29.3 5.1 %collective-permute-start.13 = (f32[3,10,128]{2,1,0:T(8,128)S(1)}, f32[3,10,128]{2,1,0:T(8,128)S(1)}, u32[]{:S(2)}, u32[]{:S(2)}) collective-permute-start(f32[3,10,128]{2,1,0:T(8,128)S(1)} %get-tuple-element.68), channel_id=1, source_target_pairs={{0,7},{1,2},{2,1},{3,4},{4,3},{5,6},{6,5},{7,0},{8,15},{9,10},{10,... | collective-permute-start | bytes 46088 | tf_op jit(solution)/shard_map/ppermute | solution.py:460
  31.8 2.7 %collective-permute-start.12 = (f32[3,10,128]{2,1,0:T(8,128)S(1)}, f32[3,10,128]{2,1,0:T(8,128)S(1)}, u32[]{:S(2)}, u32[]{:S(2)}) collective-permute-start(f32[3,10,128]{2,1,0:T(8,128)S(1)} %get-tuple-element.69), channel_id=1, source_target_pairs={{0,1},{1,0},{2,3},{3,2},{4,5},{5,4},{6,7},{7,6},{8,9},{9,8},{10,11... | collective-permute-start | bytes 46088 | tf_op jit(solution)/shard_map/ppermute | solution.py:461

commit v9 on v8

--- a/solution.py
+++ b/solution.py
@@ -419,16 +419,19 @@
         square0 = m00 / entries + EPSILON
         inverse0 = 1.0 / square0
         alpha0 = ((m00 + m01) / entries) * inverse0
-        g = 1.0 - alpha0
+        shift = entries * EPSILON
+        g = ((shift - m01) / entries) * inverse0
         u1u1 = (g * (g * m00 + 2.0 * m01) + m11) * inverse0
         u1lu1 = (g * (g * m01 + 2.0 * m11) + m12) * inverse0
         cross = ((g * (m00 + m01) + m01 + m11) / entries) * inverse0
         square1 = u1u1 / entries + EPSILON
-        alpha1 = ((u1u1 + u1lu1) / entries) / square1
+        inverse1 = 1.0 / square1
+        alpha1 = ((u1u1 + u1lu1) / entries) * inverse1
+        h = ((shift - u1lu1) / entries) * inverse1
         beta0, beta1 = jnp.sqrt(square0), jnp.sqrt(square1)
         k2 = lax.rsqrt(square0) * lax.rsqrt(square1)
-        k1 = k2 * (1.0 - alpha1 + g)
-        k0 = k2 * ((1.0 - alpha1) * g - cross)
+        k1 = k2 * (h + g)
+        k0 = k2 * (h * g - cross)
         row = lax.broadcasted_iota(jnp.int32, (2, 2), 0)
         col = lax.broadcasted_iota(jnp.int32, (2, 2), 1)
         coef_ref[...] = jnp.where(

time: 46.9 us -> 46.9 us (level)
  no operation moved by 1% of the time
where the time goes in v9:
time: 46.9 us; the launch traced here: 46.7 us
  starting transfers between devices  18 us (38%)
  waiting for transfers between devices  11.3 us (24%)
  blocking collectives  10.6 us (23%)
  Pallas kernels  5.8 us (12%)
  between operations  0.76 us (2%)
    all_to_all x1, blocking collectives, per_device(): lax.all_to_all(dots.reshape(devices, 1, CH), ('lat', 'lon'), 0, 0)  10.6 us
    ppermute x4, waiting for transfers between devices, from_neighbours(): far = lax.ppermute(jnp.where(odd, up, down), axis, outer)  8.42 us
    ppermute x4, starting transfers between devices, from_neighbours(): far = lax.ppermute(jnp.where(odd, up, down), axis, outer)  7.96 us
    ppermute x3, starting transfers between devices, from_neighbours(): lax.ppermute(up, axis, [(at, (at + 1) % count) for at in range(count)])  7 us
    pallas_call x8, Pallas kernels, kernel_call(): pl.pallas_call(body, out_shape=outs, in_specs=[VMEM_SPEC] * len(operands)...  4.7 us
    ppermute x3, starting transfers between devices, from_neighbours(): lax.ppermute(down, axis, [((at + 1) % count, at) for at in range(count)])  2.99 us
    ppermute x3, waiting for transfers between devices, from_neighbours(): lax.ppermute(up, axis, [(at, (at + 1) % count) for at in range(count)])  1.84 us
    pallas_call x1, Pallas kernels, per_device(): pl.pallas_call(prepare_kernel(cols, rows), out_shape=(message, message, p...  1.1 us
  transfers between devices with their start and end apart: 14, of which 6 were waited for; matrix products, arithmetic and copies ran while one was open for 0% of the time, Pallas kernels for 1%

profile of v9, /device:TPU:0, one launch (start us, length us, event | category | flops | bytes accessed | tf_op | source)
XLA Modules:
  0.0 46.7 jit_solution(17499930682817640457)
XLA Ops:
  0.6 0.0 copy-start
  0.6 1.1 %shard_map.77 = (f32[76,128]{1,0:T(8,128)S(1)}, f32[76,128]{1,0:T(8,128)S(1)}, f32[8,8,128]{2,1,0:T(8,128)S(1)}, f32[8,16,128]{2,1,0:T(8,128)S(1)}, f32[32,128]{...) custom-call(f32[8,16,128]{2,1,0:T(8,128)} %weight_ref.1, f32[8,16,128]{2,1,0:T(8,128)} %innovation_ref.1, ...), custom_call_target="tpu_custom_call" | custom-call | flops 536870912 | bytes 2097152 | tf_op jit(solution)/shard_map/pallas_call | solution.py:487
  1.8 3.0 %collective-permute-start = (f32[76,128]{1,0:T(8,128)S(1)}, f32[76,128]{1,0:T(8,128)S(1)}, u32[]{:S(2)}, u32[]{:S(2)}) collective-permute-start(f32[76,128]{1,0:T(8,128)S(1)} %get-tuple-element.31), channel_id=1, source_target_pairs={{0,8},{8,16},{16,24},{24,0},{1,9},{9,17},{17,25},{25,1},{2,10},{10... | collective-permute-start | bytes 116744 | tf_op jit(solution)/shard_map/ppermute | solution.py:466
  4.8 1.0 %collective-permute-start.1 = (f32[76,128]{1,0:T(8,128)S(1)}, f32[76,128]{1,0:T(8,128)S(1)}, u32[]{:S(2)}, u32[]{:S(2)}) collective-permute-start(f32[76,128]{1,0:T(8,128)S(1)} %get-tuple-element.32), channel_id=1, source_target_pairs={{8,0},{16,8},{24,16},{0,24},{9,1},{17,9},{25,17},{1,25},{10,2},{18... | collective-permute-start | bytes 116744 | tf_op jit(solution)/shard_map/ppermute | solution.py:467
  5.8 0.1 add_convert_fusion
  5.9 1.8 %collective-permute-done.low_ref = f32[76,128]{1,0:T(8,128)S(1)} collective-permute-done((f32[76,128]{1,0:T(8,128)S(1)}, f32[76,128]{1,0:T(8,128)S(1)}, u32[]{:S(2)}, u32[]{:S(2)}) %collective-permute-start) | collective-permute-done | bytes 38944 | tf_op jit(solution)/shard_map/ppermute | solution.py:466
  7.7 1.1 %collective-permute-done.1.high_ref = f32[76,128]{1,0:T(8,128)S(1)} collective-permute-done((f32[76,128]{1,0:T(8,128)S(1)}, f32[76,128]{1,0:T(8,128)S(1)}, u32[]{:S(2)}, u32[]{:S(2)}) %collective-permute-start.1) | collective-permute-done | bytes 38944 | tf_op jit(solution)/shard_map/ppermute | solution.py:467
  8.8 0.1 broadcast_in_dim.18.flags_ref
  8.9 1.9 %collective-permute-start.3 = (f32[16,128]{1,0:T(8,128)S(1)}, f32[16,128]{1,0:T(8,128)S(1)}, u32[]{:S(2)}, u32[]{:S(2)}) collective-permute-start(f32[16,128]{1,0:T(8,128)S(1)} %get-tuple-element.76), channel_id=1, source_target_pairs={{0,7},{1,2},{2,1},{3,4},{4,3},{5,6},{6,5},{7,0},{8,15},{9,10},{10,... | collective-permute-start | bytes 24584 | tf_op jit(solution)/shard_map/ppermute | solution.py:463
  10.8 0.0 collective-permute-start.2
  10.8 0.0 copy-done
  10.8 0.3 shard_map.79
  11.0 2.8 %collective-permute-done.3 = f32[16,128]{1,0:T(8,128)S(1)} collective-permute-done((f32[16,128]{1,0:T(8,128)S(1)}, f32[16,128]{1,0:T(8,128)S(1)}, u32[]{:S(2)}, u32[]{:S(2)}) %collective-permute-start.3) | collective-permute-done | bytes 8224 | tf_op jit(solution)/shard_map/ppermute | solution.py:463
  13.8 0.0 collective-permute-done.2
  13.8 1.0 %shard_map.80 = (f32[32,128]{1,0:T(8,128)S(1)}, f32[32,128]{1,0:T(8,128)S(1)}) custom-call(f32[32,128]{1,0:T(8,128)S(1)} %get-tuple-element.36.own_ref, f32[16,128]{1,0:T(8,128)S(1)} %get-tuple-element.75.left_ref, f32[16,128]{1,0:T(8,128)S(1)} %get-tuple-element.74.right_ref, f32[40,32,128]{2,1,0:T(8,128)S(1)} %get-tuple-element.39.one_ref, ...), custom_call_target="tpu_custom_call" | custom-call | tf_op jit(solution)/shard_map/pallas_call | solution.py:31
  14.8 2.4 %collective-permute-start.4 = (f32[4,2,128]{2,1,0:T(2,128)S(1)}, f32[4,2,128]{2,1,0:T(2,128)S(1)}, u32[]{:S(2)}, u32[]{:S(2)}) collective-permute-start(f32[4,2,128]{2,1,0:T(2,128)S(1)} %get-tuple-element.72), channel_id=1, source_target_pairs={{0,8},{8,16},{16,24},{24,0},{1,9},{9,17},{17,25},{25,1},{2,10},{10... | collective-permute-start | bytes 12296 | tf_op jit(solution)/shard_map/ppermute | solution.py:466
  17.3 0.5 %collective-permute-start.5 = (f32[4,2,128]{2,1,0:T(2,128)S(1)}, f32[4,2,128]{2,1,0:T(2,128)S(1)}, u32[]{:S(2)}, u32[]{:S(2)}) collective-permute-start(f32[4,2,128]{2,1,0:T(2,128)S(1)} %get-tuple-element.73), channel_id=1, source_target_pairs={{8,0},{16,8},{24,16},{0,24},{9,1},{17,9},{25,17},{1,25},{10,2},{18... | collective-permute-start | bytes 12296 | tf_op jit(solution)/shard_map/ppermute | solution.py:467
  17.8 0.2 shard_map.81
  18.0 1.5 %collective-permute-start.10 = (f32[4,10240]{1,0:T(4,128)S(1)}, f32[4,10240]{1,0:T(4,128)S(1)}, u32[]{:S(2)}, u32[]{:S(2)}) collective-permute-start(f32[4,10240]{1,0:T(4,128)S(1)} %get-tuple-element.48), channel_id=1, source_target_pairs={{0,8},{8,16},{16,24},{24,0},{1,9},{9,17},{17,25},{25,1},{2,10},{10... | collective-permute-start | bytes 491528 | tf_op jit(solution)/shard_map/ppermute | solution.py:466
  19.6 1.4 %collective-permute-start.11 = (f32[4,10240]{1,0:T(4,128)S(1)}, f32[4,10240]{1,0:T(4,128)S(1)}, u32[]{:S(2)}, u32[]{:S(2)}) collective-permute-start(f32[4,10240]{1,0:T(4,128)S(1)} %get-tuple-element.49), channel_id=1, source_target_pairs={{8,0},{16,8},{24,16},{0,24},{9,1},{17,9},{25,17},{1,25},{10,2},{18... | collective-permute-start | bytes 491528 | tf_op jit(solution)/shard_map/ppermute | solution.py:467
  21.0 0.0 collective-permute-done.4
  21.0 0.0 collective-permute-done.5
  21.1 0.7 %collective-permute-start.7 = (f32[3,12,128]{2,1,0:T(8,128)S(1)}, f32[3,12,128]{2,1,0:T(8,128)S(1)}, u32[]{:S(2)}, u32[]{:S(2)}) collective-permute-start(f32[3,12,128]{2,1,0:T(8,128)S(1)} %get-tuple-element.70), channel_id=1, source_target_pairs={{0,7},{1,2},{2,1},{3,4},{4,3},{5,6},{6,5},{7,0},{8,15},{9,10},{10,... | collective-permute-start | bytes 55304 | tf_op jit(solution)/shard_map/ppermute | solution.py:463
  21.8 0.0 collective-permute-start.6
  21.8 2.9 %collective-permute-start.9 = (f32[3,28,128]{2,1,0:T(8,128)S(1)}, f32[3,28,128]{2,1,0:T(8,128)S(1)}, u32[]{:S(2)}, u32[]{:S(2)}) collective-permute-start(f32[3,28,128]{2,1,0:T(8,128)S(1)} %get-tuple-element.62), channel_id=1, source_target_pairs={{0,7},{1,2},{2,1},{3,4},{4,3},{5,6},{6,5},{7,0},{8,15},{9,10},{10,... | collective-permute-start | bytes 129032 | tf_op jit(solution)/shard_map/ppermute | solution.py:463
  24.7 1.5 %collective-permute-done.7 = f32[3,12,128]{2,1,0:T(8,128)S(1)} collective-permute-done((f32[3,12,128]{2,1,0:T(8,128)S(1)}, f32[3,12,128]{2,1,0:T(8,128)S(1)}, u32[]{:S(2)}, u32[]{:S(2)}) %collective-permute-start.7) | collective-permute-done | bytes 18464 | tf_op jit(solution)/shard_map/ppermute | solution.py:463
  26.3 0.0 collective-permute-start.8
  26.3 0.0 collective-permute-done.6
  26.3 1.4 %collective-permute-done.9 = f32[3,28,128]{2,1,0:T(8,128)S(1)} collective-permute-done((f32[3,28,128]{2,1,0:T(8,128)S(1)}, f32[3,28,128]{2,1,0:T(8,128)S(1)}, u32[]{:S(2)}, u32[]{:S(2)}) %collective-permute-start.9) | collective-permute-done | bytes 43040 | tf_op jit(solution)/shard_map/ppermute | solution.py:463
  27.7 0.0 collective-permute-done.8
  27.7 0.0 collective-permute-done.10.refs_0_
  27.7 0.0 collective-permute-done.11.refs_1_
  27.7 0.1 shard_map.82
  27.9 1.4 %shard_map.83 = (f32[32,128]{1,0:T(8,128)S(1)}, f32[32,128]{1,0:T(8,128)S(1)}, f32[4,10,128]{2,1,0:T(8,128)S(1)}) custom-call(f32[4,12,128]{2,1,0:T(8,128)S(1)} %pad_maximum_fusion.mid_ref, f32[3,12,128]{2,1,0:T(8,128)S(1)} %get-tuple-element.67.left_ref, f32[3,12,128]{2,1,0:T(8,128)S(1)} %get-tuple-element.66.right_ref, ...), custom_call_target="tpu_custom_call" | custom-call | tf_op jit(solution)/shard_map/pallas_call | solution.py:31
  29.3 2.4 %collective-permute-start.13 = (f32[3,10,128]{2,1,0:T(8,128)S(1)}, f32[3,10,128]{2,1,0:T(8,128)S(1)}, u32[]{:S(2)}, u32[]{:S(2)}) collective-permute-start(f32[3,10,128]{2,1,0:T(8,128)S(1)} %get-tuple-element.68), channel_id=1, source_target_pairs={{0,7},{1,2},{2,1},{3,4},{4,3},{5,6},{6,5},{7,0},{8,15},{9,10},{10,... | collective-permute-start | bytes 46088 | tf_op jit(solution)/shard_map/ppermute | solution.py:463
  31.8 0.0 collective-permute-start.12
  31.8 2.7 %collective-permute-done.13 = f32[3,10,128]{2,1,0:T(8,128)S(1)} collective-permute-done((f32[3,10,128]{2,1,0:T(8,128)S(1)}, f32[3,10,128]{2,1,0:T(8,128)S(1)}, u32[]{:S(2)}, u32[]{:S(2)}) %collective-permute-start.13) | collective-permute-done | bytes 15392 | tf_op jit(solution)/shard_map/ppermute | solution.py:463
  34.4 0.0 collective-permute-done.12
  34.5 0.2 shard_map.84
  34.7 10.6 %all_to_all.5 = f32[32,1,128]{2,1,0:T(1,128)S(1)} all-to-all(f32[32,1,128]{2,1,0:T(1,128)S(1)} %bitcast.17), channel_id=1, replica_groups=mesh['lat'=4,'lon'=8] {'lat','lon'}, dimensions={0} | all-to-all | bytes 32768 | tf_op jit(solution)/shard_map/all_to_all | solution.py:549
  45.4 1.4 %shard_map.85 = (f32[2,2]{1,0:T(2,128)}, bf16[32,5120]{1,0:T(8,128)(2,1)}) custom-call(f32[32,128]{1,0:T(8,128)S(1)} %bitcast.16, f32[32,128]{1,0:T(8,128)S(1)} %get-tuple-element.53.y0_ref, f32[32,128]{1,0:T(8,128)S(1)} %get-tuple-element.54.y1_ref, f32[32,128]{1,0:T(8,128)S(1)} %get-tuple-element.57.y2_ref, f32[40,32,128]{2,1,0:T(8,128)S(1)} %get-tuple-element.39.one_ref, ...), custom_call_target="tpu_custom_call" | custom-call | tf_op jit(solution)/shard_map/pallas_call | solution.py:31
  (11 shorter events, 0.1 us)
Async XLA Ops:
  0.6 10.1 %copy-start = (bf16[4,8,10240]{2,1,0:T(8,128)(2,1)S(1)}, bf16[4,8,10240]{2,1,0:T(8,128)(2,1)}, u32[]{:S(2)}) copy-start(bf16[4,8,10240]{2,1,0:T(8,128)(2,1)} %param.6) | copy-start | bytes 1966084
  1.8 6.0 %collective-permute-start = (f32[76,128]{1,0:T(8,128)S(1)}, f32[76,128]{1,0:T(8,128)S(1)}, u32[]{:S(2)}, u32[]{:S(2)}) collective-permute-start(f32[76,128]{1,0:T(8,128)S(1)} %get-tuple-element.31), channel_id=1, source_target_pairs={{0,8},{8,16},{16,24},{24,0},{1,9},{9,17},{17,25},{25,1},{2,10},{10... | collective-permute-start | bytes 116744 | tf_op jit(solution)/shard_map/ppermute | solution.py:466
  4.8 4.0 %collective-permute-start.1 = (f32[76,128]{1,0:T(8,128)S(1)}, f32[76,128]{1,0:T(8,128)S(1)}, u32[]{:S(2)}, u32[]{:S(2)}) collective-permute-start(f32[76,128]{1,0:T(8,128)S(1)} %get-tuple-element.32), channel_id=1, source_target_pairs={{8,0},{16,8},{24,16},{0,24},{9,1},{17,9},{25,17},{1,25},{10,2},{18... | collective-permute-start | bytes 116744 | tf_op jit(solution)/shard_map/ppermute | solution.py:467
  8.9 4.9 %collective-permute-start.3 = (f32[16,128]{1,0:T(8,128)S(1)}, f32[16,128]{1,0:T(8,128)S(1)}, u32[]{:S(2)}, u32[]{:S(2)}) collective-permute-start(f32[16,128]{1,0:T(8,128)S(1)} %get-tuple-element.76), channel_id=1, source_target_pairs={{0,7},{1,2},{2,1},{3,4},{4,3},{5,6},{6,5},{7,0},{8,15},{9,10},{10,... | collective-permute-start | bytes 24584 | tf_op jit(solution)/shard_map/ppermute | solution.py:463
  10.8 3.1 %collective-permute-start.2 = (f32[16,128]{1,0:T(8,128)S(1)}, f32[16,128]{1,0:T(8,128)S(1)}, u32[]{:S(2)}, u32[]{:S(2)}) collective-permute-start(f32[16,128]{1,0:T(8,128)S(1)} %get-tuple-element.77), channel_id=1, source_target_pairs={{0,1},{1,0},{2,3},{3,2},{4,5},{5,4},{6,7},{7,6},{8,9},{9,8},{10,11... | collective-permute-start | bytes 24584 | tf_op jit(solution)/shard_map/ppermute | solution.py:464
  14.8 6.2 %collective-permute-start.4 = (f32[4,2,128]{2,1,0:T(2,128)S(1)}, f32[4,2,128]{2,1,0:T(2,128)S(1)}, u32[]{:S(2)}, u32[]{:S(2)}) collective-permute-start(f32[4,2,128]{2,1,0:T(2,128)S(1)} %get-tuple-element.72), channel_id=1, source_target_pairs={{0,8},{8,16},{16,24},{24,0},{1,9},{9,17},{17,25},{25,1},{2,10},{10... | collective-permute-start | bytes 12296 | tf_op jit(solution)/shard_map/ppermute | solution.py:466
  17.3 3.7 %collective-permute-start.5 = (f32[4,2,128]{2,1,0:T(2,128)S(1)}, f32[4,2,128]{2,1,0:T(2,128)S(1)}, u32[]{:S(2)}, u32[]{:S(2)}) collective-permute-start(f32[4,2,128]{2,1,0:T(2,128)S(1)} %get-tuple-element.73), channel_id=1, source_target_pairs={{8,0},{16,8},{24,16},{0,24},{9,1},{17,9},{25,17},{1,25},{10,2},{18... | collective-permute-start | bytes 12296 | tf_op jit(solution)/shard_map/ppermute | solution.py:467
  18.0 9.7 %collective-permute-start.10 = (f32[4,10240]{1,0:T(4,128)S(1)}, f32[4,10240]{1,0:T(4,128)S(1)}, u32[]{:S(2)}, u32[]{:S(2)}) collective-permute-start(f32[4,10240]{1,0:T(4,128)S(1)} %get-tuple-element.48), channel_id=1, source_target_pairs={{0,8},{8,16},{16,24},{24,0},{1,9},{9,17},{17,25},{25,1},{2,10},{10... | collective-permute-start | bytes 491528 | tf_op jit(solution)/shard_map/ppermute | solution.py:466
  19.6 8.1 %collective-permute-start.11 = (f32[4,10240]{1,0:T(4,128)S(1)}, f32[4,10240]{1,0:T(4,128)S(1)}, u32[]{:S(2)}, u32[]{:S(2)}) collective-permute-start(f32[4,10240]{1,0:T(4,128)S(1)} %get-tuple-element.49), channel_id=1, source_target_pairs={{8,0},{16,8},{24,16},{0,24},{9,1},{17,9},{25,17},{1,25},{10,2},{18... | collective-permute-start | bytes 491528 | tf_op jit(solution)/shard_map/ppermute | solution.py:467
  21.1 5.2 %collective-permute-start.7 = (f32[3,12,128]{2,1,0:T(8,128)S(1)}, f32[3,12,128]{2,1,0:T(8,128)S(1)}, u32[]{:S(2)}, u32[]{:S(2)}) collective-permute-start(f32[3,12,128]{2,1,0:T(8,128)S(1)} %get-tuple-element.70), channel_id=1, source_target_pairs={{0,7},{1,2},{2,1},{3,4},{4,3},{5,6},{6,5},{7,0},{8,15},{9,10},{10,... | collective-permute-start | bytes 55304 | tf_op jit(solution)/shard_map/ppermute | solution.py:463
  21.8 4.5 %collective-permute-start.6 = (f32[3,12,128]{2,1,0:T(8,128)S(1)}, f32[3,12,128]{2,1,0:T(8,128)S(1)}, u32[]{:S(2)}, u32[]{:S(2)}) collective-permute-start(f32[3,12,128]{2,1,0:T(8,128)S(1)} %get-tuple-element.71), channel_id=1, source_target_pairs={{0,1},{1,0},{2,3},{3,2},{4,5},{5,4},{6,7},{7,6},{8,9},{9,8},{10,11... | collective-permute-start | bytes 55304 | tf_op jit(solution)/shard_map/ppermute | solution.py:464
  21.8 5.9 %collective-permute-start.9 = (f32[3,28,128]{2,1,0:T(8,128)S(1)}, f32[3,28,128]{2,1,0:T(8,128)S(1)}, u32[]{:S(2)}, u32[]{:S(2)}) collective-permute-start(f32[3,28,128]{2,1,0:T(8,128)S(1)} %get-tuple-element.62), channel_id=1, source_target_pairs={{0,7},{1,2},{2,1},{3,4},{4,3},{5,6},{6,5},{7,0},{8,15},{9,10},{10,... | collective-permute-start | bytes 129032 | tf_op jit(solution)/shard_map/ppermute | solution.py:463
  26.3 1.4 %collective-permute-start.8 = (f32[3,28,128]{2,1,0:T(8,128)S(1)}, f32[3,28,128]{2,1,0:T(8,128)S(1)}, u32[]{:S(2)}, u32[]{:S(2)}) collective-permute-start(f32[3,28,128]{2,1,0:T(8,128)S(1)} %get-tuple-element.63), channel_id=1, source_target_pairs={{0,1},{1,0},{2,3},{3,2},{4,5},{5,4},{6,7},{7,6},{8,9},{9,8},{10,11... | collective-permute-start | bytes 129032 | tf_op jit(solution)/shard_map/ppermute | solution.py:464
  29.3 5.1 %collective-permute-start.13 = (f32[3,10,128]{2,1,0:T(8,128)S(1)}, f32[3,10,128]{2,1,0:T(8,128)S(1)}, u32[]{:S(2)}, u32[]{:S(2)}) collective-permute-start(f32[3,10,128]{2,1,0:T(8,128)S(1)} %get-tuple-element.68), channel_id=1, source_target_pairs={{0,7},{1,2},{2,1},{3,4},{4,3},{5,6},{6,5},{7,0},{8,15},{9,10},{10,... | collective-permute-start | bytes 46088 | tf_op jit(solution)/shard_map/ppermute | solution.py:463
  31.8 2.7 %collective-permute-start.12 = (f32[3,10,128]{2,1,0:T(8,128)S(1)}, f32[3,10,128]{2,1,0:T(8,128)S(1)}, u32[]{:S(2)}, u32[]{:S(2)}) collective-permute-start(f32[3,10,128]{2,1,0:T(8,128)S(1)} %get-tuple-element.69), channel_id=1, source_target_pairs={{0,1},{1,0},{2,3},{3,2},{4,5},{5,4},{6,7},{7,6},{8,9},{9,8},{10,11... | collective-permute-start | bytes 46088 | tf_op jit(solution)/shard_map/ppermute | solution.py:464

commit v10 on v8

--- a/solution.py
+++ b/solution.py
@@ -52,13 +52,6 @@
 def hat(widths_ref, pair, distances):
     widths = jnp.broadcast_to(widths_ref[pair : pair + 1, :], (16, CH)).astype(BF16)
     return jnp.maximum(widths[None] - distances, jnp.zeros((), BF16)).reshape(CH, CH)
-
-
-def product(value, matrix):
-    cells = value.shape[0]
-    parts = jnp.concatenate(split(value), axis=0)
-    both = jnp.dot(parts, matrix, preferred_element_type=F32)
-    return both[:cells] + both[cells:]
 
 
 def swap_halves(value):
@@ -408,7 +401,7 @@
 
 
 def final_kernel(entries):
-    def body(dots_ref, y0_ref, y1_ref, y2_ref, one_ref, two_ref, widths_ref, scales_ref, coef_ref, vector_ref):
+    def body(dots_ref, y0_ref, y1_ref, y2_ref, one_ref, two_ref, widths_ref, scales_ref, coef_ref, vector_ref, once_ref):
         sums = jnp.sum(dots_ref[...], axis=0, keepdims=True)
         lane = lax.broadcasted_iota(jnp.int32, (1, CH), 1)
 
@@ -438,10 +431,14 @@
         distances = pair_distances()
         low_half = lax.broadcasted_iota(jnp.int32, coarse.shape, 1) < LEV
         field_one, field_two = by_field(coarse, low_half)
+        cells = coarse.shape[0]
+        for pair in range(PAIRS):
+            summed = one_ref[pair] * field_one + two_ref[pair] * field_two
+            once_ref[pair, 0:cells, :], once_ref[pair, cells : 2 * cells, :] = split(summed)
         for pair in range(PAIRS):
             matrix = hat(widths_ref, pair, distances)
-            summed = one_ref[pair] * field_one + two_ref[pair] * field_two
-            out = product(summed, matrix) * scales_ref[pair : pair + 1, :]
+            both = jnp.dot(once_ref[pair], matrix, preferred_element_type=F32)
+            out = (both[:cells] + both[cells:]) * scales_ref[pair : pair + 1, :]
             vector_ref[:, pair * CH : (pair + 1) * CH] = out.astype(BF16)
 
     return body
@@ -547,7 +544,7 @@
     coefficients, vector = kernel_call(
         final_kernel(entries),
         (jax.ShapeDtypeStruct((2, 2), F32), jax.ShapeDtypeStruct((cells, M * LEV), BF16)),
-        (shared, y0, y1, y2, one, two, widths, scales),
+        (shared, y0, y1, y2, one, two, widths, scales), gram_scratch(cells)[:1],
     )
     return coefficients, vector.reshape(cols, rows, M * LEV)
 

time: 46.9 us -> 46.9 us (level)
  no operation moved by 1% of the time
where the time goes in v10:
time: 46.9 us; the launch traced here: 46.8 us
  starting transfers between devices  18 us (38%)
  waiting for transfers between devices  11.3 us (24%)
  blocking collectives  10.6 us (23%)
  Pallas kernels  5.81 us (12%)
  between operations  0.76 us (2%)
    all_to_all x1, blocking collectives, per_device(): lax.all_to_all(dots.reshape(devices, 1, CH), ('lat', 'lon'), 0, 0)  10.6 us
    ppermute x4, waiting for transfers between devices, from_neighbours(): far = lax.ppermute(jnp.where(odd, up, down), axis, outer)  8.42 us
    ppermute x4, starting transfers between devices, from_neighbours(): far = lax.ppermute(jnp.where(odd, up, down), axis, outer)  7.96 us
    ppermute x3, starting transfers between devices, from_neighbours(): lax.ppermute(up, axis, [(at, (at + 1) % count) for at in range(count)])  7 us
    pallas_call x8, Pallas kernels, kernel_call(): pl.pallas_call(body, out_shape=outs, in_specs=[VMEM_SPEC] * len(operands)...  4.71 us
    ppermute x3, starting transfers between devices, from_neighbours(): lax.ppermute(down, axis, [((at + 1) % count, at) for at in range(count)])  2.99 us
    ppermute x3, waiting for transfers between devices, from_neighbours(): lax.ppermute(up, axis, [(at, (at + 1) % count) for at in range(count)])  1.84 us
    pallas_call x1, Pallas kernels, per_device(): pl.pallas_call(prepare_kernel(cols, rows), out_shape=(message, message, p...  1.1 us
  transfers between devices with their start and end apart: 14, of which 6 were waited for; matrix products, arithmetic and copies ran while one was open for 0% of the time, Pallas kernels for 1%

profile of v10, /device:TPU:0, one launch (start us, length us, event | category | flops | bytes accessed | tf_op | source)
XLA Modules:
  0.0 46.8 jit_solution(2545351003447717670)
XLA Ops:
  0.6 0.0 copy-start
  0.6 1.1 %shard_map.77 = (f32[76,128]{1,0:T(8,128)S(1)}, f32[76,128]{1,0:T(8,128)S(1)}, f32[8,8,128]{2,1,0:T(8,128)S(1)}, f32[8,16,128]{2,1,0:T(8,128)S(1)}, f32[32,128]{...) custom-call(f32[8,16,128]{2,1,0:T(8,128)} %weight_ref.1, f32[8,16,128]{2,1,0:T(8,128)} %innovation_ref.1, ...), custom_call_target="tpu_custom_call" | custom-call | flops 536870912 | bytes 2097152 | tf_op jit(solution)/shard_map/pallas_call | solution.py:481
  1.8 3.0 %collective-permute-start = (f32[76,128]{1,0:T(8,128)S(1)}, f32[76,128]{1,0:T(8,128)S(1)}, u32[]{:S(2)}, u32[]{:S(2)}) collective-permute-start(f32[76,128]{1,0:T(8,128)S(1)} %get-tuple-element.31), channel_id=1, source_target_pairs={{0,8},{8,16},{16,24},{24,0},{1,9},{9,17},{17,25},{25,1},{2,10},{10... | collective-permute-start | bytes 116744 | tf_op jit(solution)/shard_map/ppermute | solution.py:460
  4.8 1.0 %collective-permute-start.1 = (f32[76,128]{1,0:T(8,128)S(1)}, f32[76,128]{1,0:T(8,128)S(1)}, u32[]{:S(2)}, u32[]{:S(2)}) collective-permute-start(f32[76,128]{1,0:T(8,128)S(1)} %get-tuple-element.32), channel_id=1, source_target_pairs={{8,0},{16,8},{24,16},{0,24},{9,1},{17,9},{25,17},{1,25},{10,2},{18... | collective-permute-start | bytes 116744 | tf_op jit(solution)/shard_map/ppermute | solution.py:461
  5.8 0.1 add_convert_fusion
  5.9 1.8 %collective-permute-done.low_ref = f32[76,128]{1,0:T(8,128)S(1)} collective-permute-done((f32[76,128]{1,0:T(8,128)S(1)}, f32[76,128]{1,0:T(8,128)S(1)}, u32[]{:S(2)}, u32[]{:S(2)}) %collective-permute-start) | collective-permute-done | bytes 38944 | tf_op jit(solution)/shard_map/ppermute | solution.py:460
  7.7 1.1 %collective-permute-done.1.high_ref = f32[76,128]{1,0:T(8,128)S(1)} collective-permute-done((f32[76,128]{1,0:T(8,128)S(1)}, f32[76,128]{1,0:T(8,128)S(1)}, u32[]{:S(2)}, u32[]{:S(2)}) %collective-permute-start.1) | collective-permute-done | bytes 38944 | tf_op jit(solution)/shard_map/ppermute | solution.py:461
  8.8 0.1 broadcast_in_dim.18.flags_ref
  8.9 1.9 %collective-permute-start.3 = (f32[16,128]{1,0:T(8,128)S(1)}, f32[16,128]{1,0:T(8,128)S(1)}, u32[]{:S(2)}, u32[]{:S(2)}) collective-permute-start(f32[16,128]{1,0:T(8,128)S(1)} %get-tuple-element.76), channel_id=1, source_target_pairs={{0,7},{1,2},{2,1},{3,4},{4,3},{5,6},{6,5},{7,0},{8,15},{9,10},{10,... | collective-permute-start | bytes 24584 | tf_op jit(solution)/shard_map/ppermute | solution.py:457
  10.8 0.0 collective-permute-start.2
  10.8 0.0 copy-done
  10.8 0.3 shard_map.79
  11.0 2.8 %collective-permute-done.3 = f32[16,128]{1,0:T(8,128)S(1)} collective-permute-done((f32[16,128]{1,0:T(8,128)S(1)}, f32[16,128]{1,0:T(8,128)S(1)}, u32[]{:S(2)}, u32[]{:S(2)}) %collective-permute-start.3) | collective-permute-done | bytes 8224 | tf_op jit(solution)/shard_map/ppermute | solution.py:457
  13.8 0.0 collective-permute-done.2
  13.8 1.0 %shard_map.80 = (f32[32,128]{1,0:T(8,128)S(1)}, f32[32,128]{1,0:T(8,128)S(1)}) custom-call(f32[32,128]{1,0:T(8,128)S(1)} %get-tuple-element.36.own_ref, f32[16,128]{1,0:T(8,128)S(1)} %get-tuple-element.75.left_ref, f32[16,128]{1,0:T(8,128)S(1)} %get-tuple-element.74.right_ref, f32[40,32,128]{2,1,0:T(8,128)S(1)} %get-tuple-element.39.one_ref, ...), custom_call_target="tpu_custom_call" | custom-call | tf_op jit(solution)/shard_map/pallas_call | solution.py:31
  14.8 2.4 %collective-permute-start.4 = (f32[4,2,128]{2,1,0:T(2,128)S(1)}, f32[4,2,128]{2,1,0:T(2,128)S(1)}, u32[]{:S(2)}, u32[]{:S(2)}) collective-permute-start(f32[4,2,128]{2,1,0:T(2,128)S(1)} %get-tuple-element.72), channel_id=1, source_target_pairs={{0,8},{8,16},{16,24},{24,0},{1,9},{9,17},{17,25},{25,1},{2,10},{10... | collective-permute-start | bytes 12296 | tf_op jit(solution)/shard_map/ppermute | solution.py:460
  17.3 0.5 %collective-permute-start.5 = (f32[4,2,128]{2,1,0:T(2,128)S(1)}, f32[4,2,128]{2,1,0:T(2,128)S(1)}, u32[]{:S(2)}, u32[]{:S(2)}) collective-permute-start(f32[4,2,128]{2,1,0:T(2,128)S(1)} %get-tuple-element.73), channel_id=1, source_target_pairs={{8,0},{16,8},{24,16},{0,24},{9,1},{17,9},{25,17},{1,25},{10,2},{18... | collective-permute-start | bytes 12296 | tf_op jit(solution)/shard_map/ppermute | solution.py:461
  17.8 0.2 shard_map.81
  18.0 1.5 %collective-permute-start.10 = (f32[4,10240]{1,0:T(4,128)S(1)}, f32[4,10240]{1,0:T(4,128)S(1)}, u32[]{:S(2)}, u32[]{:S(2)}) collective-permute-start(f32[4,10240]{1,0:T(4,128)S(1)} %get-tuple-element.48), channel_id=1, source_target_pairs={{0,8},{8,16},{16,24},{24,0},{1,9},{9,17},{17,25},{25,1},{2,10},{10... | collective-permute-start | bytes 491528 | tf_op jit(solution)/shard_map/ppermute | solution.py:460
  19.6 1.4 %collective-permute-start.11 = (f32[4,10240]{1,0:T(4,128)S(1)}, f32[4,10240]{1,0:T(4,128)S(1)}, u32[]{:S(2)}, u32[]{:S(2)}) collective-permute-start(f32[4,10240]{1,0:T(4,128)S(1)} %get-tuple-element.49), channel_id=1, source_target_pairs={{8,0},{16,8},{24,16},{0,24},{9,1},{17,9},{25,17},{1,25},{10,2},{18... | collective-permute-start | bytes 491528 | tf_op jit(solution)/shard_map/ppermute | solution.py:461
  21.0 0.0 collective-permute-done.4
  21.0 0.0 collective-permute-done.5
  21.1 0.7 %collective-permute-start.7 = (f32[3,12,128]{2,1,0:T(8,128)S(1)}, f32[3,12,128]{2,1,0:T(8,128)S(1)}, u32[]{:S(2)}, u32[]{:S(2)}) collective-permute-start(f32[3,12,128]{2,1,0:T(8,128)S(1)} %get-tuple-element.70), channel_id=1, source_target_pairs={{0,7},{1,2},{2,1},{3,4},{4,3},{5,6},{6,5},{7,0},{8,15},{9,10},{10,... | collective-permute-start | bytes 55304 | tf_op jit(solution)/shard_map/ppermute | solution.py:457
  21.8 0.0 collective-permute-start.6
  21.8 2.9 %collective-permute-start.9 = (f32[3,28,128]{2,1,0:T(8,128)S(1)}, f32[3,28,128]{2,1,0:T(8,128)S(1)}, u32[]{:S(2)}, u32[]{:S(2)}) collective-permute-start(f32[3,28,128]{2,1,0:T(8,128)S(1)} %get-tuple-element.62), channel_id=1, source_target_pairs={{0,7},{1,2},{2,1},{3,4},{4,3},{5,6},{6,5},{7,0},{8,15},{9,10},{10,... | collective-permute-start | bytes 129032 | tf_op jit(solution)/shard_map/ppermute | solution.py:457
  24.7 1.5 %collective-permute-done.7 = f32[3,12,128]{2,1,0:T(8,128)S(1)} collective-permute-done((f32[3,12,128]{2,1,0:T(8,128)S(1)}, f32[3,12,128]{2,1,0:T(8,128)S(1)}, u32[]{:S(2)}, u32[]{:S(2)}) %collective-permute-start.7) | collective-permute-done | bytes 18464 | tf_op jit(solution)/shard_map/ppermute | solution.py:457
  26.3 0.0 collective-permute-start.8
  26.3 0.0 collective-permute-done.6
  26.3 1.4 %collective-permute-done.9 = f32[3,28,128]{2,1,0:T(8,128)S(1)} collective-permute-done((f32[3,28,128]{2,1,0:T(8,128)S(1)}, f32[3,28,128]{2,1,0:T(8,128)S(1)}, u32[]{:S(2)}, u32[]{:S(2)}) %collective-permute-start.9) | collective-permute-done | bytes 43040 | tf_op jit(solution)/shard_map/ppermute | solution.py:457
  27.7 0.0 collective-permute-done.8
  27.7 0.0 collective-permute-done.10.refs_0_
  27.7 0.0 collective-permute-done.11.refs_1_
  27.7 0.1 shard_map.82
  27.9 1.4 %shard_map.83 = (f32[32,128]{1,0:T(8,128)S(1)}, f32[32,128]{1,0:T(8,128)S(1)}, f32[4,10,128]{2,1,0:T(8,128)S(1)}) custom-call(f32[4,12,128]{2,1,0:T(8,128)S(1)} %pad_maximum_fusion.mid_ref, f32[3,12,128]{2,1,0:T(8,128)S(1)} %get-tuple-element.67.left_ref, f32[3,12,128]{2,1,0:T(8,128)S(1)} %get-tuple-element.66.right_ref, ...), custom_call_target="tpu_custom_call" | custom-call | tf_op jit(solution)/shard_map/pallas_call | solution.py:31
  29.3 2.4 %collective-permute-start.13 = (f32[3,10,128]{2,1,0:T(8,128)S(1)}, f32[3,10,128]{2,1,0:T(8,128)S(1)}, u32[]{:S(2)}, u32[]{:S(2)}) collective-permute-start(f32[3,10,128]{2,1,0:T(8,128)S(1)} %get-tuple-element.68), channel_id=1, source_target_pairs={{0,7},{1,2},{2,1},{3,4},{4,3},{5,6},{6,5},{7,0},{8,15},{9,10},{10,... | collective-permute-start | bytes 46088 | tf_op jit(solution)/shard_map/ppermute | solution.py:457
  31.8 0.0 collective-permute-start.12
  31.8 2.7 %collective-permute-done.13 = f32[3,10,128]{2,1,0:T(8,128)S(1)} collective-permute-done((f32[3,10,128]{2,1,0:T(8,128)S(1)}, f32[3,10,128]{2,1,0:T(8,128)S(1)}, u32[]{:S(2)}, u32[]{:S(2)}) %collective-permute-start.13) | collective-permute-done | bytes 15392 | tf_op jit(solution)/shard_map/ppermute | solution.py:457
  34.4 0.0 collective-permute-done.12
  34.5 0.2 shard_map.84
  34.7 10.6 %all_to_all.5 = f32[32,1,128]{2,1,0:T(1,128)S(1)} all-to-all(f32[32,1,128]{2,1,0:T(1,128)S(1)} %bitcast.17), channel_id=1, replica_groups=mesh['lat'=4,'lon'=8] {'lat','lon'}, dimensions={0} | all-to-all | bytes 32768 | tf_op jit(solution)/shard_map/all_to_all | solution.py:543
  45.4 1.4 %shard_map.85 = (f32[2,2]{1,0:T(2,128)}, bf16[32,5120]{1,0:T(8,128)(2,1)}) custom-call(f32[32,128]{1,0:T(8,128)S(1)} %bitcast.16, f32[32,128]{1,0:T(8,128)S(1)} %get-tuple-element.53.y0_ref, f32[32,128]{1,0:T(8,128)S(1)} %get-tuple-element.54.y1_ref, f32[32,128]{1,0:T(8,128)S(1)} %get-tuple-element.57.y2_ref, f32[40,32,128]{2,1,0:T(8,128)S(1)} %get-tuple-element.39.one_ref, ...), custom_call_target="tpu_custom_call" | custom-call | tf_op jit(solution)/shard_map/pallas_call | solution.py:31
  (11 shorter events, 0.1 us)
Async XLA Ops:
  0.6 10.1 %copy-start = (bf16[4,8,10240]{2,1,0:T(8,128)(2,1)S(1)}, bf16[4,8,10240]{2,1,0:T(8,128)(2,1)}, u32[]{:S(2)}) copy-start(bf16[4,8,10240]{2,1,0:T(8,128)(2,1)} %param.6) | copy-start | bytes 1966084
  1.8 6.0 %collective-permute-start = (f32[76,128]{1,0:T(8,128)S(1)}, f32[76,128]{1,0:T(8,128)S(1)}, u32[]{:S(2)}, u32[]{:S(2)}) collective-permute-start(f32[76,128]{1,0:T(8,128)S(1)} %get-tuple-element.31), channel_id=1, source_target_pairs={{0,8},{8,16},{16,24},{24,0},{1,9},{9,17},{17,25},{25,1},{2,10},{10... | collective-permute-start | bytes 116744 | tf_op jit(solution)/shard_map/ppermute | solution.py:460
  4.8 4.0 %collective-permute-start.1 = (f32[76,128]{1,0:T(8,128)S(1)}, f32[76,128]{1,0:T(8,128)S(1)}, u32[]{:S(2)}, u32[]{:S(2)}) collective-permute-start(f32[76,128]{1,0:T(8,128)S(1)} %get-tuple-element.32), channel_id=1, source_target_pairs={{8,0},{16,8},{24,16},{0,24},{9,1},{17,9},{25,17},{1,25},{10,2},{18... | collective-permute-start | bytes 116744 | tf_op jit(solution)/shard_map/ppermute | solution.py:461
  8.9 4.9 %collective-permute-start.3 = (f32[16,128]{1,0:T(8,128)S(1)}, f32[16,128]{1,0:T(8,128)S(1)}, u32[]{:S(2)}, u32[]{:S(2)}) collective-permute-start(f32[16,128]{1,0:T(8,128)S(1)} %get-tuple-element.76), channel_id=1, source_target_pairs={{0,7},{1,2},{2,1},{3,4},{4,3},{5,6},{6,5},{7,0},{8,15},{9,10},{10,... | collective-permute-start | bytes 24584 | tf_op jit(solution)/shard_map/ppermute | solution.py:457
  10.8 3.1 %collective-permute-start.2 = (f32[16,128]{1,0:T(8,128)S(1)}, f32[16,128]{1,0:T(8,128)S(1)}, u32[]{:S(2)}, u32[]{:S(2)}) collective-permute-start(f32[16,128]{1,0:T(8,128)S(1)} %get-tuple-element.77), channel_id=1, source_target_pairs={{0,1},{1,0},{2,3},{3,2},{4,5},{5,4},{6,7},{7,6},{8,9},{9,8},{10,11... | collective-permute-start | bytes 24584 | tf_op jit(solution)/shard_map/ppermute | solution.py:458
  14.8 6.2 %collective-permute-start.4 = (f32[4,2,128]{2,1,0:T(2,128)S(1)}, f32[4,2,128]{2,1,0:T(2,128)S(1)}, u32[]{:S(2)}, u32[]{:S(2)}) collective-permute-start(f32[4,2,128]{2,1,0:T(2,128)S(1)} %get-tuple-element.72), channel_id=1, source_target_pairs={{0,8},{8,16},{16,24},{24,0},{1,9},{9,17},{17,25},{25,1},{2,10},{10... | collective-permute-start | bytes 12296 | tf_op jit(solution)/shard_map/ppermute | solution.py:460
  17.3 3.7 %collective-permute-start.5 = (f32[4,2,128]{2,1,0:T(2,128)S(1)}, f32[4,2,128]{2,1,0:T(2,128)S(1)}, u32[]{:S(2)}, u32[]{:S(2)}) collective-permute-start(f32[4,2,128]{2,1,0:T(2,128)S(1)} %get-tuple-element.73), channel_id=1, source_target_pairs={{8,0},{16,8},{24,16},{0,24},{9,1},{17,9},{25,17},{1,25},{10,2},{18... | collective-permute-start | bytes 12296 | tf_op jit(solution)/shard_map/ppermute | solution.py:461
  18.0 9.7 %collective-permute-start.10 = (f32[4,10240]{1,0:T(4,128)S(1)}, f32[4,10240]{1,0:T(4,128)S(1)}, u32[]{:S(2)}, u32[]{:S(2)}) collective-permute-start(f32[4,10240]{1,0:T(4,128)S(1)} %get-tuple-element.48), channel_id=1, source_target_pairs={{0,8},{8,16},{16,24},{24,0},{1,9},{9,17},{17,25},{25,1},{2,10},{10... | collective-permute-start | bytes 491528 | tf_op jit(solution)/shard_map/ppermute | solution.py:460
  19.6 8.1 %collective-permute-start.11 = (f32[4,10240]{1,0:T(4,128)S(1)}, f32[4,10240]{1,0:T(4,128)S(1)}, u32[]{:S(2)}, u32[]{:S(2)}) collective-permute-start(f32[4,10240]{1,0:T(4,128)S(1)} %get-tuple-element.49), channel_id=1, source_target_pairs={{8,0},{16,8},{24,16},{0,24},{9,1},{17,9},{25,17},{1,25},{10,2},{18... | collective-permute-start | bytes 491528 | tf_op jit(solution)/shard_map/ppermute | solution.py:461
  21.1 5.2 %collective-permute-start.7 = (f32[3,12,128]{2,1,0:T(8,128)S(1)}, f32[3,12,128]{2,1,0:T(8,128)S(1)}, u32[]{:S(2)}, u32[]{:S(2)}) collective-permute-start(f32[3,12,128]{2,1,0:T(8,128)S(1)} %get-tuple-element.70), channel_id=1, source_target_pairs={{0,7},{1,2},{2,1},{3,4},{4,3},{5,6},{6,5},{7,0},{8,15},{9,10},{10,... | collective-permute-start | bytes 55304 | tf_op jit(solution)/shard_map/ppermute | solution.py:457
  21.8 4.5 %collective-permute-start.6 = (f32[3,12,128]{2,1,0:T(8,128)S(1)}, f32[3,12,128]{2,1,0:T(8,128)S(1)}, u32[]{:S(2)}, u32[]{:S(2)}) collective-permute-start(f32[3,12,128]{2,1,0:T(8,128)S(1)} %get-tuple-element.71), channel_id=1, source_target_pairs={{0,1},{1,0},{2,3},{3,2},{4,5},{5,4},{6,7},{7,6},{8,9},{9,8},{10,11... | collective-permute-start | bytes 55304 | tf_op jit(solution)/shard_map/ppermute | solution.py:458
  21.8 5.9 %collective-permute-start.9 = (f32[3,28,128]{2,1,0:T(8,128)S(1)}, f32[3,28,128]{2,1,0:T(8,128)S(1)}, u32[]{:S(2)}, u32[]{:S(2)}) collective-permute-start(f32[3,28,128]{2,1,0:T(8,128)S(1)} %get-tuple-element.62), channel_id=1, source_target_pairs={{0,7},{1,2},{2,1},{3,4},{4,3},{5,6},{6,5},{7,0},{8,15},{9,10},{10,... | collective-permute-start | bytes 129032 | tf_op jit(solution)/shard_map/ppermute | solution.py:457
  26.3 1.4 %collective-permute-start.8 = (f32[3,28,128]{2,1,0:T(8,128)S(1)}, f32[3,28,128]{2,1,0:T(8,128)S(1)}, u32[]{:S(2)}, u32[]{:S(2)}) collective-permute-start(f32[3,28,128]{2,1,0:T(8,128)S(1)} %get-tuple-element.63), channel_id=1, source_target_pairs={{0,1},{1,0},{2,3},{3,2},{4,5},{5,4},{6,7},{7,6},{8,9},{9,8},{10,11... | collective-permute-start | bytes 129032 | tf_op jit(solution)/shard_map/ppermute | solution.py:458
  29.3 5.1 %collective-permute-start.13 = (f32[3,10,128]{2,1,0:T(8,128)S(1)}, f32[3,10,128]{2,1,0:T(8,128)S(1)}, u32[]{:S(2)}, u32[]{:S(2)}) collective-permute-start(f32[3,10,128]{2,1,0:T(8,128)S(1)} %get-tuple-element.68), channel_id=1, source_target_pairs={{0,7},{1,2},{2,1},{3,4},{4,3},{5,6},{6,5},{7,0},{8,15},{9,10},{10,... | collective-permute-start | bytes 46088 | tf_op jit(solution)/shard_map/ppermute | solution.py:457
  31.8 2.7 %collective-permute-start.12 = (f32[3,10,128]{2,1,0:T(8,128)S(1)}, f32[3,10,128]{2,1,0:T(8,128)S(1)}, u32[]{:S(2)}, u32[]{:S(2)}) collective-permute-start(f32[3,10,128]{2,1,0:T(8,128)S(1)} %get-tuple-element.69), channel_id=1, source_target_pairs={{0,1},{1,0},{2,3},{3,2},{4,5},{5,4},{6,7},{7,6},{8,9},{9,8},{10,11... | collective-permute-start | bytes 46088 | tf_op jit(solution)/shard_map/ppermute | solution.py:458
